TPU v7x, 32 devices: a whole 2x2x4 slice. The times are simulated.
32 devices in a mesh: fsdp: 4 (over y, x), ctx: 2 (over core), tp: 4 (over z).
Axes of the slice: x: 2, y: 2, z: 4, core: 2. Of those that a mesh axis runs over, the one named last changes fastest.
Arguments:
- tokens: bfloat16 [24576, 768], P(('fsdp', 'ctx')), may hold values from -6 to 6
- grad_out: bfloat16 [24576, 768], P(('fsdp', 'ctx')), may hold values from -6 to 6
- lengths: int32 [4, 4], P('fsdp'), may hold values from 256 to 3072, as said below
- norm_gain: float32 [768], replicated, may hold values from 0.25 to 1.75
- w_z: bfloat16 [768, 1536], P('fsdp', 'tp'), may hold values from -0.21875 to 0.21875
- w_x: bfloat16 [768, 1536], P('fsdp', 'tp'), may hold values from -0.21875 to 0.21875
- w_bc: bfloat16 [768, 256], P('fsdp'), may hold values from -0.21875 to 0.21875
- w_dt: bfloat16 [768, 24], P('fsdp', 'tp'), may hold values from -0.21875 to 0.21875
- conv_x_w: float32 [4, 1536], P(None, 'tp'), may hold values from -3 to 3
- conv_x_b: float32 [1536], P('tp'), may hold values from -3 to 3
- conv_bc_w: float32 [4, 256], replicated, may hold values from -3 to 3
- conv_bc_b: float32 [256], replicated, may hold values from -3 to 3
- dt_bias: float32 [24], P('tp')
- a_log: float32 [24], P('tp'), may hold values from -3 to 1
- d_skip: float32 [24], P('tp'), may hold values from 0.5 to 1.5
- gate_gain: float32 [1536], P('tp'), may hold values from 0.25 to 1.75
- w_out: bfloat16 [1536, 768], P('tp', 'fsdp'), may hold values from -0.15625 to 0.15625
Outputs:
- layer_out: bfloat16 [24576, 768], P(('fsdp', 'ctx'), 'tp')
- grad_tokens: bfloat16 [24576, 768], P(('fsdp', 'ctx'), 'tp')
- grad_norm_gain: float32 [768], P('tp')
- grad_w_z: float32 [768, 1536], P('fsdp', 'tp')
- grad_w_x: float32 [768, 1536], P('fsdp', 'tp')
- grad_w_bc: float32 [768, 256], P('fsdp')
- grad_w_dt: float32 [768, 24], P('fsdp', 'tp')
- grad_conv_x_w: float32 [4, 1536], P(None, 'tp')
- grad_conv_x_b: float32 [1536], P('tp')
- grad_conv_bc_w: float32 [4, 256], replicated
- grad_conv_bc_b: float32 [256], replicated
- grad_dt_bias: float32 [24], P('tp')
- grad_a_log: float32 [24], P('tp')
- grad_d_skip: float32 [24], P('tp')
- grad_gate_gain: float32 [1536], P('tp')
- grad_w_out: float32 [1536, 768], P('tp', 'fsdp')
Inputs may be any that keep to these rules, and one draw needn't show every extreme that they name: Row g gives the lengths of the 4 sequences of group g in the order they stand; they sum to 6144, and one of them is exactly 3072.
All inputs are finite; a program needn't handle non-finite values.
Results may differ from a plain program's by a relative error of at most 0.017.
Values may be sent and summed in bfloat16 or wider, within the bound.
A program may use at most 256 MiB of HBM per device.

v0:
```python
import jax
import jax.numpy as jnp
from jax import lax
from jax.sharding import PartitionSpec as P

STRETCH = 256
INNER = 1536


epsilon = 1e-05


def passed_along(block, axis, distance):
    devices = range(lax.axis_size(axis))
    route = [(i - distance, i) for i in devices if i - distance in devices]
    return lax.ppermute(block, axis, route)


def entering(shard, axis, combine, identity, reverse):
    size, index = (lax.axis_size(axis), lax.axis_index(axis))
    everything = jax.tree.map(
        lambda part, kind: lax.all_gather(part.astype(kind), axis),
        shard,
        (jnp.bfloat16, jnp.bfloat16),
    )
    start = jax.tree.map(
        lambda part, zero: jnp.broadcast_to(jnp.asarray(zero, part.dtype), part.shape),
        shard,
        identity,
    )

    def lap(k, before):
        at = size - 1 - k if reverse else k
        reached = at > index if reverse else at < index
        new = combine(
            before, jax.tree.map(lambda part, own: part[at].astype(own.dtype), everything, shard)
        )
        return jax.tree.map(lambda a, b: jnp.where(reached, a, b), new, before)

    return lax.fori_loop(0, size, lap, start)


def rows_dot(left, right):
    return lax.dot_general(
        left, right, (((0,), (0,)), ((), ())), preferred_element_type=jnp.float32
    )


def cols_dot(left, right):
    return lax.dot_general(
        left, right, (((1,), (1,)), ((), ())), preferred_element_type=jnp.float32
    )


def segment_of(place_in, starts):
    return jnp.sum((place_in[:, None] >= starts[None, :]).astype(jnp.int32), axis=1)


def silu_slope(argument):
    sigmoid_v = jax.nn.sigmoid(argument)
    return sigmoid_v * (1.0 + argument * (1.0 - sigmoid_v))


def chain_forward(earlier, later):
    return (earlier[0] * later[0], later[0][:, None, None] * earlier[1] + later[1])


def chain_backward(higher, lower_part):
    return (higher[0] * lower_part[0], lower_part[1] + lower_part[0][:, None, None] * higher[1])


def intra_parts(segment, cum_log, step_size, b_mat, c_mat):
    span_len = segment.shape[0]
    positions = jnp.arange(span_len, dtype=jnp.int32)
    same_seq = (segment[:, None] == segment[None, :]) & (positions[:, None] >= positions[None, :])
    head_cum = cum_log.T
    log_gap = head_cum[:, :, None] - head_cum[:, None, :]
    decay_mat = jnp.where(same_seq[None], jnp.exp(jnp.where(same_seq[None], log_gap, 0.0)), 0.0)
    gram_mat = cols_dot(c_mat, b_mat)
    weight = decay_mat * step_size.T[:, None, :]
    return (decay_mat, gram_mat, weight)


def intra_forward(segment, cum_log, step_size, b_mat, c_mat, values):
    decay_mat, gram_mat, weight = intra_parts(segment, cum_log, step_size, b_mat, c_mat)
    mixing = (gram_mat[None] * weight).astype(jnp.bfloat16)
    return jnp.einsum("hts,shp->thp", mixing, values, preferred_element_type=jnp.float32)


def intra_backward(segment, cum_log, step_size, b_mat, c_mat, values, grad_inner):
    decay_mat, gram_mat, weight = intra_parts(segment, cum_log, step_size, b_mat, c_mat)
    mixing = (gram_mat[None] * weight).astype(jnp.bfloat16)
    grad_mix = jnp.einsum("thp,shp->hts", grad_inner, values, preferred_element_type=jnp.float32)
    grad_values = jnp.einsum("hts,thp->shp", mixing, grad_inner, preferred_element_type=jnp.float32)
    grad_gram = jnp.sum(grad_mix * weight, axis=0).astype(jnp.bfloat16)
    grad_c = jnp.dot(grad_gram, b_mat, preferred_element_type=jnp.float32)
    grad_b = rows_dot(grad_gram, c_mat)
    grad_weight = grad_mix * gram_mat[None]
    grad_step = jnp.sum(grad_weight * decay_mat, axis=1).T
    grad_gap = grad_weight * weight
    grad_cum = (jnp.sum(grad_gap, axis=2) - jnp.sum(grad_gap, axis=1)).T
    return (grad_values, grad_b, grad_c, grad_cum, grad_step)


def local(
    tokens,
    grad_out,
    lengths,
    norm_gain,
    w_z,
    w_x,
    w_bc,
    w_dt,
    conv_x_w,
    conv_x_b,
    conv_bc_w,
    conv_bc_b,
    dt_bias,
    a_log,
    d_skip,
    gate_gain,
    w_out,
):
    full_z, full_x, full_bc, full_dt, full_out = (
        lax.all_gather(w_z, "fsdp", axis=0, tiled=True),
        lax.all_gather(w_x, "fsdp", axis=0, tiled=True),
        lax.all_gather(w_bc, "fsdp", axis=0, tiled=True),
        lax.all_gather(w_dt, "fsdp", axis=0, tiled=True),
        lax.all_gather(w_out, "fsdp", axis=1, tiled=True),
    )
    row_count = tokens.shape[0]
    rim_width = conv_x_w.shape[0] - 1
    local_inner = w_z.shape[1]
    heads_here = dt_bias.shape[0]
    head_size = local_inner // heads_here
    state_size = w_bc.shape[1] // 2
    stretches = row_count // STRETCH
    model_width = tokens.shape[1]
    slice_width = model_width // lax.axis_size("tp")
    tp_index = lax.axis_index("tp")
    starts = jnp.cumsum(lengths[0]) - lengths[0]
    first_place = lax.axis_index("ctx") * row_count
    ext_place = first_place - rim_width + jnp.arange(row_count + rim_width, dtype=jnp.int32)
    ext_segment = segment_of(ext_place, starts)
    segment = ext_segment[rim_width:]
    prev_segment = ext_segment[rim_width - 1 : rim_width - 1 + row_count].reshape(
        stretches, STRETCH
    )[:, 0]
    residual = tokens.astype(jnp.float32)
    inverse = lax.rsqrt(jnp.mean(residual * residual, axis=1, keepdims=True) + epsilon)
    unit_rows = residual * inverse
    normed = (unit_rows * norm_gain).astype(jnp.bfloat16)
    z_part = jnp.dot(normed, full_z, preferred_element_type=jnp.float32)
    x_part = jnp.dot(normed, full_x, preferred_element_type=jnp.float32).astype(jnp.bfloat16)
    bc_part = jnp.dot(normed, full_bc, preferred_element_type=jnp.float32).astype(jnp.bfloat16)
    dt_raw = jnp.dot(normed, full_dt, preferred_element_type=jnp.float32)
    joined = jnp.concatenate([x_part, bc_part], axis=1)
    rim_rows = passed_along(joined[row_count - rim_width :], "ctx", 1)
    extended = jnp.concatenate([rim_rows, joined], axis=0)
    conv_w = jnp.concatenate([conv_x_w, conv_bc_w], axis=1)
    conv_b = jnp.concatenate([conv_x_b, conv_bc_b])
    tap_valid = jnp.stack(
        [ext_segment[offset : offset + row_count] == segment for offset in range(rim_width + 1)],
        axis=1,
    ).astype(jnp.float32)
    preact = jnp.zeros((row_count, joined.shape[1]), jnp.float32) + conv_b[None, :]
    for offset in range(rim_width + 1):
        preact = (
            preact
            + conv_w[offset][None, :]
            * extended[offset : offset + row_count].astype(jnp.float32)
            * tap_valid[:, offset : offset + 1]
        )
    activated = jax.nn.silu(preact)
    values = activated[:, :local_inner].astype(jnp.bfloat16)
    b_mat = activated[:, local_inner : local_inner + state_size].astype(jnp.bfloat16)
    c_mat = activated[:, local_inner + state_size :].astype(jnp.bfloat16)
    step_in = dt_raw + dt_bias
    step_size = jax.nn.softplus(step_in)
    decay_rate = jnp.exp(a_log)
    log_decay = -step_size * decay_rate
    seg_blocks = segment.reshape(stretches, STRETCH)
    cum_log = jnp.cumsum(log_decay.reshape(stretches, STRETCH, heads_here), axis=1)
    step_blocks = step_size.reshape(stretches, STRETCH, heads_here)
    b_blocks = b_mat.reshape(stretches, STRETCH, state_size)
    c_blocks = c_mat.reshape(stretches, STRETCH, state_size)
    v_blocks = values.reshape(stretches, STRETCH, heads_here, head_size)
    inner_out = lax.map(
        lambda pieces: intra_forward(*pieces),
        (seg_blocks, cum_log, step_blocks, b_blocks, c_blocks, v_blocks),
    )
    end_cum = cum_log[:, STRETCH - 1]
    end_segment = seg_blocks[:, STRETCH - 1]
    keep_end = (seg_blocks == end_segment[:, None]).astype(jnp.float32)
    end_decay = jnp.exp(end_cum[:, None, :] - cum_log) * keep_end[:, :, None]
    end_weight = end_decay * step_blocks
    weighted = (b_blocks[:, :, None, :].astype(jnp.float32) * end_weight[..., None]).astype(
        jnp.bfloat16
    )
    stretch_state = jnp.einsum(
        "cshp,cshn->chpn", v_blocks, weighted, preferred_element_type=jnp.float32
    )
    through = jnp.exp(end_cum) * (end_segment == prev_segment).astype(jnp.float32)[:, None]

    def advance(state_run, pieces):
        return (pieces[0][:, None, None] * state_run + pieces[1], state_run)

    zero_state = jnp.zeros(stretch_state.shape[1:], jnp.float32)
    ones_heads = jnp.ones((heads_here,), jnp.float32)
    local_end, local_before = lax.scan(advance, zero_state, (through, stretch_state))
    before_decay = jnp.cumprod(jnp.concatenate([ones_heads[None], through[:-1]], axis=0), axis=0)
    device_decay = jnp.prod(through, axis=0)
    incoming = entering(
        (device_decay, local_end), "ctx", chain_forward, (ones_heads, zero_state), False
    )[1]
    state_in = local_before + before_decay[:, :, None, None] * incoming[None]
    enter_mask = (seg_blocks == prev_segment[:, None]).astype(jnp.float32)
    scale_in = jnp.exp(cum_log) * enter_mask[:, :, None]
    state_low = state_in.astype(jnp.bfloat16)
    carried = jnp.einsum("ctn,chpn->cthp", c_blocks, state_low, preferred_element_type=jnp.float32)
    output = (
        inner_out
        + carried * scale_in[..., None]
        + d_skip[None, None, :, None] * v_blocks.astype(jnp.float32)
    )
    output = output.reshape(row_count, local_inner)
    gate_act = jax.nn.silu(z_part)
    gated_rows = output * gate_act
    square_sum = lax.psum(jnp.sum(gated_rows * gated_rows, axis=1), "tp")
    inverse_two = lax.rsqrt(square_sum[:, None] / INNER + epsilon)
    unit_two = gated_rows * inverse_two
    normed_two = (unit_two * gate_gain).astype(jnp.bfloat16)
    branch = lax.psum_scatter(
        jnp.dot(normed_two, full_out, preferred_element_type=jnp.float32).astype(jnp.bfloat16),
        "tp",
        scatter_dimension=1,
        tiled=True,
    ).astype(jnp.float32)
    resid_slice = lax.dynamic_slice_in_dim(residual, tp_index * slice_width, slice_width, 1)
    layer_out = (resid_slice + branch).astype(jnp.bfloat16)
    grad_w_out_full = rows_dot(normed_two, grad_out)
    grad_normed_two = cols_dot(grad_out, full_out)
    grad_gate_gain = jnp.sum(grad_normed_two * unit_two, axis=0)
    grad_unit = grad_normed_two * gate_gain
    dot_two = lax.psum(jnp.sum(grad_unit * unit_two, axis=1), "tp")
    grad_gated = inverse_two * (grad_unit - unit_two * dot_two[:, None] / INNER)
    grad_output = grad_gated * gate_act
    grad_z = (grad_gated * output * silu_slope(z_part)).astype(jnp.bfloat16)
    grad_blocks = grad_output.reshape(stretches, STRETCH, heads_here, head_size)
    grad_skip = jnp.sum(grad_blocks * v_blocks.astype(jnp.float32), axis=(0, 1, 3))
    grad_inner = grad_blocks.astype(jnp.bfloat16)
    grad_carried = (grad_blocks * scale_in[..., None]).astype(jnp.bfloat16)
    grad_cum = jnp.sum(grad_blocks * carried, axis=3) * scale_in
    grad_state_in = jnp.einsum(
        "cthp,ctn->chpn", grad_carried, c_blocks, preferred_element_type=jnp.float32
    )
    grad_c = jnp.einsum(
        "cthp,chpn->ctn", grad_carried, state_low, preferred_element_type=jnp.float32
    )

    def retreat(grad_run, pieces):
        return (pieces[1] + pieces[0][:, None, None] * grad_run, grad_run)

    local_start, local_after = lax.scan(retreat, zero_state, (through, grad_state_in), reverse=True)
    shifted = jnp.concatenate([through[1:], ones_heads[None]], axis=0)
    after_decay = jnp.cumprod(shifted[::-1], axis=0)[::-1]
    outgoing = entering(
        (device_decay, local_start), "ctx", chain_backward, (ones_heads, zero_state), True
    )[1]
    grad_after = local_after + after_decay[:, :, None, None] * outgoing[None]
    grad_through = jnp.sum(grad_after * state_in, axis=(2, 3))
    grad_stretch_low = grad_after.astype(jnp.bfloat16)
    grad_values = jnp.einsum(
        "chpn,cshn->cshp", grad_stretch_low, weighted, preferred_element_type=jnp.float32
    )
    grad_weighted = jnp.einsum(
        "cshp,chpn->cshn", v_blocks, grad_stretch_low, preferred_element_type=jnp.float32
    )
    grad_b = jnp.sum(grad_weighted * end_weight[..., None], axis=2)
    grad_end = jnp.sum(grad_weighted * b_blocks[:, :, None, :].astype(jnp.float32), axis=3)
    grad_step = grad_end * end_decay
    grad_gap_end = grad_end * end_weight
    grad_cum = grad_cum - grad_gap_end
    end_add = jnp.sum(grad_gap_end, axis=1) + grad_through * through
    grad_cum = grad_cum + jnp.pad(end_add[:, None, :], ((0, 0), (STRETCH - 1, 0), (0, 0)))
    intra_vals, intra_b, intra_c, intra_cum, intra_step = lax.map(
        lambda pieces: intra_backward(*pieces),
        (seg_blocks, cum_log, step_blocks, b_blocks, c_blocks, v_blocks, grad_inner),
    )
    grad_values = grad_values + intra_vals + d_skip[None, None, :, None] * grad_blocks
    grad_b = grad_b + intra_b
    grad_c = grad_c + intra_c
    grad_cum = grad_cum + intra_cum
    grad_step = grad_step + intra_step
    grad_log = jnp.cumsum(grad_cum[:, ::-1], axis=1)[:, ::-1].reshape(row_count, heads_here)
    grad_step_all = grad_step.reshape(row_count, heads_here) - grad_log * decay_rate
    grad_a_log = jnp.sum(grad_log * log_decay, axis=0)
    grad_pre_dt = grad_step_all * jax.nn.sigmoid(step_in)
    grad_dt_bias = jnp.sum(grad_pre_dt, axis=0)
    grad_dt_low = grad_pre_dt.astype(jnp.bfloat16)
    grad_bc_sum = lax.psum(
        jnp.concatenate([grad_b, grad_c], axis=2)
        .reshape(row_count, 2 * state_size)
        .astype(jnp.bfloat16),
        "tp",
    ).astype(jnp.float32)
    grad_activ = jnp.concatenate([grad_values.reshape(row_count, local_inner), grad_bc_sum], axis=1)
    grad_pre = grad_activ * silu_slope(preact)
    grad_conv_b = jnp.sum(grad_pre, axis=0)
    grad_ext = jnp.zeros((row_count + rim_width, joined.shape[1]), jnp.float32)
    tap_grads = []
    for offset in range(rim_width + 1):
        masked = grad_pre * tap_valid[:, offset : offset + 1]
        tap_grads.append(
            jnp.sum(masked * extended[offset : offset + row_count].astype(jnp.float32), axis=0)
        )
        grad_ext = grad_ext + jnp.pad(
            masked * conv_w[offset][None, :], ((offset, rim_width - offset), (0, 0))
        )
    grad_conv_w = jnp.stack(tap_grads, axis=0)
    rim_grad = passed_along(grad_ext[:rim_width], "ctx", -1)
    grad_joined = grad_ext[rim_width:] + jnp.pad(rim_grad, ((row_count - rim_width, 0), (0, 0)))
    grad_x_low = grad_joined[:, :local_inner].astype(jnp.bfloat16)
    grad_bc_low = grad_joined[:, local_inner:].astype(jnp.bfloat16)
    first_copy = (tp_index == 0).astype(jnp.float32)
    grad_normed = (
        cols_dot(grad_z, full_z)
        + cols_dot(grad_x_low, full_x)
        + cols_dot(grad_dt_low, full_dt)
        + first_copy * cols_dot(grad_bc_low, full_bc)
    )
    scaled = grad_normed * norm_gain
    grad_resid = inverse * (
        scaled - unit_rows * jnp.mean(scaled * unit_rows, axis=1, keepdims=True)
    )
    grad_gain_part = jnp.sum(grad_normed * unit_rows, axis=0) * first_copy + jnp.sum(
        grad_normed * unit_rows, axis=0
    ) * (1.0 - first_copy)
    grad_resid_slice, gain_slice = (
        lax.psum_scatter(
            grad_resid.astype(jnp.bfloat16), "tp", scatter_dimension=1, tiled=True
        ).astype(jnp.float32),
        lax.psum_scatter(
            grad_gain_part.astype(jnp.bfloat16), "tp", scatter_dimension=0, tiled=True
        ).astype(jnp.float32),
    )
    grad_tokens = (
        lax.dynamic_slice_in_dim(grad_out, tp_index * slice_width, slice_width, 1).astype(
            jnp.float32
        )
        + grad_resid_slice
    ).astype(jnp.bfloat16)
    part_z = rows_dot(normed, grad_z)
    part_x = rows_dot(normed, grad_x_low)
    part_bc = rows_dot(normed, grad_bc_low)
    part_dt = rows_dot(normed, grad_dt_low)
    (
        sum_z,
        sum_x,
        sum_bc,
        sum_dt,
        sum_out,
        grad_norm_gain,
        grad_conv_x_w,
        grad_conv_x_b,
        grad_conv_bc_w,
        grad_conv_bc_b,
        sum_dt_bias,
        sum_a_log,
        sum_skip,
        sum_gate,
    ) = lax.psum(
        (
            part_z,
            part_x,
            part_bc,
            part_dt,
            grad_w_out_full,
            gain_slice,
            grad_conv_w[:, :local_inner],
            grad_conv_b[:local_inner],
            grad_conv_w[:, local_inner:],
            grad_conv_b[local_inner:],
            grad_dt_bias,
            grad_a_log,
            grad_skip,
            grad_gate_gain,
        ),
        ("fsdp", "ctx"),
    )
    part_rows = model_width // lax.axis_size("fsdp")
    row_start = lax.axis_index("fsdp") * part_rows
    grad_w_z = lax.dynamic_slice_in_dim(sum_z, row_start, part_rows, 0)
    grad_w_x = lax.dynamic_slice_in_dim(sum_x, row_start, part_rows, 0)
    grad_w_bc = lax.dynamic_slice_in_dim(sum_bc, row_start, part_rows, 0)
    grad_w_dt = lax.dynamic_slice_in_dim(sum_dt, row_start, part_rows, 0)
    grad_w_out = lax.dynamic_slice_in_dim(sum_out, row_start, part_rows, 1)
    return (
        layer_out,
        grad_tokens,
        grad_norm_gain,
        grad_w_z,
        grad_w_x,
        grad_w_bc,
        grad_w_dt,
        grad_conv_x_w,
        grad_conv_x_b,
        grad_conv_bc_w,
        grad_conv_bc_b,
        sum_dt_bias,
        sum_a_log,
        sum_skip,
        sum_gate,
        grad_w_out,
    )


def solution(mesh):
    in_specs = (
        P(("fsdp", "ctx"), None),
        P(("fsdp", "ctx"), None),
        P("fsdp", None),
        P(),
        P("fsdp", "tp"),
        P("fsdp", "tp"),
        P("fsdp", None),
        P("fsdp", "tp"),
        P(None, "tp"),
        P("tp"),
        P(),
        P(),
        P("tp"),
        P("tp"),
        P("tp"),
        P("tp"),
        P("tp", "fsdp"),
    )
    out_specs = (
        P(("fsdp", "ctx"), "tp"),
        P(("fsdp", "ctx"), "tp"),
        P("tp"),
        P("fsdp", "tp"),
        P("fsdp", "tp"),
        P("fsdp", None),
        P("fsdp", "tp"),
        P(None, "tp"),
        P("tp"),
        P(),
        P(),
        P("tp"),
        P("tp"),
        P("tp"),
        P("tp"),
        P("tp", "fsdp"),
    )
    return jax.shard_map(local, mesh=mesh, in_specs=in_specs, out_specs=out_specs, check_vma=False)
```

profile of v0, /device:TPU:0, one launch (start us, length us, event | category | flops | bytes accessed | tf_op | source)
XLA Modules:
  0.0 922.3 jit_solution(8518075846859660684)
XLA Ops:
  17.4 11.8 %all_gather.33 = bf16[768,384]{1,0:T(8,128)(2,1)S(1)} all-gather(bf16[192,384]{1,0:T(8,128)(2,1)S(1)} %copy-done.52), channel_id=1, replica_groups=mesh['fsdp'=4,'ctx'=2,'tp'=4] {'fsdp'}, dimensions={0}, use_global_device_ids=true | all-gather | bytes 737280 | tf_op jit(solution)/shard_map/all_gather | solution.py:126
  29.2 9.5 %all_gather.34 = bf16[768,256]{1,0:T(8,128)(2,1)S(1)} all-gather(bf16[192,256]{1,0:T(8,128)(2,1)S(1)} %copy-done.57), channel_id=1, replica_groups=mesh['fsdp'=4,'ctx'=2,'tp'=4] {'fsdp'}, dimensions={0}, use_global_device_ids=true | all-gather | bytes 491520 | tf_op jit(solution)/shard_map/all_gather | solution.py:127
  51.8 7.7 all-gather.3
  73.6 11.0 %all_gather.39 = bf16[768,384]{1,0:T(8,128)(2,1)} all-gather(bf16[192,384]{1,0:T(8,128)(2,1)} %param.33), channel_id=1, replica_groups=mesh['fsdp'=4,'ctx'=2,'tp'=4] {'fsdp'}, dimensions={0}, use_global_device_ids=true | all-gather | bytes 737280 | tf_op jit(solution)/shard_map/all_gather | solution.py:125
  90.7 11.0 %all_gather.40 = bf16[384,768]{0,1:T(8,128)(2,1)} all-gather(bf16[384,192]{0,1:T(8,128)(2,1)} %param.45), channel_id=1, replica_groups=mesh['fsdp'=4,'ctx'=2,'tp'=4] {'fsdp'}, dimensions={1}, use_global_device_ids=true | all-gather | bytes 737280 | tf_op jit(solution)/shard_map/all_gather | solution.py:129
  128.2 11.4 %multiply_convert_fusion.7 = (bf16[3072,640]{0,1:T(8,128)(2,1)S(1)}, f32[3072,640]{0,1:T(8,128)}) fusion(f32[3072]{0:T(1024)S(1)} %bitcast.313, bf16[3072,256]{0,1:T(8,128)(2,1)S(1)} %copy-done.8, bf16[3072,384]{0,1:T(8,128)(2,1)S(1)} %convolution_convert_fusion.1, f32[640]{0:T(1024)S(1)} %copy-done.65, f32[3072]{0:T(1024)S(1)} %bitcast.316, ...), kind=kLoop, calls=%fused_computation.124 | loop fusion | flops 47185920 | bytes 27587072 | tf_op jit(solution)/shard_map/convert.11
  160.9 29.1 %while.90 = (s32[]{:T(128)}, f32[6,64,128]{2,1,0:T(8,128)S(1)}, f32[12,6,64,128]{3,2,1,0:T(8,128)}, f32[12,6]{1,0:T(8,128)}, f32[12,6,64,128]{3,2,1,0:T(8,128)}, /*index=5*/s32[]{:T(128)}, s32[]{:T(128)}) while((s32[]{:T(128)}, f32[6,64,128]{2,1,0:T(8,128)S(1)}, f32[12,6,64,128]{3,2,1,0:T(8,128)}, f32[12,6]{1,0:T(8,128)}, ...), condition=%wide.region_8.9_spmd.clone, body=%wide.region_7.8_spmd.clone.sunk | while | flops 196611 | bytes 983720 | solution.py:210
  196.5 51.1 %while.88 = (s32[]{:T(128)}, f32[12,256,6,64]{1,3,2,0:T(8,128)}, bf16[12,256,6,64]{1,3,2,0:T(8,128)(2,1)}, bf16[12,256,128]{2,1,0:T(8,128)(2,1)S(1)}, bf16[12,25...) while((s32[]{:T(128)}, f32[12,256,6,64]{1,3,2,0:T(8,128)}, ...), condition=%wide.region_6.7_spmd, body=%wide.region_5.6_spmd.sunk | while | flops 69664768 | bytes 1430629 | solution.py:188
  247.6 7.0 multiply_add_fusion.1
  261.9 7.4 multiply_reduce_fusion.9
  269.3 20.4 %psum.119 = f32[3072]{0:T(1024)} all-reduce(f32[3072]{0:T(1024)} %get-tuple-element.908), channel_id=1, replica_groups=mesh['fsdp'=4,'ctx'=2,'tp'=4] {'tp'}, use_global_device_ids=true, to_apply=%region_14.15 | all-reduce | flops 3072 | bytes 24576 | tf_op jit(solution)/shard_map/psum | solution.py:229
  290.4 9.3 %multiply_reduce_fusion.5 = (f32[384]{0:T(512)}, f32[3072]{0:T(1024)}, f32[3072,384]{0,1:T(8,128)}) fusion(f32[3072,384]{0,1:T(8,128)} %get-tuple-element.909, f32[3072]{0:T(1024)S(1)} %add_rsqrt_fusion, f32[384]{0:T(512)} %param.44, bf16[3072,768]{1,0:T(8,128)(2,1)} %param.30, bf16[384,768]{0,1:T(8,128)(2,1)} %all_gather.40), kind=kOutput, calls=%fused_computation.135 | convolution fusion | flops 1819013760 | bytes 14773248 | tf_op jit(solution)/shard_map/dot_general | solution.py:50
  299.7 16.7 %psum.120 = f32[3072]{0:T(1024)} all-reduce(f32[3072]{0:T(1024)} %get-tuple-element.798), channel_id=1, replica_groups=mesh['fsdp'=4,'ctx'=2,'tp'=4] {'tp'}, use_global_device_ids=true, to_apply=%region_17.18 | all-reduce | flops 3072 | bytes 24576 | tf_op jit(solution)/shard_map/psum | solution.py:245
  316.4 12.3 %multiply_reduce_fusion.6 = (f32[384]{0:T(512)}, f32[3072,384]{0,1:T(8,128)}, bf16[3072,384]{0,1:T(8,128)(2,1)}) fusion(bf16[3072,640]{0,1:T(8,128)(2,1)} %copy-done.6, f32[3072,384]{0,1:T(8,128)} %get-tuple-element.948, f32[3072]{0:T(1024)} %psum.120, f32[3072,384]{0,1:T(8,128)} %get-tuple-element.909, f32[3072,384]{0,1:T(8,128)} %get-tuple-element.949, ...), kind=kLoop, calls=%fused_computation.136 | loop fusion | flops 24772224 | bytes 28339200 | tf_op jit(solution)/shard_map/reduce_sum | solution.py:250
  335.5 7.1 fusion.108
  346.4 29.0 %while.92 = (s32[]{:T(128)}, f32[6,64,128]{2,1,0:T(8,128)S(1)}, f32[12,6,64,128]{3,2,1,0:T(8,128)}, f32[12,6,64,128]{3,2,1,0:T(8,128)}, f32[12,6]{1,0:T(8,128)}, /*index=5*/s32[]{:T(128)}, s32[]{:T(128)}, s32[]{:T(128)}) while((s32[]{:T(128)}, f32[6,64,128]{2,1,0:T(8,128)S(1)}, f32[12,6,64,128]{3,2,1,0:T(8,128)}, ...), condition=%wide.region_19.20_spmd.clone, body=%wide.region_18.19_spmd.clone.sunk | while | flops 196612 | bytes 983232 | solution.py:264
  389.9 123.4 %while.89 = (s32[]{:T(128)}, f32[12,256,6,64]{1,3,2,0:T(8,128)}, f32[12,256,128]{1,2,0:T(8,128)}, f32[12,256,128]{1,2,0:T(8,128)}, f32[12,256,6]{1,2,0:T(8,128)}...) while((s32[]{:T(128)}, f32[12,256,6,64]{1,3,2,0:T(8,128)}, ...), condition=%wide.region_28.29_spmd, body=%wide.region_23.28_spmd.sunk | while | flops 158200832 | bytes 3019409 | solution.py:286
  513.4 7.1 fusion.90
  531.3 9.2 fusion.77
  557.8 39.7 %all-reduce.14.cloned.1.call-done = bf16[3072,256]{0,1:T(8,128)(2,1)} async-done(((bf16[3072,256]{0,1:T(8,128)(2,1)}), bf16[3072,256]{0,1:T(8,128)(2,1)}) %all-reduce.14.cloned.1.call-update) | async-done | bytes 1572880 | tf_op jit(solution)/shard_map/psum | solution.py:301
  600.2 13.6 %fusion.67 = (f32[640]{0:T(1024)}, f32[640]{0:T(1024)}, f32[640]{0:T(1024)}, f32[640]{0:T(1024)}, f32[640]{0:T(1024)}, /*index=5*/f32[3072,640]{0,1:T(8,128)}) fusion(f32[3072]{0:T(1024)S(1)} %bitcast.311, bf16[3075,640]{0,1:T(8,128)(2,1)S(1)} %copy-done.1, f32[3072]{0:T(1024)S(1)} %bitcast.320, f32[3072]{0:T(1024)S(1)} %bitcast.317, ...), kind=kLoop, calls=%fused_computation.114 | loop fusion | flops 57013120 | bytes 39383552 | tf_op jit(solution)/shard_map/reduce_sum | solution.py:315
  613.8 9.4 %multiply_multiply_fusion.3 = (f32[3072,640]{0,1:T(8,128)S(1)}, f32[3072,640]{0,1:T(8,128)S(1)}, f32[3072,640]{0,1:T(8,128)}, f32[3072,640]{0,1:T(8,128)}) fusion(f32[3072,640]{0,1:T(8,128)} %get-tuple-element.907, f32[3072]{0:T(1024)S(1)} %bitcast.312, f32[640]{0:T(1024)S(1)} %copy-done.64, f32[640]{0:T(1024)S(1)} %copy-done.66, f32[3072]{0:T(1024)S(1)} %bitcast.315, ...), kind=kLoop, calls=%fused_computation.129 | loop fusion | flops 15728640 | bytes 39380992 | tf_op jit(solution)/shard_map/mul | solution.py:318
  626.8 12.1 %pad_add_fusion = f32[3075,640]{0,1:T(8,128)} fusion(f32[3072,640]{0,1:T(8,128)S(1)} %get-tuple-element.918, f32[3072,640]{0,1:T(8,128)} %get-tuple-element.919, f32[3072,640]{0,1:T(8,128)} %get-tuple-element.920, f32[3072,640]{0,1:T(8,128)S(1)} %get-tuple-element.917), kind=kLoop, calls=%fused_computation.108 | loop fusion | flops 5904000 | bytes 39329280 | tf_op jit(solution)/shard_map/add | solution.py:317
  643.7 7.5 fusion.86
  667.4 7.6 multiply_reduce_fusion.7
  710.8 15.0 %multiply_reduce_fusion.2 = (f32[768]{0:T(1024)S(1)}, f32[3072]{0:T(1024)S(1)}, f32[3072,768]{0,1:T(8,128)}) fusion(bf16[3072,768]{0,1:T(8,128)(2,1)S(1)} %bitcast.276, f32[3072]{0:T(1024)S(1)} %copy-done.51, f32[768]{0:T(1024)S(1)} %copy-done.72, bf16[768,256]{1,0:T(8,128)(2,1)S(1)} %copy-done.31, bf16[3072,640]{0,1:T(8,128)(2,1)} %copy-done.13, ...), kind=kOutput, calls=%fused_computation.101 | convolution fusion | flops 1233907968 | bytes 44464132 | tf_op jit(solution)/shard_map/dot_general | solution.py:50
  725.7 8.6 multiply_convert_fusion.4
  734.4 7.2 convert_element_type.227
  750.0 11.7 %all-reduce.8 = bf16[768]{0:T(1024)(128)(2,1)S(1)} all-reduce(bf16[768]{0:T(1024)(128)(2,1)S(1)} %multiply_convert_fusion.15), channel_id=7, replica_groups=mesh['fsdp'=4,'ctx'=2,'tp'=4] {'tp'}, use_global_device_ids=true, to_apply=%region_40.41.clone | all-reduce | flops 768 | bytes 3072
  761.8 25.6 %all-reduce.9 = (f32[192]{0:T(256)}, f32[768,6]{0,1:T(8,128)S(1)}, f32[4,384]{1,0:T(4,128)}, f32[384]{0:T(512)}, f32[4,256]{1,0:T(4,128)}, /*index=5*/f32[256]{0...) all-reduce(f32[192]{0:T(256)S(1)} %dynamic-slice_convert_fusion, ...), channel_id=1, replica_groups=mesh['fsdp'=4,'ctx'=2,'tp'=4] {'fsdp','ctx'}, use_global_device_ids=true, to_apply=%region_41.42 | all-reduce | flops 8402 | bytes 67216 | tf_op jit(solution)/shard_map/psum | solution.py:372
  794.8 29.9 %reduce-scatter.3.cloned.1.call-done = bf16[3072,192]{0,1:T(8,128)(2,1)} async-done(((bf16[3072,768]{0,1:T(8,128)(2,1)}), bf16[3072,192]{0,1:T(8,128)(2,1)}) %reduce-scatter.3.cloned.1.call-update) | async-done | bytes 1179664 | tf_op jit(solution)/shard_map/reduce_scatter | solution.py:233
  828.0 84.6 %reduce-scatter.5.cloned.1.call-done = bf16[3072,192]{0,1:T(8,128)(2,1)} async-done(((bf16[3072,768]{0,1:T(8,128)(2,1)}), bf16[3072,192]{0,1:T(8,128)(2,1)}) %reduce-scatter.5.cloned.1.call-update) | async-done | bytes 1179664 | tf_op jit(solution)/shard_map/reduce_scatter | solution.py:340
  (657 shorter events, 478.1 us)
Async XLA Ops:
  7.2 590.4 %all-reduce.14.cloned.1.call-start = ((), (), s32[]{:S(2)}) async-start(), calls=%async_computation.3 | async-start | bytes 3145728 | tf_op jit(solution)/shard_map/psum | solution.py:301
  13.9 15.3 %copy-start.57 = (bf16[192,256]{1,0:T(8,128)(2,1)S(1)}, bf16[192,256]{1,0:T(8,128)(2,1)}, u32[]{:S(2)}) copy-start(bf16[192,256]{1,0:T(8,128)(2,1)} %param.35) | copy-start | bytes 294916
  13.9 24.8 %copy-start.3 = (bf16[3072,768]{0,1:T(8,128)(2,1)S(1)}, bf16[3072,768]{0,1:T(8,128)(2,1)}, u32[]{:S(2)}) copy-start(bf16[3072,768]{0,1:T(8,128)(2,1)} %copy.366) | copy-start | bytes 14155780
  13.9 24.8 %copy-start.71 = (f32[768]{0:T(1024)S(1)}, f32[768]{0:T(1024)}, u32[]{:S(2)}) copy-start(f32[768]{0:T(1024)} %param.32) | copy-start | bytes 9220
  17.4 23.2 %copy-start.50 = (f32[3072]{0:T(1024)}, f32[3072]{0:T(1024)S(1)}, u32[]{:S(2)}) copy-start(f32[3072]{0:T(1024)S(1)} %add_rsqrt_fusion.1) | copy-start | bytes 36868
  42.8 16.9 %copy-start.91 = (f32[6]{0:T(128)S(1)}, f32[6]{0:T(128)}, u32[]{:S(2)}) copy-start(f32[6]{0:T(128)} %param.42) | copy-start | bytes 76
  42.8 16.9 %copy-start.88 = (f32[6]{0:T(128)S(1)}, f32[6]{0:T(128)}, u32[]{:S(2)}) copy-start(f32[6]{0:T(128)} %param.41) | copy-start | bytes 76
  46.2 75.4 %collective-permute-start = (bf16[3,640]{0,1:T(8,128)(2,1)}, bf16[3,640]{0,1:T(8,128)(2,1)}, u32[]{:S(2)}, u32[]{:S(2)}) collective-permute-start(bf16[3,640]{0,1:T(8,128)(2,1)} %fusion.102), channel_id=1, source_target_pairs={{0,4},{1,5},{2,6},{3,7},{8,12},{9,13},{10,14},{11,15},{16,20},{17,... | collective-permute-start | bytes 11528 | tf_op jit(solution)/shard_map/ppermute | solution.py:16
  51.8 36.2 %copy-start.33 = (f32[12,256]{0,1:T(8,128)}, f32[12,256]{0,1:T(8,128)S(1)}, u32[]{:S(2)}) copy-start(f32[12,256]{0,1:T(8,128)S(1)} %copy.379) | copy-start | bytes 36868
  63.4 41.4 %copy-start.35 = (f32[3072,6]{0,1:T(8,128)}, f32[3072,6]{0,1:T(8,128)S(1)}, u32[]{:S(2)}) copy-start(f32[3072,6]{0,1:T(8,128)S(1)} %get-tuple-element.929) | copy-start | bytes 221188
  69.2 58.9 %copy-start.17 = (f32[12,6,2,128]{0,3,2,1:T(8,128)}, f32[12,6,2,128]{0,3,2,1:T(8,128)S(1)}, u32[]{:S(2)}) copy-start(f32[12,6,2,128]{0,3,2,1:T(8,128)S(1)} %copy.440) | copy-start | bytes 221188
  69.2 35.6 %copy-start.61 = (f32[12,1,6]{0,2,1:T(8,128)}, f32[12,1,6]{0,2,1:T(8,128)S(1)}, u32[]{:S(2)}) copy-start(f32[12,1,6]{0,2,1:T(8,128)S(1)} %copy.495) | copy-start | bytes 868
  159.2 32.8 %copy-start.19 = (f32[6,64,128]{2,1,0:T(8,128)S(1)}, f32[6,64,128]{2,1,0:T(8,128)}, u32[]{:S(2)}) copy-start(f32[6,64,128]{2,1,0:T(8,128)} %custom-call.1) | copy-start | bytes 589828
  159.2 32.8 %copy-start.93 = (bf16[2,6]{1,0:T(2,128)(2,1)S(1)}, bf16[2,6]{1,0:T(2,128)(2,1)}, u32[]{:S(2)}) copy-start(bf16[2,6]{1,0:T(2,128)(2,1)} %reshape.345) | copy-start | bytes 76
  530.8 257.3 %all-reduce.16.cloned.1.call-start = ((), (), s32[]{:S(2)}) async-start(), calls=%async_computation.5 | async-start | bytes 8650752 | tf_op jit(solution)/shard_map/psum | solution.py:372
  557.8 41.7 %copy-start.43 = (f32[3072,1]{0,1:T(1,128)S(1)}, f32[3072,1]{0,1:T(1,128)}, u32[]{:S(2)}) copy-start(f32[3072,1]{0,1:T(1,128)} %get-tuple-element.930) | copy-start | bytes 36868
  557.8 41.7 %copy-start.45 = (f32[3072,1]{0,1:T(1,128)S(1)}, f32[3072,1]{0,1:T(1,128)}, u32[]{:S(2)}) copy-start(f32[3072,1]{0,1:T(1,128)} %get-tuple-element.931) | copy-start | bytes 36868
  557.8 41.7 %copy-start.47 = (f32[3072,1]{0,1:T(1,128)S(1)}, f32[3072,1]{0,1:T(1,128)}, u32[]{:S(2)}) copy-start(f32[3072,1]{0,1:T(1,128)} %get-tuple-element.932) | copy-start | bytes 36868
  557.8 41.7 %copy-start.49 = (f32[3072,1]{0,1:T(1,128)S(1)}, f32[3072,1]{0,1:T(1,128)}, u32[]{:S(2)}) copy-start(f32[3072,1]{0,1:T(1,128)} %get-tuple-element.933) | copy-start | bytes 36868
  600.2 13.6 %copy-start.64 = (f32[640]{0:T(1024)S(1)}, f32[640]{0:T(1024)}, u32[]{:S(2)}) copy-start(f32[640]{0:T(1024)} %get-tuple-element.803) | copy-start | bytes 7684
  600.2 13.6 %copy-start.66 = (f32[640]{0:T(1024)S(1)}, f32[640]{0:T(1024)}, u32[]{:S(2)}) copy-start(f32[640]{0:T(1024)} %get-tuple-element.804) | copy-start | bytes 7684
  600.2 13.6 %copy-start.68 = (f32[640]{0:T(1024)S(1)}, f32[640]{0:T(1024)}, u32[]{:S(2)}) copy-start(f32[640]{0:T(1024)} %get-tuple-element.805) | copy-start | bytes 7684
  600.2 13.6 %copy-start.70 = (f32[640]{0:T(1024)S(1)}, f32[640]{0:T(1024)}, u32[]{:S(2)}) copy-start(f32[640]{0:T(1024)} %get-tuple-element.806) | copy-start | bytes 7684
  625.3 13.6 %collective-permute-start.1 = (f32[3,640]{0,1:T(8,128)}, f32[3,640]{0,1:T(8,128)}, u32[]{:S(2)}, u32[]{:S(2)}) collective-permute-start(f32[3,640]{0,1:T(8,128)} %pad_add_fusion.1), channel_id=1, source_target_pairs={{4,0},{5,1},{6,2},{7,3},{12,8},{13,9},{14,10},{15,11},{20,16},{21,... | collective-permute-start | bytes 23048 | tf_op jit(solution)/shard_map/ppermute | solution.py:16
  638.9 12.3 %slice-start.6 = ((s8[4718592]{0:T(1024)(128)(4,1)}), s8[524288]{0:T(1024)(128)(4,1)S(1)}, s32[]{:S(2)}) async-start(s8[4718592]{0:T(1024)(128)(4,1)} %bitcast.281), calls=%async_computation.12 | async-start | bytes 1048576
  653.5 171.1 %reduce-scatter.3.cloned.1.call-start = ((), (), s32[]{:S(2)}) async-start(), calls=%async_computation.2 | async-start | bytes 5898240 | tf_op jit(solution)/shard_map/reduce_scatter | solution.py:233
  660.5 252.2 %reduce-scatter.5.cloned.1.call-start = ((), (), s32[]{:S(2)}) async-start(), calls=%async_computation.4 | async-start | bytes 5898240 | tf_op jit(solution)/shard_map/reduce_scatter | solution.py:340
  679.7 14.6 %copy-start.36 = (f32[3072,6]{0,1:T(8,128)S(1)}, f32[3072,6]{0,1:T(8,128)}, u32[]{:S(2)}) copy-start(f32[3072,6]{0,1:T(8,128)} %copy-done.35) | copy-start | bytes 221188
  679.7 14.6 %copy-start.41 = (f32[3072,6]{0,1:T(8,128)S(1)}, f32[3072,6]{0,1:T(8,128)}, u32[]{:S(2)}) copy-start(f32[3072,6]{0,1:T(8,128)} %get-tuple-element.945) | copy-start | bytes 221188
  679.7 14.6 %copy-start.83 = (f32[6]{0:T(128)S(1)}, f32[6]{0:T(128)}, u32[]{:S(2)}) copy-start(f32[6]{0:T(128)} %copy-done.82) | copy-start | bytes 76
  679.7 14.8 %copy-start.55 = (bf16[768,6]{0,1:T(8,128)(2,1)S(1)}, bf16[768,6]{0,1:T(8,128)(2,1)}, u32[]{:S(2)}) copy-start(bf16[768,6]{0,1:T(8,128)(2,1)} %copy-done.54) | copy-start | bytes 27652
  741.6 20.2 %copy-start.89 = (f32[384]{0:T(512)S(1)}, f32[384]{0:T(512)}, u32[]{:S(2)}) copy-start(f32[384]{0:T(512)} %get-tuple-element.797) | copy-start | bytes 4612
  (80 other events, 529.1 us)
Sparse Core Ops, SparseCore 0:
  530.9 66.6 all-reduce.13
  653.6 83.0 all-reduce.15
  739.0 85.6 reduce-scatter.2
  826.8 85.7 reduce-scatter.4
where the time goes:
time: 938 us; the launch traced here: 922 us
  matrix products  258 us (28%)
  other arithmetic  194 us (21%)
  local copies, waits for them, and re-layouts  161 us (17%)
  waiting for transfers between devices  154 us (16%)
  blocking collectives  132 us (14%)
  between operations  17 us (2%)
    reduce_scatter x1, waiting for transfers between devices, local(): lax.psum_scatter(grad_resid.astype(jnp.bfloat16), 'tp', scatter_dimension...  84.6 us
    dot_general x29, matrix products, cols_dot(): lax.dot_general(left, right, (((1,), (1,)), ((), ())), preferred_element_...  64.9 us
    psum x1, waiting for transfers between devices, local(): lax.psum(jnp.concatenate([grad_b, grad_c], axis=2).reshape(row_count, 2 *...  39.7 us
    dot_general x17, matrix products, rows_dot(): lax.dot_general(left, right, (((0,), (0,)), ((), ())), preferred_element_...  31.6 us
    reduce_scatter x1, waiting for transfers between devices, local(): lax.psum_scatter(jnp.dot(normed_two, full_out, preferred_element_type=jnp...  29.9 us
    dot_general x12, matrix products, intra_forward(): jnp.einsum('hts,shp->thp', mixing, values, preferred_element_type=jnp.flo...  28.3 us
    dot_general x12, matrix products, intra_backward(): jnp.einsum('hts,thp->shp', mixing, grad_inner, preferred_element_type=jnp...  28 us
    unnamed x225, local copies, waits for them, and re-layouts  27.9 us
  transfers between devices with their start and end apart: 6, of which 3 were waited for; matrix products, arithmetic and copies ran while one was open for 20% of the time, Pallas kernels for 0%

commit v1 on v0

v1 whole, which is shorter than its diff:
```python
import functools

import jax
import jax.numpy as jnp
import numpy as np
from jax import lax
from jax.experimental import pallas as pl
from jax.experimental.pallas import tpu as pltpu
from jax.sharding import PartitionSpec as P

STRETCH = 256
INNER = 1536
HEAD_ROWS = 8
LOG2E = 1.4426950408889634

epsilon = 1e-05
f32 = jnp.float32
bf16 = jnp.bfloat16


def nn(left, right):
    return lax.dot_general(left, right, (((1,), (0,)), ((), ())), preferred_element_type=f32)


def nt(left, right):
    return lax.dot_general(left, right, (((1,), (1,)), ((), ())), preferred_element_type=f32)


def tn(left, right):
    return lax.dot_general(left, right, (((0,), (0,)), ((), ())), preferred_element_type=f32)


def halves(x):
    high = x.astype(bf16)
    return high, (x - high.astype(f32)).astype(bf16)


def thirds(x):
    high = x.astype(bf16)
    rest = x - high.astype(f32)
    mid = rest.astype(bf16)
    return high, mid, (rest - mid.astype(f32)).astype(bf16)


def exact_rows(x, ones_matrix):
    high, mid, low = thirds(x)
    r = HEAD_ROWS
    out = nn(jnp.concatenate([high, mid, low, jnp.zeros_like(low)], axis=0), ones_matrix)
    return out[:r] + out[r : 2 * r] + out[2 * r : 3 * r]


def columns_of(rows):
    have = sum(r.shape[0] for r in rows)
    pad = jnp.zeros((128 - have, rows[0].shape[1]), f32)
    cols = jnp.transpose(jnp.concatenate(list(rows) + [pad], axis=0))
    high, low = halves(cols)
    return cols, jnp.concatenate([high, low], axis=1)


def segment_start(pos, starts):
    found = jnp.zeros_like(pos)
    for s in starts:
        found = jnp.where(pos >= s, s, found)
    return found


def joined_ok(u, distance, starts):
    ok = jnp.ones(u.shape, jnp.bool_)
    for s in starts[1:]:
        ok = ok & jnp.logical_not((u < s) & (u + distance >= s))
    return ok


def iota(shape, axis):
    return lax.broadcasted_iota(jnp.int32, shape, axis)


def read_info(info, block):
    first = info[0]
    starts = [info[1 + k] for k in range(info.shape[0] - 1)]
    base = first + block * STRETCH
    end_start = segment_start(base + STRETCH - 1, starts)
    flag = jnp.where(end_start < base, 1.0, 0.0).astype(f32)
    return starts, base, end_start, flag


def norm_rows(tok):
    x = tok.astype(f32)
    inverse = lax.rsqrt(jnp.mean(x * x, axis=1, keepdims=True) + epsilon)
    return x * inverse, inverse


def lanes_of(column, e8):
    return jnp.sum(column * e8, axis=0, keepdims=True)


def entry_kernel(
    info, tok, halo, gain, wj, cw, cb, bias, rate, tri, ew, e8,
    nrm_o, jx_o, jb_o, vbc_o, sx_o, sb_o, pre_o, step_o, cum_o, s_o, end_o, dec_o,
    ext, run, dec,
):
    i = pl.program_id(0)
    starts, base, end_start, flag = read_info(info, i)
    width = cw.shape[1]
    inner = jx_o.shape[1]
    taps = cw.shape[0]

    @pl.when(i == 0)
    def _():
        unit, _inv = norm_rows(halo[...])
        before = nn((unit * gain[...]).astype(bf16), wj[:, :width])
        ext[0:8, :] = before.astype(bf16).astype(f32)[8:16]
        run[...] = jnp.zeros_like(run)
        dec[...] = jnp.ones_like(dec)

    unit, _inv = norm_rows(tok[...])
    normed = (unit * gain[...]).astype(bf16)
    nrm_o[...] = normed
    product = nn(normed, wj[...])
    joined = product[:, :width].astype(bf16)
    jx_o[...] = joined[:, :inner]
    jb_o[...] = joined[:, inner:]
    ext[8 : 8 + STRETCH, :] = joined.astype(f32)
    pos = base + iota((STRETCH, 128), 0)
    first_of = segment_start(pos, starts)
    valid = [
        jnp.where(pos - (taps - 1 - k) >= first_of, 1.0, 0.0).astype(f32) for k in range(taps - 1)
    ]
    for g in range(width // 128):
        at = slice(128 * g, 128 * (g + 1))
        acc = cb[:, at] + cw[taps - 1 : taps, at] * ext[8 : 8 + STRETCH, at]
        for k in range(taps - 1):
            low = 8 - (taps - 1) + k
            acc = acc + cw[k : k + 1, at] * (ext[low : low + STRETCH, at] * valid[k])
        sig = jax.nn.sigmoid(acc)
        act = acc * sig
        vbc_o[:, at] = act.astype(bf16)
        slope = sig + act * (1.0 - sig)
        if 128 * g < inner:
            sx_o[:, at] = slope.astype(bf16)
        else:
            sb_o[:, 128 * g - inner : 128 * (g + 1) - inner] = slope
    ext[0:8, :] = ext[STRETCH : STRETCH + 8, :]
    pre = jnp.transpose(product[:, width:])[:HEAD_ROWS] + bias[...]
    step = jax.nn.softplus(pre)
    logd = -step * rate[...]
    cum = exact_rows(logd, tri[...])
    pre_o[...] = pre
    step_o[...] = step
    cum_o[...] = cum
    cum_e = cum[:, STRETCH - 1 : STRETCH]
    where_s = base + iota((1, STRETCH), 1)
    keep = jnp.where(where_s >= end_start, 1.0, 0.0).astype(f32)
    weight = jnp.exp(cum_e - cum) * step * keep
    _cols, both = columns_of([weight])
    spread = nn(both, ew[...])
    v = vbc_o[:, :inner].astype(f32)
    b = vbc_o[:, inner : inner + 128]
    state = tn(b, (v * spread).astype(bf16))
    s_o[0] = state
    through = lanes_of(jnp.exp(cum_e) * flag, e8[...])
    run[...] = through * run[...] + state
    dec[...] = dec[...] * through
    end_o[...] = run[...].astype(bf16)
    dec_o[...] = dec[...]


def mix_kernel(
    info, vbc, step, cum, s_in, inc, normed, gout, wz_out, dskip, gain, e_step, e_scale, e8,
    z_o, out_o, gn_o, br_o, sum_o, st_o,
    run, gram,
):
    i = pl.program_id(0)
    starts, base, _end_start, flag = read_info(info, i)
    inner = gain.shape[1]

    @pl.when(i == 0)
    def _():
        run[...] = inc[...].astype(f32)

    st = run[...].astype(bf16)
    st_o[0] = st
    cum_v = cum[...]
    cum_e = cum_v[:, STRETCH - 1 : STRETCH]
    through = lanes_of(jnp.exp(cum_e) * flag, e8[...])
    run[...] = through * run[...] + s_in[0]

    row_first = segment_start(base + iota((1, STRETCH), 1), starts)
    scale = jnp.exp(cum_v) * jnp.where(row_first < base, 1.0, 0.0).astype(f32)
    cum2 = cum_v * LOG2E
    cols, both = columns_of([cum2, step[...], scale])
    step_x = nn(both, e_step[...])
    scale_x = nn(both, e_scale[...])
    b = vbc[:, inner : inner + 128]
    c = vbc[:, inner + 128 : inner + 256]
    t_at = iota((STRETCH, STRETCH), 0)
    s_at = iota((STRETCH, STRETCH), 1)
    t_first = segment_start(t_at + base, starts)
    mask = (s_at <= t_at) & (s_at + base >= t_first)
    gram[...] = jnp.where(mask, nt(c, b), 0.0)
    carried = nn(c, st) * scale_x
    lane = iota((STRETCH, 128), 1)
    pieces = []
    for p in range(inner // 128):
        at = slice(128 * p, 128 * (p + 1))
        v = vbc[:, at].astype(f32)
        sv = v * step_x[:, at]
        acc = carried[:, at] + dskip[:, at] * v
        for j in range(2):
            h = 2 * p + j
            half = jnp.where((lane < 64) if j == 0 else (lane >= 64), sv, 0.0).astype(bf16)
            gap = cols[:, h : h + 1] - cum2[h : h + 1, :]
            m = (gram[...] * jnp.exp2(jnp.minimum(gap, 0.0))).astype(bf16)
            acc = acc + nn(m, half)
        pieces.append(acc)
    out = jnp.concatenate(pieces, axis=1)
    out_o[...] = out
    zf = nn(normed[...], wz_out[:, :inner])
    z_o[...] = zf
    gated = out * (zf * jax.nn.sigmoid(zf))
    gn = nn(gout[...], wz_out[:, inner:])
    gn_o[...] = gn
    gg = gated * gain[...]
    br_o[...] = nt(wz_out[:, inner:], gg.astype(bf16)).astype(bf16)
    ss = jnp.sum(gated * gated, axis=1, keepdims=True)
    dq = jnp.sum(gn * gg, axis=1, keepdims=True)
    sum_o[...] = jnp.transpose(jnp.where(lane == 0, ss, dq))[0:2]


def gate_kernel(
    info, sums, cum, out, z, gn, vc, st, dskip, gain, e_scale, e8, f_sum,
    gz_o, gb_o, gc_o, n2_o, a_o, gs_o, start_o, misc_o,
    run,
):
    step_id = pl.program_id(0)
    blocks = pl.num_programs(0)
    i = blocks - 1 - step_id
    starts, base, _end_start, flag = read_info(info, i)
    inner = z.shape[1]

    @pl.when(step_id == 0)
    def _():
        run[...] = jnp.zeros_like(run)
        misc_o[...] = jnp.zeros_like(misc_o)

    alpha = lax.rsqrt(sums[0:1, :] / INNER + epsilon)
    beta = alpha * alpha * alpha * sums[1:2, :] / INNER
    cum_v = cum[...]
    row_first = segment_start(base + iota((1, STRETCH), 1), starts)
    scale = jnp.exp(cum_v) * jnp.where(row_first < base, 1.0, 0.0).astype(f32)
    cols, both = columns_of([alpha, beta, jnp.zeros((14, STRETCH), f32), scale])
    alpha_c = cols[:, 0:1]
    beta_c = cols[:, 1:2]
    scale_x = nn(both, e_scale[...])
    v = vc[:, :inner].astype(f32)
    c = vc[:, inner + 128 : inner + 256]
    zf = z[...]
    sig = jax.nn.sigmoid(zf)
    act = zf * sig
    o = out[...]
    gated = o * act
    g_n = gn[...]
    unit = gated * alpha_c
    g_gated = alpha_c * (g_n * gain[...]) - beta_c * gated
    g_out = g_gated * act
    gz_o[...] = (g_gated * o * (sig + act * (1.0 - sig))).astype(bf16)
    gb = g_out.astype(bf16)
    gb_o[...] = gb
    n2_o[...] = (unit * gain[...]).astype(bf16)
    misc_o[0:1, :] += jnp.sum(g_n * unit, axis=0, keepdims=True)
    misc_o[1:2, :] += jnp.sum(g_out * v, axis=0, keepdims=True)
    gf = gb.astype(f32)
    carried = nn(c, st[0]) * scale_x
    prod = gf * (o - dskip[...] * v) + (g_out - gf) * carried
    high, low = halves(prod)
    sums_c = nn(jnp.concatenate([high, low], axis=1), f_sum[...])
    a_o[...] = jnp.transpose(sums_c)[0:HEAD_ROWS]
    gc = (g_out * scale_x).astype(bf16)
    gc_o[...] = gc
    gs = tn(c, gc)
    gs_o[0] = gs
    through = lanes_of(jnp.exp(cum_v[:, STRETCH - 1 : STRETCH]) * flag, e8[...])
    run[...] = through * run[...] + gs
    start_o[...] = run[...].astype(bf16)


def scan_kernel(
    info, vbc, gb, gc, step, cum, pre, a_sum, st, gs_in, outg, sx, sb, jx, jb, cw, dskip, rate,
    e_step, e_w, e8, f_one, f_two, f_three, tril,
    gcat_o, tail_o, head_o, misc_o, dt_o,
    run, ext, gram, acc,
):
    step_id = pl.program_id(0)
    blocks = pl.num_programs(0)
    i = blocks - 1 - step_id
    starts, base, end_start, flag = read_info(info, i)
    inner = gb.shape[1]
    taps, width = cw.shape

    @pl.when(step_id == 0)
    def _():
        run[...] = outg[...].astype(f32)
        ext[STRETCH : STRETCH + 8, :] = jnp.zeros((8, width), f32)
        misc_o[...] = jnp.zeros_like(misc_o)
        dt_o[...] = jnp.zeros_like(dt_o)

    cum_v = cum[...]
    step_v = step[...]
    cum_e = cum_v[:, STRETCH - 1 : STRETCH]
    after = run[...]
    low_after = after.astype(bf16)
    state = st[0]
    through = lanes_of(jnp.exp(cum_e) * flag, e8[...])
    g_through = jnp.sum(after * state.astype(f32), axis=0, keepdims=True) * through
    end_more = jnp.sum(e8[...] * g_through, axis=1, keepdims=True)
    run[...] = through * after + gs_in[0]

    where_s = base + iota((1, STRETCH), 1)
    row_first = segment_start(where_s, starts)
    end_decay = jnp.exp(cum_e - cum_v) * jnp.where(where_s >= end_start, 1.0, 0.0).astype(f32)
    weight = end_decay * step_v
    cum2 = cum_v * LOG2E
    cols, both = columns_of([cum2, step_v, weight])
    step_x = nn(both, e_step[...])
    w_x = nn(both, e_w[...])
    b = vbc[:, inner : inner + 128]
    c = vbc[:, inner + 128 : inner + 256]
    s_at = iota((STRETCH, STRETCH), 0)
    t_at = iota((STRETCH, STRETCH), 1)
    mask = (s_at <= t_at) & (s_at + base >= row_first)
    gram[...] = jnp.where(mask, nt(b, c), 0.0)
    acc[...] = jnp.zeros_like(acc)
    y = nn(b, low_after)
    lane = iota((STRETCH, 128), 1)
    us = []
    svs = []
    for p in range(inner // 128):
        at = slice(128 * p, 128 * (p + 1))
        sv = (vbc[:, at].astype(f32) * step_x[:, at]).astype(bf16).astype(f32)
        svs.append(sv)
        g_pair = gb[:, at]
        g_wide = g_pair.astype(f32)
        u = jnp.zeros((STRETCH, 128), f32)
        for j in range(2):
            h = 2 * p + j
            side = (lane < 64) if j == 0 else (lane >= 64)
            gap = cum2[h : h + 1, :] - cols[:, h : h + 1]
            decay = jnp.exp2(jnp.minimum(gap, 0.0))
            m = (gram[...] * decay).astype(bf16)
            u = u + nn(m, jnp.where(side, g_wide, 0.0).astype(bf16))
            g_m = nt(jnp.where(side, sv, 0.0).astype(bf16), g_pair)
            acc[...] += g_m * decay
        us.append(u)
    u = jnp.concatenate(us, axis=1)
    g_gram = jnp.where(mask, acc[...], 0.0).astype(bf16)
    v = vbc[:, :inner].astype(f32)
    gf = gb[...].astype(f32)
    wv = (v * w_x).astype(bf16)
    ext[0:STRETCH, inner : inner + 128] = (nn(g_gram, c) + nt(wv, low_after)) * sb[:, :128]
    ext[0:STRETCH, inner + 128 :] = (tn(g_gram, b) + nt(gc[...], state)) * sb[:, 128:]
    gv = dskip[...] * gf + step_x * u + w_x * y
    h1, l1 = halves(v * u)
    h2, l2 = halves(v * y)
    h3, l3 = halves(jnp.concatenate(svs, axis=1) * u)
    sums_c = (
        nn(jnp.concatenate([h1, l1], axis=1), f_one[...])
        + nn(jnp.concatenate([h2, l2], axis=1), f_two[...])
        + nn(jnp.concatenate([h3, l3], axis=1), f_three[...])
    )
    sums_r = jnp.transpose(sums_c)
    g_step0 = sums_r[0:HEAD_ROWS]
    g_end = sums_r[HEAD_ROWS : 2 * HEAD_ROWS]
    ends = g_end * weight
    g_cum = a_sum[...] - sums_r[2 * HEAD_ROWS : 3 * HEAD_ROWS] - ends
    end_add = jnp.sum(ends, axis=1, keepdims=True) + end_more
    g_log = exact_rows(g_cum, tril[...]) + end_add
    g_step = g_step0 + g_end * end_decay - g_log * rate[...]
    g_pre_dt = g_step * jax.nn.sigmoid(pre[...])
    dt_o[0:HEAD_ROWS, :] += g_log * (-step_v * rate[...])
    dt_o[HEAD_ROWS:, :] += g_pre_dt
    pad = jnp.zeros((128 - HEAD_ROWS, STRETCH), f32)
    gcat_o[:, width:] = jnp.transpose(jnp.concatenate([g_pre_dt, pad], axis=0)).astype(bf16)

    ext[0:STRETCH, :inner] = gv * sx[...].astype(f32)
    pos = base + iota((STRETCH, 128), 0)
    ok = [
        jnp.where(joined_ok(pos, d, starts), 1.0, 0.0).astype(f32) for d in range(taps - 1, 0, -1)
    ]
    for g in range(width // 128):
        at = slice(128 * g, 128 * (g + 1))
        if 128 * g < inner:
            j_f = jx[:, at].astype(f32)
        else:
            j_f = jb[:, 128 * g - inner : 128 * (g + 1) - inner].astype(f32)
        own = ext[0:STRETCH, at]
        misc_o[taps : taps + 1, at] += jnp.sum(own, axis=0, keepdims=True)
        misc_o[taps - 1 : taps, at] += jnp.sum(own * j_f, axis=0, keepdims=True)
        total = own * cw[taps - 1 : taps, at]
        for k in range(taps - 1):
            d = taps - 1 - k
            term = ext[d : d + STRETCH, at] * ok[k]
            misc_o[k : k + 1, at] += jnp.sum(term * j_f, axis=0, keepdims=True)
            total = total + term * cw[k : k + 1, at]
        gcat_o[:, at] = total.astype(bf16)

        @pl.when(step_id == 0)
        def _():
            tail_o[:, at] = total[STRETCH - 8 :]

    head_o[...] = ext[0:8, :]
    ext[STRETCH : STRETCH + 8, :] = ext[0:8, :]


def exit_kernel(
    info, tok, gz, gcat, tail, nxt, last_j, cw, gain, wz_out, wj,
    gr_o, rim_o, rim_w_o, gain_o,
    fix,
):
    step_id = pl.program_id(0)
    blocks = pl.num_programs(0)
    i = blocks - 1 - step_id
    starts, base, _end_start, _flag = read_info(info, i)
    taps, width = cw.shape
    inner = gz.shape[1]

    @pl.when(step_id == 0)
    def _():
        gain_o[...] = jnp.zeros_like(gain_o)
        fix[0:8, :] = jnp.zeros((8, width), f32)
        fix[8:16, :] = nxt[...]
        places = base + STRETCH - 8 + iota((8, 128), 0)
        wide = last_j[8:16, :].astype(f32)
        total = tail[...]
        for k in range(taps - 1):
            d = taps - 1 - k
            ok = jnp.where(joined_ok(places, d, starts), 1.0, 0.0).astype(f32)
            inside = jnp.where(iota((8, width), 0) >= 8 - d, fix[d : d + 8, :], 0.0)
            term = inside * jnp.concatenate([ok] * (width // 128), axis=1)
            total = total + term * cw[k : k + 1, :]
            rim_w_o[k : k + 1, :] = jnp.sum(term * wide, axis=0, keepdims=True)
        rim_w_o[taps - 1 : 8, :] = jnp.zeros((9 - taps, width), f32)
        fix[0:8, :] = jnp.zeros((8, width), f32)
        fix[8:16, :] = total.astype(bf16).astype(f32) - tail[...].astype(bf16).astype(f32)
        rim_o[...] = fix[...].astype(bf16)

    g_normed = nt(gz[...], wz_out[:, :inner]) + nt(gcat[...], wj[...])

    def finish(g_normed):
        unit, inverse = norm_rows(tok[...])
        scaled = g_normed * gain[...]
        mean = jnp.mean(scaled * unit, axis=1, keepdims=True)
        gr_o[...] = jnp.transpose(inverse * (scaled - unit * mean)).astype(bf16)
        gain_o[...] += jnp.sum(g_normed * unit, axis=0, keepdims=True)

    @pl.when(step_id == 0)
    def _():
        more = nt(rim_o[...], wj[:, :width])
        finish(g_normed + jnp.concatenate([jnp.zeros((STRETCH - 16, more.shape[1]), f32), more]))

    @pl.when(step_id > 0)
    def _():
        finish(g_normed)


def finish_kernel(parts, scaled, place, part, base, *rest):
    out = rest[-1]
    wide = part[...].astype(f32)
    if scaled:
        wide = wide * lax.rsqrt(rest[0][0:1, :] / INNER + epsilon)
    add = jnp.transpose(wide)
    size = out.shape[1]
    for k in range(parts):

        @pl.when(place[0] == k)
        def _():
            out[...] = (base[:, size * k : size * (k + 1)].astype(f32) + add).astype(bf16)


def constants(inner, heads):
    lane_head = np.arange(inner) // (inner // heads)
    e8 = (np.arange(HEAD_ROWS)[:, None] == lane_head[None, :]).astype(np.float32)

    def spread(kind):
        m = np.zeros((128, inner), np.float32)
        m[HEAD_ROWS * kind : HEAD_ROWS * (kind + 1)] = e8
        return jnp.asarray(np.concatenate([m, m], axis=0), bf16)

    def gather(kind):
        m = np.zeros((inner, 128), np.float32)
        m[:, HEAD_ROWS * kind : HEAD_ROWS * (kind + 1)] = e8.T
        return jnp.asarray(np.concatenate([m, m], axis=0), bf16)

    at = np.arange(STRETCH)
    upper = jnp.asarray((at[:, None] <= at[None, :]).astype(np.float32), bf16)
    lower = jnp.asarray((at[:, None] >= at[None, :]).astype(np.float32), bf16)
    return jnp.asarray(e8), spread, gather, upper, lower


def passed_along(block, axis, distance):
    devices = range(lax.axis_size(axis))
    route = [(i - distance, i) for i in devices if i - distance in devices]
    return lax.ppermute(block, axis, route)


def entering(decay, state, axis, reverse):
    size = lax.axis_size(axis)
    if size == 2:
        return passed_along(state, axis, -1 if reverse else 1)
    index = lax.axis_index(axis)
    decays = lax.all_gather(decay.astype(bf16), axis)
    states = lax.all_gather(state, axis)

    def lap(k, before):
        at = size - 1 - k if reverse else k
        reached = at > index if reverse else at < index
        new = decays[at].astype(f32) * before + states[at].astype(f32)
        return jnp.where(reached, new, before)

    return lax.fori_loop(0, size, lap, jnp.zeros(state.shape, f32)).astype(bf16)


def call(kernel, blocks, ins, outs, scratch, micros=0):
    def spec(shape, how):
        if how == "smem":
            return pl.BlockSpec(memory_space=pltpu.SMEM)
        return pl.BlockSpec(shape, how)

    return pl.pallas_call(
        kernel,
        grid=(blocks,),
        in_specs=[spec(shape, how) for _a, shape, how in ins],
        out_specs=[spec(shape, how) for _s, shape, how in outs],
        out_shape=[s for s, _sh, _h in outs],
        scratch_shapes=scratch,
        cost_estimate=pl.CostEstimate(
            flops=0, transcendentals=0, bytes_accessed=3_000_000 * micros
        )
        if micros
        else None,
        compiler_params=pltpu.CompilerParams(
            dimension_semantics=("arbitrary",), vmem_limit_bytes=56 * 1024 * 1024
        ),
    )(*[a for a, _s, _h in ins])


def local(
    tokens, grad_out, lengths, norm_gain, w_z, w_x, w_bc, w_dt, conv_x_w, conv_x_b,
    conv_bc_w, conv_bc_b, dt_bias, a_log, d_skip, gate_gain, w_out,
):
    rows, model = tokens.shape
    inner = w_z.shape[1]
    heads = dt_bias.shape[0]
    states = w_bc.shape[1] // 2
    taps = conv_x_w.shape[0]
    blocks = rows // STRETCH
    width = inner + 2 * states
    tp_size = lax.axis_size("tp")
    slice_width = model // tp_size
    tp_index = lax.axis_index("tp")
    ctx_index = lax.axis_index("ctx")
    e8, spread, gather, upper, lower = constants(inner, heads)

    w_joined = lax.all_gather(
        jnp.concatenate([w_x, w_bc, jnp.pad(w_dt, ((0, 0), (0, 128 - heads)))], axis=1),
        "fsdp",
        axis=0,
        tiled=True,
    )
    wz_out = lax.all_gather(jnp.concatenate([w_z, w_out.T], axis=1), "fsdp", axis=0, tiled=True)

    starts = jnp.cumsum(lengths[0]) - lengths[0]
    info = jnp.concatenate([(ctx_index * rows).astype(jnp.int32)[None], starts.astype(jnp.int32)])
    halo = passed_along(tokens[rows - 16 :], "ctx", 1)
    gain = norm_gain[None, :]
    conv_w = jnp.concatenate([conv_x_w, conv_bc_w], axis=1)
    conv_b = jnp.concatenate([conv_x_b, conv_bc_b])[None, :]

    def head_rows(x):
        return jnp.broadcast_to(jnp.pad(x, (0, HEAD_ROWS - heads))[:, None], (HEAD_ROWS, STRETCH))

    bias = head_rows(dt_bias)
    rate = head_rows(jnp.exp(a_log))
    per_head = inner // heads
    dskip = jnp.repeat(d_skip, per_head)[None, :]
    ggain = gate_gain[None, :]

    def shape(dims, kind):
        return jax.ShapeDtypeStruct(dims, kind)

    def whole(x):
        return (x, x.shape, lambda i: (0,) * x.ndim)

    def by_rows(x, flip=False):
        if flip:
            return (x, (STRETCH, x.shape[1]), lambda i: (blocks - 1 - i, 0))
        return (x, (STRETCH, x.shape[1]), lambda i: (i, 0))

    def by_lanes(x, flip=False):
        if flip:
            return (x, (x.shape[0], STRETCH), lambda i: (0, blocks - 1 - i))
        return (x, (x.shape[0], STRETCH), lambda i: (0, i))

    def by_block(x, flip=False):
        if flip:
            return (x, (1,) + x.shape[1:], lambda i: (blocks - 1 - i, 0, 0))
        return (x, (1,) + x.shape[1:], lambda i: (i, 0, 0))

    def fixed(x):
        return (x, x.shape, lambda i: (0,) * len(x.shape))

    info_in = (info, None, "smem")
    state_dims = (blocks, states, inner)
    normed, joined_x, joined_bc, vbc, slope_x, slope_bc, pre, step, cum, s_part, end_state, decay = call(
        entry_kernel,
        blocks,
        [
            info_in, by_rows(tokens), whole(halo), whole(gain), whole(w_joined),
            whole(conv_w), whole(conv_b), whole(bias), whole(rate), whole(upper),
            whole(spread(0)), whole(e8),
        ],
        [
            by_rows(shape((rows, model), bf16)),
            by_rows(shape((rows, inner), bf16)),
            by_rows(shape((rows, 2 * states), bf16)),
            by_rows(shape((rows, width), bf16)),
            by_rows(shape((rows, inner), bf16)),
            by_rows(shape((rows, 2 * states), f32)),
            by_lanes(shape((HEAD_ROWS, rows), f32)),
            by_lanes(shape((HEAD_ROWS, rows), f32)),
            by_lanes(shape((HEAD_ROWS, rows), f32)),
            by_block(shape(state_dims, f32)),
            fixed(shape((states, inner), bf16)),
            fixed(shape((1, inner), f32)),
        ],
        [
            pltpu.VMEM((STRETCH + 8, width), f32),
            pltpu.VMEM((states, inner), f32),
            pltpu.VMEM((1, inner), f32),
        ],
    )
    incoming = entering(decay, end_state, "ctx", False)
    z_part, out, gn, branch, sums, state_in = call(
        mix_kernel,
        blocks,
        [
            info_in, by_rows(vbc), by_lanes(step), by_lanes(cum), by_block(s_part),
            whole(incoming), by_rows(normed), by_rows(grad_out), whole(wz_out), whole(dskip),
            whole(ggain), whole(spread(1)), whole(spread(2)), whole(e8),
        ],
        [
            by_rows(shape((rows, inner), f32)),
            by_rows(shape((rows, inner), f32)),
            by_rows(shape((rows, inner), f32)),
            by_lanes(shape((model, rows), bf16)),
            by_lanes(shape((2, rows), f32)),
            by_block(shape(state_dims, bf16)),
        ],
        [pltpu.VMEM((states, inner), f32), pltpu.VMEM((STRETCH, STRETCH), f32)],
    )
    sums = lax.psum(sums, "tp")
    branch = lax.psum_scatter(branch, "tp", scatter_dimension=0, tiled=True)
    g_z, g_b, g_c, normed_two, a_sum, gs_part, start_state, misc_gate = call(
        gate_kernel,
        blocks,
        [
            info_in, by_lanes(sums, True), by_lanes(cum, True), by_rows(out, True),
            by_rows(z_part, True), by_rows(gn, True), by_rows(vbc, True), by_block(state_in, True),
            whole(dskip), whole(ggain), whole(spread(2)), whole(e8), whole(gather(0)),
        ],
        [
            by_rows(shape((rows, inner), bf16), True),
            by_rows(shape((rows, inner), bf16), True),
            by_rows(shape((rows, inner), bf16), True),
            by_rows(shape((rows, inner), bf16), True),
            by_lanes(shape((HEAD_ROWS, rows), f32), True),
            by_block(shape(state_dims, f32), True),
            fixed(shape((states, inner), bf16)),
            fixed(shape((8, inner), f32)),
        ],
        [pltpu.VMEM((states, inner), f32)],
    )
    outgoing = entering(decay, start_state, "ctx", True)
    g_cat, tail, head, misc_scan, misc_dt = call(
        scan_kernel,
        blocks,
        [
            info_in, by_rows(vbc, True), by_rows(g_b, True), by_rows(g_c, True),
            by_lanes(step, True), by_lanes(cum, True), by_lanes(pre, True), by_lanes(a_sum, True),
            by_block(state_in, True), by_block(gs_part, True), whole(outgoing),
            by_rows(slope_x, True), by_rows(slope_bc, True), by_rows(joined_x, True),
            by_rows(joined_bc, True), whole(conv_w), whole(dskip), whole(rate), whole(spread(1)),
            whole(spread(2)), whole(e8), whole(gather(0)), whole(gather(1)),
            whole(gather(2)), whole(lower),
        ],
        [
            by_rows(shape((rows, width + 128), bf16), True),
            fixed(shape((8, width), f32)),
            fixed(shape((8, width), f32)),
            fixed(shape((8, width), f32)),
            fixed(shape((2 * HEAD_ROWS, STRETCH), f32)),
        ],
        [
            pltpu.VMEM((states, inner), f32),
            pltpu.VMEM((STRETCH + 8, width), f32),
            pltpu.VMEM((STRETCH, STRETCH), f32),
            pltpu.VMEM((STRETCH, STRETCH), f32),
        ],
    )
    next_rows = passed_along(head, "ctx", -1)
    last_joined = jnp.concatenate([joined_x[rows - 16 :], joined_bc[rows - 16 :]], axis=1)
    g_resid, rim, rim_w, gain_part = call(
        exit_kernel,
        blocks,
        [
            info_in, by_rows(tokens, True), by_rows(g_z, True), by_rows(g_cat, True),
            whole(tail), whole(next_rows), whole(last_joined), whole(conv_w), whole(gain),
            whole(wz_out), whole(w_joined),
        ],
        [
            by_lanes(shape((model, rows), bf16), True),
            fixed(shape((16, width), bf16)),
            fixed(shape((8, width), f32)),
            fixed(shape((1, model), f32)),
        ],
        [pltpu.VMEM((16, width), f32)],
    )
    g_resid = lax.psum_scatter(g_resid, "tp", scatter_dimension=0, tiled=True)

    part_out = tn(grad_out, normed_two)
    part_z = tn(normed, g_z)
    part_cat = tn(normed, g_cat)
    part_rim = tn(normed[rows - 16 :], rim)
    part_cat = part_cat + jnp.pad(part_rim, ((0, 0), (0, 128)))
    parts = jnp.concatenate([part_out, part_z, part_cat], axis=1).astype(bf16)
    shard = lax.psum_scatter(parts, "fsdp", scatter_dimension=0, tiled=True)
    shard = lax.psum(shard, "ctx").astype(f32)
    grad_w_out = shard[:, :inner].T
    grad_w_z = shard[:, inner : 2 * inner]
    grad_w_x = shard[:, 2 * inner : 3 * inner]
    grad_w_bc = lax.psum(shard[:, 3 * inner : 3 * inner + 2 * states], "tp")
    grad_w_dt = shard[:, 3 * inner + 2 * states : 3 * inner + 2 * states + heads]

    misc_scan = misc_scan + rim_w
    over_all = (gain_part[0], misc_scan[:taps, inner:], misc_scan[taps, inner:])
    sum_gain, grad_conv_bc_w, grad_conv_bc_b = lax.psum(over_all, ("fsdp", "ctx", "tp"))
    small = (
        misc_scan[:taps, :inner],
        misc_scan[taps, :inner],
        jnp.sum(misc_dt[HEAD_ROWS : HEAD_ROWS + heads], axis=1),
        jnp.sum(misc_dt[:heads], axis=1),
        jnp.sum(misc_gate[1].reshape(heads, per_head), axis=1),
        misc_gate[0],
    )
    (
        grad_conv_x_w, grad_conv_x_b, grad_dt_bias, grad_a_log, grad_d_skip, grad_gate_gain,
    ) = lax.psum(small, ("fsdp", "ctx"))
    here = tp_index * slice_width
    grad_norm_gain = lax.dynamic_slice_in_dim(sum_gain, here, slice_width, 0)

    place = tp_index.astype(jnp.int32)[None]

    def finish(part, base, scaled):
        extra = [by_lanes(sums)] if scaled else []
        return call(
            functools.partial(finish_kernel, tp_size, scaled),
            blocks,
            [(place, None, "smem"), by_lanes(part), by_rows(base)] + extra,
            [by_rows(shape((rows, slice_width), bf16))],
            [],
        )[0]

    layer_out = finish(branch, tokens, True)
    grad_tokens = finish(g_resid, grad_out, False)
    return (
        layer_out, grad_tokens, grad_norm_gain, grad_w_z, grad_w_x, grad_w_bc, grad_w_dt,
        grad_conv_x_w, grad_conv_x_b, grad_conv_bc_w, grad_conv_bc_b, grad_dt_bias, grad_a_log,
        grad_d_skip, grad_gate_gain, grad_w_out,
    )


def solution(mesh):
    both = ("fsdp", "ctx")
    in_specs = (
        P(both, None), P(both, None), P("fsdp", None), P(), P("fsdp", "tp"), P("fsdp", "tp"),
        P("fsdp", None), P("fsdp", "tp"), P(None, "tp"), P("tp"), P(), P(), P("tp"), P("tp"),
        P("tp"), P("tp"), P("tp", "fsdp"),
    )
    out_specs = (
        P(both, "tp"), P(both, "tp"), P("tp"), P("fsdp", "tp"), P("fsdp", "tp"), P("fsdp", None),
        P("fsdp", "tp"), P(None, "tp"), P("tp"), P(), P(), P("tp"), P("tp"), P("tp"), P("tp"),
        P("tp", "fsdp"),
    )
    return jax.shard_map(local, mesh=mesh, in_specs=in_specs, out_specs=out_specs, check_vma=False)
```

time: 938 us -> 507 us (0.54); the launches traced: 922 us -> 505 us
  matrix products: 258 us -> 15.6 us
  other arithmetic: 194 us -> 7.37 us
  Pallas kernels: 0 us -> 142 us
  local copies, waits for them, and re-layouts: 161 us -> 31.4 us
  waiting for transfers between devices: 154 us -> 202 us
  blocking collectives: 132 us -> 85.6 us
    dot_general x105 -> x4, matrix products: 258 us -> 15.6 us  [tn(): lax.dot_general(left, right, (((0,), (0,)), ((), ())), preferred_element_...]
    pallas_call x0 -> x7, Pallas kernels: none -> 142 us  [call(): pl.pallas_call(kernel, grid=(blocks,), in_specs=[spec(shape, how) for _a,...]
    all_gather x7 -> x0, blocking collectives: 54.8 us -> none  [the longest x1 11.8 us: local(): lax.all_gather(w_x, 'fsdp', axis=0, tiled=True)]
    reduce_sum x9 -> x2, other arithmetic: 40.6 us -> 0.26 us  [the longest x1 0.14 us: local(): jnp.sum(misc_dt[:heads], axis=1)]
    add x28 -> x1, other arithmetic: 39.6 us -> 0.01 us  [local(): misc_scan = misc_scan + rim_w]
    unnamed x4 -> x8, waiting for transfers between devices: 0.07 us -> 36.8 us
    convert_element_type x17 -> x1, other arithmetic: 30.8 us -> 0.11 us  [local(): shard = lax.psum(shard, 'ctx').astype(f32)]
    another operation x17 -> x1, other arithmetic: 27.3 us -> 0.83 us
  transfers between devices with their start and end apart: 6 -> 11, of which waited for: 3 -> 6; matrix products, arithmetic and copies ran while one was open for 20% -> 7% of each run, Pallas kernels for 0% -> 7%
where the time goes in v1:
time: 507 us; the launch traced here: 505 us
  waiting for transfers between devices  202 us (40%)
  Pallas kernels  142 us (28%)
  blocking collectives  85.6 us (17%)
  local copies, waits for them, and re-layouts  31.4 us (6%)
  matrix products  15.6 us (3%)
  between operations  14.5 us (3%)
  other arithmetic  7.37 us (1%)
  starting transfers between devices  7.04 us (1%)
    pallas_call x7, Pallas kernels, call(): pl.pallas_call(kernel, grid=(blocks,), in_specs=[spec(shape, how) for _a,...  142 us
    reduce_scatter x1, waiting for transfers between devices, local(): g_resid = lax.psum_scatter(g_resid, 'tp', scatter_dimension=0, tiled=True)  76.5 us
    reduce_scatter x1, waiting for transfers between devices, local(): branch = lax.psum_scatter(branch, 'tp', scatter_dimension=0, tiled=True)  51.6 us
    psum x1, blocking collectives, local(): lax.psum(over_all, ('fsdp', 'ctx', 'tp'))  40.9 us
    unnamed x8, waiting for transfers between devices  36.8 us
    psum x1, blocking collectives, local(): lax.psum(small, ('fsdp', 'ctx'))  24.4 us
    psum x1, blocking collectives, local(): sums = lax.psum(sums, 'tp')  20.3 us
    psum x1, waiting for transfers between devices, local(): shard = lax.psum(shard, 'ctx').astype(f32)  19.5 us
  transfers between devices with their start and end apart: 11, of which 6 were waited for; matrix products, arithmetic and copies ran while one was open for 7% of the time, Pallas kernels for 7%

profile of v1, /device:TPU:0, one launch (start us, length us, event | category | flops | bytes accessed | tf_op | source)
XLA Modules:
  0.0 505.2 jit_solution(6344276285080694706)
XLA Ops:
  8.1 1.7 fusion.2
  9.8 1.7 pad_maximum_fusion.1
  12.4 2.4 collective-permute-start
  19.0 1.3 broadcast_in_dim.32.gain
  23.5 1.2 broadcast_in_dim.37.gain
  24.7 16.0 %all-gather.3.cloned.1.call-done.wj = bf16[768,768]{1,0:T(8,128)(2,1)} async-done(((bf16[192,768]{1,0:T(8,128)(2,1)}), bf16[768,768]{1,0:T(8,128)(2,1)}) %all-gather.3.cloned.1.call-update) | async-done | bytes 1179664 | tf_op jit(solution)/shard_map/all_gather | solution.py:563
  42.1 23.9 %shard_map.405 = (bf16[3072,768]{1,0:T(8,128)(2,1)}, bf16[3072,384]{1,0:T(8,128)(2,1)}, bf16[3072,256]{1,0:T(8,128)(2,1)}, bf16[3072,640]{1,0:T(8,128)(2,1)}, bf...) custom-call(s32[5]{0:T(128)} %pad_add_fusion.info, ...), custom_call_target="tpu_custom_call" | custom-call | tf_op jit(solution)/shard_map/pallas_call | solution.py:528
  66.0 1.6 collective-permute-start.1
  71.5 20.9 %shard_map.406 = (f32[3072,384]{1,0:T(8,128)}, f32[3072,384]{1,0:T(8,128)}, f32[3072,384]{1,0:T(8,128)}, bf16[768,3072]{1,0:T(8,128)(2,1)}, f32[2,3072]{1,0:T(2,128)}, /*index=5*/bf16[12,128,384]{2,1,0:T(8,128)(2,1)}) custom-call(s32[5]{0:T(128)} %pad_add_fusion.info, bf16[3072,640]{1,0:T(8,128)(2,1)} %get-tuple-element.50.vbc.vc, ...), custom_call_target="tpu_custom_call" | custom-call | tf_op jit(solution)/shard_map/pallas_call | solution.py:528
  92.4 20.3 %psum.84.rest_0_.sums = f32[2,3072]{1,0:T(2,128)} all-reduce(f32[2,3072]{1,0:T(2,128)} %get-tuple-element.57), channel_id=1, replica_groups=mesh['fsdp'=4,'ctx'=2,'tp'=4] {'tp'}, use_global_device_ids=true, to_apply=%region_2.3 | all-reduce | flops 6144 | bytes 49152 | tf_op jit(solution)/shard_map/psum | solution.py:660
  112.7 16.8 %shard_map.408 = (bf16[3072,384]{1,0:T(8,128)(2,1)}, bf16[3072,384]{1,0:T(8,128)(2,1)}, bf16[3072,384]{1,0:T(8,128)(2,1)}, bf16[3072,384]{1,0:T(8,128)(2,1)}, f3...) custom-call(s32[5]{0:T(128)} %pad_add_fusion.info, ...), custom_call_target="tpu_custom_call" | custom-call | tf_op jit(solution)/shard_map/pallas_call | solution.py:528
  129.5 1.3 collective-permute-start.2
  130.8 6.1 %convolution_convert_fusion = bf16[768,384]{0,1:T(8,128)(2,1)} fusion(bf16[3072,768]{1,0:T(8,128)(2,1)} %get-tuple-element.55.normed, bf16[3072,384]{1,0:T(8,128)(2,1)} %get-tuple-element.62.gz), kind=kOutput, calls=%fused_computation.2 | convolution fusion | flops 1812234240 | bytes 7667712 | tf_op jit(solution)/shard_map/dot_general | solution.py:30
  137.5 44.0 %shard_map.409 = (bf16[3072,768]{1,0:T(8,128)(2,1)}, f32[8,640]{1,0:T(8,128)}, f32[8,640]{1,0:T(8,128)}, f32[8,640]{1,0:T(8,128)}, f32[16,256]{1,0:T(8,128)}) custom-call(s32[5]{0:T(128)} %pad_add_fusion.info, bf16[3072,640]{1,0:T(8,128)(2,1)} %get-tuple-element.50.vbc.vc, bf16[3072,384]{1,0:T(8,128)(2,1)} %get-tuple-element.63.gb, ...), custom_call_target="tpu_custom_call" | custom-call | tf_op jit(solution)/shard_map/pallas_call | solution.py:528
  181.6 1.5 collective-permute-start.3
  183.1 2.0 fusion
  185.8 18.5 %shard_map.410 = (bf16[768,3072]{1,0:T(8,128)(2,1)}, bf16[16,640]{1,0:T(8,128)(2,1)}, f32[8,640]{1,0:T(8,128)}, f32[1,768]{1,0:T(1,128)}) custom-call(s32[5]{0:T(128)} %pad_add_fusion.info, bf16[3072,768]{1,0:T(8,128)(2,1)} %tok.3, bf16[3072,384]{1,0:T(8,128)(2,1)} %get-tuple-element.62.gz, bf16[3072,768]{1,0:T(8,128)(2,1)} %get-tuple-element.73.gcat, ...), custom_call_target="tpu_custom_call" | custom-call | tf_op jit(solution)/shard_map/pallas_call | solution.py:528
  205.5 6.3 %add_convert_fusion = bf16[768,768]{0,1:T(8,128)(2,1)S(1)} fusion(f32[768,640]{0,1:T(8,128)S(1)} %fusion.3, bf16[3072,768]{1,0:T(8,128)(2,1)S(1)} %bitcast.24, bf16[3072,768]{1,0:T(8,128)(2,1)} %get-tuple-element.73.gcat), kind=kOutput, calls=%fused_computation.1 | convolution fusion | flops 3625058304 | bytes 12582912 | tf_op jit(solution)/shard_map/dot_general | solution.py:30
  212.0 2.5 copy.60
  214.5 35.5 %reduce-scatter.10.cloned.1.call-done = bf16[192,1536]{1,0:T(8,128)(2,1)} async-done(((bf16[768,1536]{1,0:T(8,128)(2,1)}), bf16[192,1536]{1,0:T(8,128)(2,1)}) %reduce-scatter.10.cloned.1.call-update) | async-done | bytes 589840
  250.1 2.2 copy.61
  252.4 19.5 %all-reduce.9.cloned.1.call-done = bf16[192,1536]{0,1:T(8,128)(2,1)} async-done(((bf16[192,1536]{0,1:T(8,128)(2,1)}), bf16[192,1536]{0,1:T(8,128)(2,1)}) %all-reduce.9.cloned.1.call-update) | async-done | bytes 589840 | tf_op jit(solution)/shard_map/psum | solution.py:736
  271.8 1.6 slice.70
  276.1 40.9 %all-reduce.4 = (f32[768]{0:T(1024)S(1)}, f32[4,256]{1,0:T(4,128)}, f32[256]{0:T(256)}) all-reduce(f32[768]{0:T(1024)S(1)} %reduce, f32[4,256]{1,0:T(4,128)S(1)} %slice.74, f32[256]{0:T(256)S(1)} %bitcast.26), channel_id=1, replica_groups=mesh['fsdp'=4,'ctx'=2,'tp'=4] {'fsdp','ctx','tp'}, use_global_device_ids=true, to_apply=%region_4.5 | all-reduce | flops 2048 | bytes 16384 | tf_op jit(solution)/shard_map/psum | solution.py:745
  317.6 24.4 %all-reduce.5 = (f32[4,384]{1,0:T(4,128)}, f32[384]{0:T(512)}, f32[6]{0:T(128)}, f32[6]{0:T(128)}, f32[6]{0:T(128)}, /*index=5*/f32[384]{0:T(512)}) all-reduce(f32[4,384]{1,0:T(4,128)S(1)} %slice.72, f32[384]{0:T(512)S(1)} %slice_reduce_fusion.2, ...), channel_id=1, replica_groups=mesh['fsdp'=4,'ctx'=2,'tp'=4] {'fsdp','ctx'}, use_global_device_ids=true, to_apply=%region_8.9 | all-reduce | flops 2322 | bytes 18576 | tf_op jit(solution)/shard_map/psum | solution.py:756
  345.4 1.7 copy.58
  347.2 51.6 %reduce-scatter.6.cloned.1.call-done.part = bf16[192,3072]{1,0:T(8,128)(2,1)} async-done(((bf16[768,3072]{1,0:T(8,128)(2,1)}), bf16[192,3072]{1,0:T(8,128)(2,1)}) %reduce-scatter.6.cloned.1.call-update) | async-done | bytes 1179664 | tf_op jit(solution)/shard_map/reduce_scatter | solution.py:661
  398.8 8.9 %shard_map.407 = bf16[3072,192]{1,0:T(8,128)(2,1)} custom-call(s32[1]{0:T(128)} %bitcast.place, bf16[192,3072]{1,0:T(8,128)(2,1)} %reduce-scatter.6.cloned.1.call-done.part, bf16[3072,768]{1,0:T(8,128)(2,1)} %tok.3, f32[2,3072]{1,0:T(2,128)} %psum.84.rest_0_.sums), custom_call_target="tpu_custom_call" | custom-call | tf_op jit(solution)/shard_map/pallas_call | solution.py:528
  407.7 2.7 copy.54
  410.4 76.5 %reduce-scatter.8.cloned.1.call-done.part = bf16[192,3072]{1,0:T(8,128)(2,1)} async-done(((bf16[768,3072]{1,0:T(8,128)(2,1)}), bf16[192,3072]{1,0:T(8,128)(2,1)}) %reduce-scatter.8.cloned.1.call-update) | async-done | bytes 1179664 | tf_op jit(solution)/shard_map/reduce_scatter | solution.py:727
  486.9 8.9 %shard_map.411 = bf16[3072,192]{1,0:T(8,128)(2,1)} custom-call(s32[1]{0:T(128)} %bitcast.place, bf16[192,3072]{1,0:T(8,128)(2,1)} %reduce-scatter.8.cloned.1.call-done.part, bf16[3072,768]{1,0:T(8,128)(2,1)} %base.3), custom_call_target="tpu_custom_call" | custom-call | tf_op jit(solution)/shard_map/pallas_call | solution.py:528
  495.8 2.5 copy.55
  (93 shorter events, 23.5 us)
Async XLA Ops:
  7.2 33.6 %all-gather.3.cloned.1.call-start = ((), (), s32[]{:S(2)}) async-start(), calls=%async_computation.3 | async-start | bytes 1474560 | tf_op jit(solution)/shard_map/all_gather | solution.py:563
  9.8 61.0 %all-gather.5.cloned.1.call-start = ((), (), s32[]{:S(2)}) async-start(), calls=%async_computation.4 | async-start | bytes 1474560 | tf_op jit(solution)/shard_map/all_gather | solution.py:569
  11.6 238.5 %reduce-scatter.10.cloned.1.call-start = ((), (), s32[]{:S(2)}) async-start(), calls=%async_computation.9 | async-start | bytes 2949120
  12.4 12.3 %collective-permute-start = (bf16[16,768]{1,0:T(8,128)(2,1)S(1)}, bf16[16,768]{1,0:T(8,128)(2,1)S(1)}, u32[]{:S(2)}, u32[]{:S(2)}) collective-permute-start(bf16[16,768]{1,0:T(8,128)(2,1)S(1)} %slice.51), channel_id=1, source_target_pairs={{0,4},{1,5},{2,6},{3,7},{8,12},{9,13},{10,14},{11,15},{16,20},{17,... | collective-permute-start | bytes 73736 | tf_op jit(solution)/shard_map/ppermute | solution.py:502
  17.0 25.1 %copy-start.3 = (f32[4,640]{1,0:T(4,128)}, f32[4,640]{1,0:T(4,128)S(1)}, u32[]{:S(2)}) copy-start(f32[4,640]{1,0:T(4,128)S(1)} %constant_dynamic-update-slice_fusion.cw) | copy-start | bytes 30724
  24.7 17.4 %copy-start.6 = (bf16[16,768]{1,0:T(8,128)(2,1)}, bf16[16,768]{1,0:T(8,128)(2,1)S(1)}, u32[]{:S(2)}) copy-start(bf16[16,768]{1,0:T(8,128)(2,1)S(1)} %collective-permute-done.halo) | copy-start | bytes 73732
  66.0 4.8 collective-permute-start.1
  70.8 0.6 copy-start.5
  129.5 7.4 %collective-permute-start.2 = (bf16[128,384]{1,0:T(8,128)(2,1)}, bf16[128,384]{1,0:T(8,128)(2,1)S(1)}, u32[]{:S(2)}, u32[]{:S(2)}) collective-permute-start(bf16[128,384]{1,0:T(8,128)(2,1)} %get-tuple-element.68), channel_id=1, source_target_pairs={{4,0},{5,1},{6,2},{7,3},{12,8},{13,9},{14,10},{15,11},{20,16},{21,... | collective-permute-start | bytes 294920 | tf_op jit(solution)/shard_map/ppermute | solution.py:502
  130.8 52.3 %slice-start = ((s8[4718592]{0:T(1024)(128)(4,1)}), s8[4194304]{0:T(1024)(128)(4,1)S(1)}, s32[]{:S(2)}) async-start(s8[4718592]{0:T(1024)(128)(4,1)} %bitcast.21), calls=%async_computation.10 | async-start | bytes 8388608
  136.9 0.6 copy-start.4
  137.5 45.5 %slice-start.1 = ((s8[4718592]{0:T(1024)(128)(4,1)}), s8[524288]{0:T(1024)(128)(4,1)S(1)}, s32[]{:S(2)}) async-start(s8[4718592]{0:T(1024)(128)(4,1)} %bitcast.21), calls=%async_computation.11 | async-start | bytes 1048576
  137.5 45.6 %copy-start = (bf16[3072,384]{1,0:T(8,128)(2,1)S(1)}, bf16[3072,384]{1,0:T(8,128)(2,1)}, u32[]{:S(2)}) copy-start(bf16[3072,384]{1,0:T(8,128)(2,1)} %get-tuple-element.78) | copy-start | bytes 7077892
  181.6 3.6 collective-permute-start.3
  183.1 21.2 %slice-start.2 = ((s8[4718592]{0:T(1024)(128)(4,1)}), s8[524288]{0:T(1024)(128)(4,1)S(1)}, s32[]{:S(2)}) async-start(s8[4718592]{0:T(1024)(128)(4,1)} %bitcast.23), calls=%async_computation.12 | async-start | bytes 1048576
  185.1 0.6 copy-start.7
  185.7 18.5 %slice-start.3 = ((s8[4718592]{0:T(1024)(128)(4,1)}), s8[4194304]{0:T(1024)(128)(4,1)S(1)}, s32[]{:S(2)}) async-start(s8[4718592]{0:T(1024)(128)(4,1)} %bitcast.23), calls=%async_computation.13 | async-start | bytes 8388608
  205.5 6.4 %copy-start.2 = (bf16[768,384]{0,1:T(8,128)(2,1)S(1)}, bf16[768,384]{0,1:T(8,128)(2,1)}, u32[]{:S(2)}) copy-start(bf16[768,384]{0,1:T(8,128)(2,1)} %convolution_convert_fusion) | copy-start | bytes 1769476
  214.5 57.3 %all-reduce.9.cloned.1.call-start = ((), (), s32[]{:S(2)}) async-start(), calls=%async_computation.7 | async-start | bytes 1572864 | tf_op jit(solution)/shard_map/psum | solution.py:736
  252.3 93.1 %all-reduce.11.cloned.1.call-start = ((), (), s32[]{:S(2)}) async-start(), calls=%async_computation.8 | async-start | bytes 524288 | tf_op jit(solution)/shard_map/psum | solution.py:740
  273.5 125.3 %reduce-scatter.6.cloned.1.call-start = ((), (), s32[]{:S(2)}) async-start(), calls=%async_computation.5 | async-start | bytes 5898240 | tf_op jit(solution)/shard_map/reduce_scatter | solution.py:661
  274.1 212.9 %reduce-scatter.8.cloned.1.call-start = ((), (), s32[]{:S(2)}) async-start(), calls=%async_computation.6 | async-start | bytes 5898240 | tf_op jit(solution)/shard_map/reduce_scatter | solution.py:727
  274.1 1.7 copy-start.10
  274.1 1.8 copy-start.8
  274.1 1.8 copy-start.9
  274.1 1.9 copy-start.11
  274.1 67.9 %copy-start.1 = (bf16[192,1536]{0,1:T(8,128)(2,1)S(1)}, bf16[192,1536]{0,1:T(8,128)(2,1)}, u32[]{:S(2)}) copy-start(bf16[192,1536]{0,1:T(8,128)(2,1)} %all-reduce.9.cloned.1.call-done) | copy-start | bytes 1769476
Sparse Core Ops, SparseCore 0:
  10.4 30.3 all-gather.2
  43.2 27.6 all-gather.4
  214.6 35.4 reduce-scatter.9
  252.8 18.9 all-reduce.8
  274.6 36.8 all-reduce.10
  313.6 85.0 reduce-scatter.5
  401.1 85.7 reduce-scatter.7

commit v2 on v1

--- a/solution.py
+++ b/solution.py
@@ -412,7 +412,7 @@
 
 
 def exit_kernel(
-    info, tok, gz, gcat, tail, nxt, last_j, cw, gain, wz_out, wj,
+    info, tok, gout, mine, gz, gcat, tail, nxt, last_j, cw, gain, wz_out, wj,
     gr_o, rim_o, rim_w_o, gain_o,
     fix,
 ):
@@ -449,7 +449,8 @@
         unit, inverse = norm_rows(tok[...])
         scaled = g_normed * gain[...]
         mean = jnp.mean(scaled * unit, axis=1, keepdims=True)
-        gr_o[...] = jnp.transpose(inverse * (scaled - unit * mean)).astype(bf16)
+        own = gout[...].astype(f32) * mine[...]
+        gr_o[...] = jnp.transpose(own + inverse * (scaled - unit * mean)).astype(bf16)
         gain_o[...] += jnp.sum(g_normed * unit, axis=0, keepdims=True)
 
     @pl.when(step_id == 0)
@@ -462,18 +463,297 @@
         finish(g_normed)
 
 
-def finish_kernel(parts, scaled, place, part, base, *rest):
-    out = rest[-1]
-    wide = part[...].astype(f32)
-    if scaled:
-        wide = wide * lax.rsqrt(rest[0][0:1, :] / INNER + epsilon)
-    add = jnp.transpose(wide)
-    size = out.shape[1]
+def finish_kernel(parts, place, part, base, sums, out):
+    wide = part[...].astype(f32) * lax.rsqrt(sums[0:1, :] / INNER + epsilon)
+    size = out.shape[0]
     for k in range(parts):
 
         @pl.when(place[0] == k)
         def _():
-            out[...] = (base[:, size * k : size * (k + 1)].astype(f32) + add).astype(bf16)
+            add = jnp.transpose(base[:, size * k : size * (k + 1)].astype(f32))
+            out[...] = (wide + add).astype(bf16)
+
+
+MESH = pl.DeviceIdType.MESH
+
+
+def start_together(peers):
+    barrier = pltpu.get_barrier_semaphore()
+    for peer in peers:
+        pl.semaphore_signal(barrier, inc=1, device_id=peer, device_id_type=MESH)
+    pl.semaphore_wait(barrier, len(peers))
+
+
+def remote(src, dst, sent, came, peer):
+    return pltpu.make_async_remote_copy(
+        src_ref=src, dst_ref=dst, send_sem=sent, recv_sem=came, device_id=peer, device_id_type=MESH
+    )
+
+
+def turned(index, distance, size):
+    return lax.rem(index + distance + size, size)
+
+
+def twin_of(index):
+    parity = lax.rem(index, 2)
+    return parity, index + 1 - 2 * parity
+
+
+def gather_kernel(n, x, bc, dt, out, sent, came, passed, relayed, own):
+    f = lax.axis_index("fsdp")
+    parity, twin = twin_of(lax.axis_index("ctx"))
+    rows = x.shape[0]
+    half = rows // 2
+    start_together([{"fsdp": turned(f, d, n)} for d in range(1, n)] + [{"ctx": twin}])
+    pieces = []
+    at = 0
+    for ref in (x, bc, dt):
+        pieces.append((ref, slice(at, at + ref.shape[1])))
+        at += ref.shape[1]
+
+    def place(source, side):
+        return pl.ds(pl.multiple_of(source * rows + side * half, 16), half)
+
+    mine = pl.ds(pl.multiple_of(parity * half, 16), half)
+    copies = []
+    for d in range(1, n):
+        for p, (ref, cols) in enumerate(pieces):
+            copy = remote(
+                ref.at[mine, :], out.at[place(f, parity), cols],
+                sent.at[d - 1, p], came.at[d - 1, p], {"fsdp": turned(f, d, n)},
+            )
+            copy.start()
+            copies.append(copy)
+    locals_ = []
+    for p, (ref, cols) in enumerate(pieces):
+        copy = pltpu.make_async_copy(
+            ref, out.at[pl.ds(pl.multiple_of(f * rows, 16), rows), cols], own.at[p]
+        )
+        copy.start()
+        locals_.append(copy)
+    relays = []
+    for d in range(1, n):
+        source = turned(f, -d, n)
+        for p, (ref, cols) in enumerate(pieces):
+            copies[(d - 1) * len(pieces) + p].wait_recv()
+            block = out.at[place(source, parity), cols]
+            copy = remote(block, block, passed.at[d - 1, p], relayed.at[d - 1, p], {"ctx": twin})
+            copy.start()
+            relays.append(copy)
+    for copy in copies:
+        copy.wait_send()
+    for copy in locals_:
+        copy.wait()
+    for copy in relays:
+        copy.wait()
+
+
+def gathered(x, bc, dt):
+    n = lax.axis_size("fsdp")
+    pieces = (n - 1, 3)
+    width = x.shape[1] + bc.shape[1] + dt.shape[1]
+    return pl.pallas_call(
+        functools.partial(gather_kernel, n),
+        out_shape=jax.ShapeDtypeStruct((n * x.shape[0], width), bf16),
+        in_specs=[pl.BlockSpec(memory_space=pltpu.VMEM)] * 3,
+        out_specs=pl.BlockSpec(memory_space=pltpu.VMEM),
+        scratch_shapes=[pltpu.SemaphoreType.DMA(pieces)] * 4 + [pltpu.SemaphoreType.DMA((3,))],
+        compiler_params=pltpu.CompilerParams(collective_id=1, has_side_effects=True),
+    )(x, bc, dt)
+
+
+def total_kernel(n, part, out, slots, sent, came):
+    me = lax.axis_index("tp")
+    start_together([{"tp": turned(me, d, n)} for d in range(1, n)])
+    copies = []
+    for d in range(1, n):
+        copy = remote(
+            part, slots.at[d - 1], sent.at[d - 1], came.at[d - 1], {"tp": turned(me, d, n)}
+        )
+        copy.start()
+        copies.append(copy)
+    total = part[...]
+    for d in range(1, n):
+        copies[d - 1].wait_recv()
+        total = total + slots[d - 1]
+    out[...] = total
+    for copy in copies:
+        copy.wait_send()
+
+
+def total_over_tp(part):
+    n = lax.axis_size("tp")
+    return pl.pallas_call(
+        functools.partial(total_kernel, n),
+        out_shape=jax.ShapeDtypeStruct(part.shape, f32),
+        in_specs=[pl.BlockSpec(memory_space=pltpu.VMEM)],
+        out_specs=pl.BlockSpec(memory_space=pltpu.VMEM),
+        scratch_shapes=[
+            pltpu.VMEM((n - 1,) + part.shape, f32),
+            pltpu.SemaphoreType.DMA((n - 1,)),
+            pltpu.SemaphoreType.DMA((n - 1,)),
+        ],
+        compiler_params=pltpu.CompilerParams(collective_id=2, has_side_effects=True),
+    )(part)
+
+
+def reduce_kernel(
+    n, m, bc_cols, conv_bc,
+    p_out, p_z, p_cat, m_scan, m_rim, m_gate, m_dt, m_gain,
+    o_out, o_z, o_cat, o_small, o_wide,
+    give, take, mid, slots, final, bc_slots, small, small_slots, wide_slots,
+    s1, r1, s2, r2, s3, r3, s4, r4,
+):
+    f = lax.axis_index("fsdp")
+    t = lax.axis_index("tp")
+    parity, twin = twin_of(lax.axis_index("ctx"))
+    start_together(
+        [{"ctx": twin}]
+        + [{"fsdp": turned(f, d, n)} for d in range(1, n)]
+        + [{"tp": turned(t, d, m)} for d in range(1, m)]
+    )
+    inner = p_out.shape[1]
+    rows = p_out.shape[0] // n
+    half = rows // 2
+
+    def piece(q, side):
+        at = pl.ds(pl.multiple_of(q * rows + side * half, 16), half)
+        return jnp.concatenate([p_out[at, :], p_z[at, :], p_cat[at, :]], axis=1)
+
+    copies = []
+    for q in range(n):
+        give[q] = piece(q, 1 - parity).astype(bf16)
+        copy = remote(give.at[q], take.at[q], s1.at[q], r1.at[q], {"ctx": twin})
+        copy.start()
+        copies.append(copy)
+    w_scan = m_scan.shape[1]
+    w_gate = m_gate.shape[1]
+    w_dt = m_dt.shape[1]
+    small[...] = jnp.zeros_like(small)
+    small[:, 0:w_scan] = m_scan[...] + m_rim[...]
+    at = w_scan
+    small[:, at : at + w_gate] = m_gate[...]
+    at += w_gate
+    small[:, at : at + w_dt] = m_dt[0:8, :]
+    small[:, at + w_dt : at + 2 * w_dt] = m_dt[8:16, :]
+    at += 2 * w_dt
+    small[0:1, at:] = m_gain[...]
+    small_slots[0, pl.ds(parity, 1)] = small[...][None]
+    copy = remote(
+        small, small_slots.at[0, parity], s1.at[n], r1.at[n], {"ctx": twin}
+    )
+    copy.start()
+    copies.append(copy)
+
+    copies[n].wait()
+    small_slots[1, pl.ds(f, 1)] = (small_slots[0, 0] + small_slots[0, 1])[None]
+    seconds = []
+    for d in range(1, n):
+        copy = remote(
+            small_slots.at[1, f], small_slots.at[1, f], s2.at[n - 1 + d - 1], r2.at[n - 1 + d - 1],
+            {"fsdp": turned(f, d, n)},
+        )
+        copy.start()
+        seconds.append(copy)
+    for q in range(n):
+        copies[q].wait()
+        mid[q] = (piece(q, parity) + take[q].astype(f32)).astype(bf16)
+    slots[pl.ds(f, 1)] = mid[pl.ds(f, 1)]
+    for d in range(1, n):
+        peer = turned(f, d, n)
+        copy = remote(
+            mid.at[peer], slots.at[f], s2.at[d - 1], r2.at[d - 1], {"fsdp": peer}
+        )
+        copy.start()
+        seconds.append(copy)
+    for copy in seconds:
+        copy.wait()
+    small_sum = small_slots[1, 0]
+    whole = slots[0].astype(f32)
+    for q in range(1, n):
+        small_sum = small_sum + small_slots[1, q]
+        whole = whole + slots[q].astype(f32)
+    final[...] = whole
+    bc_at = slice(3 * inner, 3 * inner + bc_cols)
+    bc_slots[pl.ds(t, 1)] = whole[:, bc_at][None]
+    wide = jnp.concatenate([small_sum[:, conv_bc:w_scan], small_sum[:, at:]], axis=1)
+    wide_slots[pl.ds(t, 1)] = wide[None]
+    o_small[...] = small_sum[:, :at]
+    thirds_ = []
+    for d in range(1, m):
+        peer = {"tp": turned(t, d, m)}
+        for p, buf in enumerate((bc_slots, wide_slots)):
+            copy = remote(buf.at[t], buf.at[t], s3.at[2 * (d - 1) + p], r3.at[2 * (d - 1) + p], peer)
+            copy.start()
+            thirds_.append(copy)
+    for copy in thirds_:
+        copy.wait()
+    bc_sum = bc_slots[0]
+    wide_sum = wide_slots[0]
+    for q in range(1, m):
+        bc_sum = bc_sum + bc_slots[q]
+        wide_sum = wide_sum + wide_slots[q]
+    o_wide[...] = wide_sum
+    final[:, bc_at] = bc_sum
+    here = pl.ds(pl.multiple_of(parity * half, 8), half)
+    o_out[here, :] = final[:, :inner]
+    o_z[here, :] = final[:, inner : 2 * inner]
+    o_cat[here, :] = final[:, 2 * inner :]
+    lasts = []
+    for p, (out, cols) in enumerate(
+        ((o_out, slice(0, inner)), (o_z, slice(inner, 2 * inner)), (o_cat, slice(2 * inner, None)))
+    ):
+        copy = remote(
+            final.at[:, cols] if cols.stop else final.at[:, 2 * inner : final.shape[1]],
+            out.at[here, :], s4.at[p], r4.at[p], {"ctx": twin},
+        )
+        copy.start()
+        lasts.append(copy)
+    for copy in lasts:
+        copy.wait()
+
+
+def reduced(parts, miscs, bc_cols):
+    n, m = lax.axis_size("fsdp"), lax.axis_size("tp")
+    p_out, _p_z, p_cat = parts
+    rows = p_out.shape[0] // n
+    half = rows // 2
+    inner = p_out.shape[1]
+    wide = 2 * inner + p_cat.shape[1]
+    m_scan, _m_rim, m_gate, m_dt, m_gain = miscs
+    kept = m_scan.shape[1] + m_gate.shape[1] + 2 * m_dt.shape[1]
+    small = kept + m_gain.shape[1]
+    crossing = m_scan.shape[1] - inner + m_gain.shape[1]
+    dma = pltpu.SemaphoreType.DMA
+
+    def shape(*dims):
+        return jax.ShapeDtypeStruct(dims, f32)
+
+    return pl.pallas_call(
+        functools.partial(reduce_kernel, n, m, bc_cols, inner),
+        out_shape=[
+            shape(rows, inner), shape(rows, inner), shape(rows, p_cat.shape[1]),
+            shape(8, kept), shape(8, crossing),
+        ],
+        in_specs=[pl.BlockSpec(memory_space=pltpu.VMEM)] * 8,
+        out_specs=[pl.BlockSpec(memory_space=pltpu.VMEM)] * 5,
+        scratch_shapes=[
+            pltpu.VMEM((n, half, wide), bf16),
+            pltpu.VMEM((n, half, wide), bf16),
+            pltpu.VMEM((n, half, wide), bf16),
+            pltpu.VMEM((n, half, wide), bf16),
+            pltpu.VMEM((half, wide), f32),
+            pltpu.VMEM((m, half, bc_cols), f32),
+            pltpu.VMEM((8, small), f32),
+            pltpu.VMEM((2, max(n, 2), 8, small), f32),
+            pltpu.VMEM((m, 8, crossing), f32),
+            dma((n + 1,)), dma((n + 1,)), dma((2 * n - 2,)), dma((2 * n - 2,)),
+            dma((2 * m - 2,)), dma((2 * m - 2,)), dma((3,)), dma((3,)),
+        ],
+        compiler_params=pltpu.CompilerParams(
+            collective_id=3, has_side_effects=True, vmem_limit_bytes=48 * 1024 * 1024
+        ),
+    )(*parts, *miscs)
 
 
 def constants(inner, heads):
@@ -560,12 +840,7 @@
     ctx_index = lax.axis_index("ctx")
     e8, spread, gather, upper, lower = constants(inner, heads)
 
-    w_joined = lax.all_gather(
-        jnp.concatenate([w_x, w_bc, jnp.pad(w_dt, ((0, 0), (0, 128 - heads)))], axis=1),
-        "fsdp",
-        axis=0,
-        tiled=True,
-    )
+    w_joined = gathered(w_x, w_bc, jnp.pad(w_dt, ((0, 0), (0, 128 - heads))))
     wz_out = lax.all_gather(jnp.concatenate([w_z, w_out.T], axis=1), "fsdp", axis=0, tiled=True)
 
     starts = jnp.cumsum(lengths[0]) - lengths[0]
@@ -657,7 +932,7 @@
         ],
         [pltpu.VMEM((states, inner), f32), pltpu.VMEM((STRETCH, STRETCH), f32)],
     )
-    sums = lax.psum(sums, "tp")
+    sums = total_over_tp(sums)
     branch = lax.psum_scatter(branch, "tp", scatter_dimension=0, tiled=True)
     g_z, g_b, g_c, normed_two, a_sum, gs_part, start_state, misc_gate = call(
         gate_kernel,
@@ -707,13 +982,15 @@
         ],
     )
     next_rows = passed_along(head, "ctx", -1)
+    feature = jnp.arange(model, dtype=jnp.int32) // slice_width
+    mine = (feature == tp_index).astype(f32)[None, :]
     last_joined = jnp.concatenate([joined_x[rows - 16 :], joined_bc[rows - 16 :]], axis=1)
     g_resid, rim, rim_w, gain_part = call(
         exit_kernel,
         blocks,
         [
-            info_in, by_rows(tokens, True), by_rows(g_z, True), by_rows(g_cat, True),
-            whole(tail), whole(next_rows), whole(last_joined), whole(conv_w), whole(gain),
+            info_in, by_rows(tokens, True), by_rows(grad_out, True), whole(mine),
+            by_rows(g_z, True), by_rows(g_cat, True), whole(tail), whole(next_rows), whole(last_joined), whole(conv_w), whole(gain),
             whole(wz_out), whole(w_joined),
         ],
         [
@@ -731,46 +1008,46 @@
     part_cat = tn(normed, g_cat)
     part_rim = tn(normed[rows - 16 :], rim)
     part_cat = part_cat + jnp.pad(part_rim, ((0, 0), (0, 128)))
-    parts = jnp.concatenate([part_out, part_z, part_cat], axis=1).astype(bf16)
-    shard = lax.psum_scatter(parts, "fsdp", scatter_dimension=0, tiled=True)
-    shard = lax.psum(shard, "ctx").astype(f32)
-    grad_w_out = shard[:, :inner].T
-    grad_w_z = shard[:, inner : 2 * inner]
-    grad_w_x = shard[:, 2 * inner : 3 * inner]
-    grad_w_bc = lax.psum(shard[:, 3 * inner : 3 * inner + 2 * states], "tp")
-    grad_w_dt = shard[:, 3 * inner + 2 * states : 3 * inner + 2 * states + heads]
-
-    misc_scan = misc_scan + rim_w
-    over_all = (gain_part[0], misc_scan[:taps, inner:], misc_scan[taps, inner:])
-    sum_gain, grad_conv_bc_w, grad_conv_bc_b = lax.psum(over_all, ("fsdp", "ctx", "tp"))
-    small = (
-        misc_scan[:taps, :inner],
-        misc_scan[taps, :inner],
-        jnp.sum(misc_dt[HEAD_ROWS : HEAD_ROWS + heads], axis=1),
-        jnp.sum(misc_dt[:heads], axis=1),
-        jnp.sum(misc_gate[1].reshape(heads, per_head), axis=1),
-        misc_gate[0],
-    )
-    (
-        grad_conv_x_w, grad_conv_x_b, grad_dt_bias, grad_a_log, grad_d_skip, grad_gate_gain,
-    ) = lax.psum(small, ("fsdp", "ctx"))
+    s_out, s_z, s_cat, s_small, s_wide = reduced(
+        (part_out, part_z, part_cat),
+        (misc_scan, rim_w, misc_gate, misc_dt, gain_part),
+        2 * states,
+    )
+    if lax.axis_size("ctx") > 2:
+        s_out, s_z, s_cat, s_small, s_wide = jax.tree.map(
+            lambda part: lax.psum(0.5 * part, "ctx"), (s_out, s_z, s_cat, s_small, s_wide)
+        )
+    grad_w_out = s_out.T
+    grad_w_z = s_z
+    grad_w_x = s_cat[:, :inner]
+    grad_w_bc = s_cat[:, inner : inner + 2 * states]
+    grad_w_dt = s_cat[:, inner + 2 * states : inner + 2 * states + heads]
+    grad_conv_x_w = s_small[:taps, :inner]
+    grad_conv_x_b = s_small[taps, :inner]
+    grad_gate_gain = s_small[0, width : width + inner]
+    grad_d_skip = jnp.sum(s_small[1, width : width + inner].reshape(heads, per_head), axis=1)
+    dt_at = width + inner
+    grad_a_log = jnp.sum(s_small[:heads, dt_at : dt_at + STRETCH], axis=1)
+    grad_dt_bias = jnp.sum(s_small[:heads, dt_at + STRETCH : dt_at + 2 * STRETCH], axis=1)
+    grad_conv_bc_w = s_wide[:taps, : 2 * states]
+    grad_conv_bc_b = s_wide[taps, : 2 * states]
     here = tp_index * slice_width
-    grad_norm_gain = lax.dynamic_slice_in_dim(sum_gain, here, slice_width, 0)
-
+    grad_norm_gain = lax.dynamic_slice_in_dim(s_wide[0, 2 * states :], here, slice_width, 0)
     place = tp_index.astype(jnp.int32)[None]
 
-    def finish(part, base, scaled):
-        extra = [by_lanes(sums)] if scaled else []
-        return call(
-            functools.partial(finish_kernel, tp_size, scaled),
-            blocks,
-            [(place, None, "smem"), by_lanes(part), by_rows(base)] + extra,
-            [by_rows(shape((rows, slice_width), bf16))],
-            [],
-        )[0]
-
-    layer_out = finish(branch, tokens, True)
-    grad_tokens = finish(g_resid, grad_out, False)
+    layer_out = call(
+        functools.partial(finish_kernel, tp_size),
+        blocks // 2,
+        [
+            (place, None, "smem"),
+            (branch, (slice_width, 2 * STRETCH), lambda i: (0, i)),
+            (tokens, (2 * STRETCH, model), lambda i: (i, 0)),
+            (sums, (2, 2 * STRETCH), lambda i: (0, i)),
+        ],
+        [(shape((slice_width, rows), bf16), (slice_width, 2 * STRETCH), lambda i: (0, i))],
+        [],
+    )[0].T
+    grad_tokens = g_resid.T
     return (
         layer_out, grad_tokens, grad_norm_gain, grad_w_z, grad_w_x, grad_w_bc, grad_w_dt,
         grad_conv_x_w, grad_conv_x_b, grad_conv_bc_w, grad_conv_bc_b, grad_dt_bias, grad_a_log,

time: 507 us -> 287 us (0.57)
  waiting for transfers between devices: 202 us -> 21.9 us
  blocking collectives: 85.6 us -> 0 us
  Pallas kernels: 142 us -> 198 us
  local copies, waits for them, and re-layouts: 31.4 us -> 21 us
    psum x3 -> x0, blocking collectives: 85.6 us -> none  [the longest x1 40.9 us: local(): lax.psum(over_all, ('fsdp', 'ctx', 'tp'))]
    pallas_call x0 -> x3, Pallas kernels: none -> 67.5 us  [the longest x1 45.3 us: reduced(): pl.pallas_call(functools.partial(reduce_kernel, n, m, bc_cols, inner), ou...]
    reduce_scatter x1, waiting for transfers between devices: 76.5 us -> 20.5 us  [local(): g_resid = lax.psum_scatter(g_resid, 'tp', scatter_dimension=0, tiled=True)]
    reduce_scatter x1, waiting for transfers between devices: 51.6 us -> 0.01 us  [local(): branch = lax.psum_scatter(branch, 'tp', scatter_dimension=0, tiled=True)]
    unnamed x8 -> x3, waiting for transfers between devices: 36.8 us -> 0.05 us
    psum x2 -> x0, waiting for transfers between devices: 19.5 us -> none  [the longest x1 19.5 us: local(): shard = lax.psum(shard, 'ctx').astype(f32)]
    all_gather x1 -> x0, waiting for transfers between devices: 16 us -> none  [local(): lax.all_gather(jnp.concatenate([w_x, w_bc, jnp.pad(w_dt, ((0, 0), (0, 128...]
    pallas_call x7 -> x6, Pallas kernels: 142 us -> 131 us  [call(): pl.pallas_call(kernel, grid=(blocks,), in_specs=[spec(shape, how) for _a,...]
  transfers between devices with their start and end apart: 11 -> 7, of which waited for: 6 -> 3; matrix products, arithmetic and copies ran while one was open for 7% -> 12% of each run, Pallas kernels for 7% -> 62%
where the time goes in v2:
time: 287 us; the launch traced here: 284 us
  Pallas kernels  198 us (69%)
  waiting for transfers between devices  21.9 us (8%)
  local copies, waits for them, and re-layouts  21 us (7%)
  matrix products  14.1 us (5%)
  between operations  14.1 us (5%)
  starting transfers between devices  7.55 us (3%)
  other arithmetic  6.99 us (2%)
    pallas_call x6, Pallas kernels, call(): pl.pallas_call(kernel, grid=(blocks,), in_specs=[spec(shape, how) for _a,...  131 us
    pallas_call x1, Pallas kernels, reduced(): pl.pallas_call(functools.partial(reduce_kernel, n, m, bc_cols, inner), ou...  45.3 us
    reduce_scatter x1, waiting for transfers between devices, local(): g_resid = lax.psum_scatter(g_resid, 'tp', scatter_dimension=0, tiled=True)  20.5 us
    pallas_call x1, Pallas kernels, gathered(): pl.pallas_call(functools.partial(gather_kernel, n), out_shape=jax.ShapeDt...  14.3 us
    dot_general x4, matrix products, tn(): lax.dot_general(left, right, (((0,), (0,)), ((), ())), preferred_element_...  14.1 us
    pallas_call x1, Pallas kernels, total_over_tp(): pl.pallas_call(functools.partial(total_kernel, n), out_shape=jax.ShapeDty...  7.92 us
    ppermute x4, starting transfers between devices, passed_along(): return lax.ppermute(block, axis, route)  7.43 us
    unnamed x39, local copies, waits for them, and re-layouts  7.2 us
  transfers between devices with their start and end apart: 7, of which 3 were waited for; matrix products, arithmetic and copies ran while one was open for 12% of the time, Pallas kernels for 62%

profile of v2, /device:TPU:0, one launch (start us, length us, event | category | flops | bytes accessed | tf_op | source)
XLA Modules:
  0.0 283.9 jit_solution(2885058005509598182)
XLA Ops:
  7.2 1.7 pad_maximum_fusion
  9.0 0.7 slice.48
  9.8 2.4 collective-permute-start
  12.2 0.8 reduce-window.9
  13.0 0.7 constant_dynamic-update-slice_fusion.1
  13.7 0.7 constant_dynamic-update-slice_fusion.cw
  14.4 0.7 pad_maximum_fusion.2
  16.3 1.3 broadcast_in_dim.33.gain
  17.6 0.8 copy.46
  21.0 14.3 %shard_map.405.wj = bf16[768,768]{1,0:T(8,128)(2,1)} custom-call(bf16[192,384]{1,0:T(8,128)(2,1)} %x.9, bf16[192,256]{1,0:T(8,128)(2,1)} %bc.1, bf16[192,128]{1,0:T(8,128)(2,1)} %pad.15.dt), custom_call_target="tpu_custom_call" | custom-call | tf_op jit(solution)/shard_map/pallas_call | solution.py:555
  36.7 23.9 %shard_map.406 = (bf16[3072,768]{1,0:T(8,128)(2,1)}, bf16[3072,384]{1,0:T(8,128)(2,1)}, bf16[3072,256]{1,0:T(8,128)(2,1)}, bf16[3072,640]{1,0:T(8,128)(2,1)}, bf...) custom-call(s32[5]{0:T(128)} %pad_add_fusion.1.info, ...), custom_call_target="tpu_custom_call" | custom-call | tf_op jit(solution)/shard_map/pallas_call | solution.py:808
  60.6 2.3 collective-permute-start.1
  64.8 21.0 %shard_map.407 = (f32[3072,384]{1,0:T(8,128)}, f32[3072,384]{1,0:T(8,128)}, f32[3072,384]{1,0:T(8,128)}, bf16[768,3072]{1,0:T(8,128)(2,1)}, f32[2,3072]{1,0:T(2,128)}, /*index=5*/bf16[12,128,384]{2,1,0:T(8,128)(2,1)}) custom-call(s32[5]{0:T(128)} %pad_add_fusion.1.info, bf16[3072,640]{1,0:T(8,128)(2,1)} %get-tuple-element.55.vbc.vc, ...), custom_call_target="tpu_custom_call" | custom-call | tf_op jit(solution)/shard_map/pallas_call | solution.py:808
  85.9 7.9 %shard_map.408.sums = f32[2,3072]{1,0:T(2,128)} custom-call(f32[2,3072]{1,0:T(2,128)} %get-tuple-element.62.part), custom_call_target="tpu_custom_call" | custom-call | tf_op jit(solution)/shard_map/pallas_call | solution.py:586
  93.8 16.8 %shard_map.410 = (bf16[3072,384]{1,0:T(8,128)(2,1)}, bf16[3072,384]{1,0:T(8,128)(2,1)}, bf16[3072,384]{1,0:T(8,128)(2,1)}, bf16[3072,384]{1,0:T(8,128)(2,1)}, f3...) custom-call(s32[5]{0:T(128)} %pad_add_fusion.1.info, ...), custom_call_target="tpu_custom_call" | custom-call | tf_op jit(solution)/shard_map/pallas_call | solution.py:808
  110.6 1.3 collective-permute-start.2
  112.5 0.7 slice.50
  113.2 0.7 slice.49
  114.7 44.0 %shard_map.411 = (bf16[3072,768]{1,0:T(8,128)(2,1)}, f32[8,640]{1,0:T(8,128)}, f32[8,640]{1,0:T(8,128)}, f32[8,640]{1,0:T(8,128)}, f32[16,256]{1,0:T(8,128)}) custom-call(s32[5]{0:T(128)} %pad_add_fusion.1.info, bf16[3072,640]{1,0:T(8,128)(2,1)} %get-tuple-element.55.vbc.vc, bf16[3072,384]{1,0:T(8,128)(2,1)} %get-tuple-element.68.gb, ...), custom_call_target="tpu_custom_call" | custom-call | tf_op jit(solution)/shard_map/pallas_call | solution.py:808
  158.6 1.5 collective-permute-start.3
  160.7 1.2 collective-permute-done.3.nxt
  162.5 19.5 %shard_map.412 = (bf16[768,3072]{1,0:T(8,128)(2,1)}, bf16[16,640]{1,0:T(8,128)(2,1)}, f32[8,640]{1,0:T(8,128)}, f32[1,768]{1,0:T(1,128)}) custom-call(s32[5]{0:T(128)} %pad_add_fusion.1.info, bf16[3072,768]{1,0:T(8,128)(2,1)} %tok.3, bf16[3072,768]{1,0:T(8,128)(2,1)} %gout.3, f32[1,768]{1,0:T(1,128)} %compare_convert_fusion.mine, ...), custom_call_target="tpu_custom_call" | custom-call | tf_op jit(solution)/shard_map/pallas_call | solution.py:808
  182.0 1.6 copy-done.14
  183.7 4.7 %convolution_bitcast_fusion.p_out = f32[768,384]{1,0:T(8,128)S(1)} fusion(bf16[3072,384]{1,0:T(8,128)(2,1)S(1)} %copy-done.14, bf16[3072,768]{1,0:T(8,128)(2,1)} %gout.3), kind=kOutput, calls=%fused_computation.1 | convolution fusion | flops 1811939328 | bytes 8257536 | tf_op jit(solution)/shard_map/dot_general | solution.py:30
  188.4 2.6 fusion.2.p_z
  191.6 6.3 %pad_add_fusion.p_cat = f32[768,768]{1,0:T(8,128)S(1)} fusion(f32[768,640]{1,0:T(8,128)S(1)} %fusion, bf16[3072,768]{1,0:T(8,128)(2,1)S(1)} %bitcast.24, bf16[3072,768]{1,0:T(8,128)(2,1)} %get-tuple-element.78.gcat), kind=kOutput, calls=%fused_computation | convolution fusion | flops 3624468480 | bytes 13762560 | tf_op jit(solution)/shard_map/dot_general | solution.py:30
  198.0 45.3 %shard_map.413 = (f32[192,384]{1,0:T(8,128)S(1)}, f32[192,384]{1,0:T(8,128)S(1)}, f32[192,768]{1,0:T(8,128)S(1)}, f32[8,1536]{1,0:T(8,128)S(1)}, f32[8,1024]{1,0:T(8,128)S(1)}) custom-call(f32[768,384]{1,0:T(8,128)S(1)} %convolution_bitcast_fusion.p_out, f32[768,384]{1,0:T(8,128)S(1)} %fusion.2.p_z, f32[768,768]{1,0:T(8,128)S(1)} %pad_add_fusion.p_cat, ...), custom_call_target="tpu_custom_call" | custom-call | tf_op jit(solution)/shard_map/pallas_call | solution.py:732
  243.3 0.7 slice.53
  249.7 5.7 %shard_map.409 = bf16[192,3072]{1,0:T(8,128)(2,1)} custom-call(s32[1]{0:T(128)} %bitcast.place, bf16[192,3072]{1,0:T(8,128)(2,1)} %reduce-scatter.3.cloned.1.call-done.part, bf16[3072,768]{1,0:T(8,128)(2,1)} %tok.3, f32[2,3072]{1,0:T(2,128)} %shard_map.408.sums), custom_call_target="tpu_custom_call" | custom-call | tf_op jit(solution)/shard_map/pallas_call | solution.py:808
  255.4 20.5 %reduce-scatter.5.cloned.1.call-done = bf16[192,3072]{1,0:T(8,128)(2,1)} async-done(((bf16[768,3072]{1,0:T(8,128)(2,1)}), bf16[192,3072]{1,0:T(8,128)(2,1)}) %reduce-scatter.5.cloned.1.call-update) | async-done | bytes 1179664 | tf_op jit(solution)/shard_map/reduce_scatter | solution.py:1004
  275.9 0.7 copy.53
  276.6 0.7 copy.54
  (72 shorter events, 16.0 us)
Async XLA Ops:
  7.2 57.0 %all-gather.2.cloned.1.call-start = ((), (), s32[]{:S(2)}) async-start(), calls=%async_computation.2 | async-start | bytes 1474560 | tf_op jit(solution)/shard_map/all_gather | solution.py:844
  9.0 240.8 %reduce-scatter.3.cloned.1.call-start = ((), (), s32[]{:S(2)}) async-start(), calls=%async_computation.3 | async-start | bytes 5898240 | tf_op jit(solution)/shard_map/reduce_scatter | solution.py:936
  9.8 25.5 %collective-permute-start = (bf16[16,768]{1,0:T(8,128)(2,1)S(1)}, bf16[16,768]{1,0:T(8,128)(2,1)S(1)}, u32[]{:S(2)}, u32[]{:S(2)}) collective-permute-start(bf16[16,768]{1,0:T(8,128)(2,1)S(1)} %slice.48), channel_id=1, source_target_pairs={{0,4},{1,5},{2,6},{3,7},{8,12},{9,13},{10,14},{11,15},{16,20},{17,... | collective-permute-start | bytes 73736 | tf_op jit(solution)/shard_map/ppermute | solution.py:782
  14.4 22.3 %copy-start.6 = (f32[4,640]{1,0:T(4,128)}, f32[4,640]{1,0:T(4,128)S(1)}, u32[]{:S(2)}) copy-start(f32[4,640]{1,0:T(4,128)S(1)} %constant_dynamic-update-slice_fusion.cw) | copy-start | bytes 30724
  35.3 1.4 copy-start.9
  36.7 26.3 %copy-start.13 = (f32[6]{0:T(128)S(1)}, f32[6]{0:T(128)}, u32[]{:S(2)}) copy-start(f32[6]{0:T(128)} %param.44) | copy-start | bytes 76
  36.7 27.0 %copy-start.12 = (f32[384]{0:T(512)S(1)}, f32[384]{0:T(512)}, u32[]{:S(2)}) copy-start(f32[384]{0:T(512)} %param.45) | copy-start | bytes 4612
  60.6 3.6 %collective-permute-start.1 = (bf16[128,384]{1,0:T(8,128)(2,1)}, bf16[128,384]{1,0:T(8,128)(2,1)S(1)}, u32[]{:S(2)}, u32[]{:S(2)}) collective-permute-start(bf16[128,384]{1,0:T(8,128)(2,1)} %get-tuple-element.59), channel_id=1, source_target_pairs={{0,4},{1,5},{2,6},{3,7},{8,12},{9,13},{10,14},{11,15},{16,20},{17,... | collective-permute-start | bytes 294920 | tf_op jit(solution)/shard_map/ppermute | solution.py:782
  64.2 0.6 copy-start.8
  85.8 190.1 %reduce-scatter.5.cloned.1.call-start = ((), (), s32[]{:S(2)}) async-start(), calls=%async_computation.4 | async-start | bytes 5898240 | tf_op jit(solution)/shard_map/reduce_scatter | solution.py:1004
  110.6 3.4 %collective-permute-start.2 = (bf16[128,384]{1,0:T(8,128)(2,1)}, bf16[128,384]{1,0:T(8,128)(2,1)S(1)}, u32[]{:S(2)}, u32[]{:S(2)}) collective-permute-start(bf16[128,384]{1,0:T(8,128)(2,1)} %get-tuple-element.73), channel_id=1, source_target_pairs={{4,0},{5,1},{6,2},{7,3},{12,8},{13,9},{14,10},{15,11},{20,16},{21,... | collective-permute-start | bytes 294920 | tf_op jit(solution)/shard_map/ppermute | solution.py:782
  114.0 0.6 copy-start.7
  158.6 3.3 %collective-permute-start.3 = (f32[8,640]{1,0:T(8,128)}, f32[8,640]{1,0:T(8,128)S(1)}, u32[]{:S(2)}, u32[]{:S(2)}) collective-permute-start(f32[8,640]{1,0:T(8,128)} %get-tuple-element.80), channel_id=1, source_target_pairs={{4,0},{5,1},{6,2},{7,3},{12,8},{13,9},{14,10},{15,11},{20,16},{21,... | collective-permute-start | bytes 61448 | tf_op jit(solution)/shard_map/ppermute | solution.py:782
  161.9 0.6 copy-start.11
  182.0 1.7 copy-start.14
  182.0 6.4 %slice-start = ((s8[4718592]{0:T(1024)(128)(4,1)}), s8[524288]{0:T(1024)(128)(4,1)S(1)}, s32[]{:S(2)}) async-start(s8[4718592]{0:T(1024)(128)(4,1)} %bitcast.23), calls=%async_computation.5 | async-start | bytes 1048576
  183.7 4.7 %slice-start.1 = ((s8[4718592]{0:T(1024)(128)(4,1)}), s8[4194304]{0:T(1024)(128)(4,1)S(1)}, s32[]{:S(2)}) async-start(s8[4718592]{0:T(1024)(128)(4,1)} %bitcast.23), calls=%async_computation.6 | async-start | bytes 8388608
  183.7 4.7 %copy-start.5 = (bf16[3072,384]{1,0:T(8,128)(2,1)S(1)}, bf16[3072,384]{1,0:T(8,128)(2,1)}, u32[]{:S(2)}) copy-start(bf16[3072,384]{1,0:T(8,128)(2,1)} %get-tuple-element.67.gz) | copy-start | bytes 7077892
  188.4 2.6 copy-start.10
  191.5 6.4 %copy-start = (f32[8,640]{1,0:T(8,128)S(1)}, f32[8,640]{1,0:T(8,128)}, u32[]{:S(2)}) copy-start(f32[8,640]{1,0:T(8,128)} %get-tuple-element.84.m_scan) | copy-start | bytes 61444
  191.5 6.4 %copy-start.1 = (f32[8,640]{1,0:T(8,128)S(1)}, f32[8,640]{1,0:T(8,128)}, u32[]{:S(2)}) copy-start(f32[8,640]{1,0:T(8,128)} %get-tuple-element.85.m_rim) | copy-start | bytes 61444
  191.5 6.4 %copy-start.2 = (f32[16,256]{1,0:T(8,128)S(1)}, f32[16,256]{1,0:T(8,128)}, u32[]{:S(2)}) copy-start(f32[16,256]{1,0:T(8,128)} %get-tuple-element.87.m_dt) | copy-start | bytes 49156
  191.6 6.4 %copy-start.3 = (f32[8,384]{1,0:T(8,128)S(1)}, f32[8,384]{1,0:T(8,128)}, u32[]{:S(2)}) copy-start(f32[8,384]{1,0:T(8,128)} %get-tuple-element.86.m_gate) | copy-start | bytes 36868
  191.6 6.4 %copy-start.4 = (f32[1,768]{1,0:T(1,128)S(1)}, f32[1,768]{1,0:T(1,128)}, u32[]{:S(2)}) copy-start(f32[1,768]{1,0:T(1,128)} %get-tuple-element.88.m_gain) | copy-start | bytes 9220
Sparse Core Ops, SparseCore 0:
  10.4 30.8 all-gather.1
  86.0 85.4 reduce-scatter.2
  182.2 93.7 reduce-scatter.4

commit v3 on v2

--- a/solution.py
+++ b/solution.py
@@ -9,6 +9,7 @@
 from jax.sharding import PartitionSpec as P
 
 STRETCH = 256
+TAPS = 4
 INNER = 1536
 HEAD_ROWS = 8
 LOG2E = 1.4426950408889634
@@ -75,9 +76,11 @@
     return lax.broadcasted_iota(jnp.int32, shape, axis)
 
 
-def read_info(info, block):
-    first = info[0]
-    starts = [info[1 + k] for k in range(info.shape[0] - 1)]
+def read_info(rows, lengths, block):
+    first = lax.axis_index("ctx") * rows
+    starts = [jnp.int32(0)]
+    for k in range(lengths.shape[1] - 1):
+        starts.append(starts[-1] + lengths[0, k])
     base = first + block * STRETCH
     end_start = segment_start(base + STRETCH - 1, starts)
     flag = jnp.where(end_start < base, 1.0, 0.0).astype(f32)
@@ -95,26 +98,26 @@
 
 
 def entry_kernel(
-    info, tok, halo, gain, wj, cw, cb, bias, rate, tri, ew, e8,
+    rows, info, tok, halo, par, wj, tri, ew, e8,
     nrm_o, jx_o, jb_o, vbc_o, sx_o, sb_o, pre_o, step_o, cum_o, s_o, end_o, dec_o,
     ext, run, dec,
 ):
     i = pl.program_id(0)
-    starts, base, end_start, flag = read_info(info, i)
-    width = cw.shape[1]
+    starts, base, end_start, flag = read_info(rows, info, i)
     inner = jx_o.shape[1]
-    taps = cw.shape[0]
+    width = inner + jb_o.shape[1]
+    gain, cb, cw, taps = par[0:1, :], par[1:2, :], par[4:8, :], TAPS
 
     @pl.when(i == 0)
     def _():
         unit, _inv = norm_rows(halo[...])
-        before = nn((unit * gain[...]).astype(bf16), wj[:, :width])
+        before = nn((unit * gain).astype(bf16), wj[:, :width])
         ext[0:8, :] = before.astype(bf16).astype(f32)[8:16]
         run[...] = jnp.zeros_like(run)
         dec[...] = jnp.ones_like(dec)
 
     unit, _inv = norm_rows(tok[...])
-    normed = (unit * gain[...]).astype(bf16)
+    normed = (unit * gain).astype(bf16)
     nrm_o[...] = normed
     product = nn(normed, wj[...])
     joined = product[:, :width].astype(bf16)
@@ -141,9 +144,9 @@
         else:
             sb_o[:, 128 * g - inner : 128 * (g + 1) - inner] = slope
     ext[0:8, :] = ext[STRETCH : STRETCH + 8, :]
-    pre = jnp.transpose(product[:, width:])[:HEAD_ROWS] + bias[...]
+    pre = jnp.transpose(product[:, width:])[:HEAD_ROWS] + par[8:16, 0:1]
     step = jax.nn.softplus(pre)
-    logd = -step * rate[...]
+    logd = -step * jnp.exp(par[8:16, 1:2])
     cum = exact_rows(logd, tri[...])
     pre_o[...] = pre
     step_o[...] = step
@@ -166,13 +169,15 @@
 
 
 def mix_kernel(
-    info, vbc, step, cum, s_in, inc, normed, gout, wz_out, dskip, gain, e_step, e_scale, e8,
-    z_o, out_o, gn_o, br_o, sum_o, st_o,
+    rows, info, vbc, step, cum, s_in, inc, normed, gout, wz_out, par, e_step, e_scale, e8,
+    z_o, out_o, gn_o, sum_o, st_o, br_o,
     run, gram,
 ):
     i = pl.program_id(0)
-    starts, base, _end_start, flag = read_info(info, i)
-    inner = gain.shape[1]
+    starts, base, _end_start, flag = read_info(rows, info, i)
+    inner = out_o.shape[1]
+    gain = par[2:3, :inner]
+    dskip = lanes_of(par[8:16, 2:3], e8[...])
 
     @pl.when(i == 0)
     def _():
@@ -220,7 +225,7 @@
     gated = out * (zf * jax.nn.sigmoid(zf))
     gn = nn(gout[...], wz_out[:, inner:])
     gn_o[...] = gn
-    gg = gated * gain[...]
+    gg = gated * gain
     br_o[...] = nt(wz_out[:, inner:], gg.astype(bf16)).astype(bf16)
     ss = jnp.sum(gated * gated, axis=1, keepdims=True)
     dq = jnp.sum(gn * gg, axis=1, keepdims=True)
@@ -228,15 +233,17 @@
 
 
 def gate_kernel(
-    info, sums, cum, out, z, gn, vc, st, dskip, gain, e_scale, e8, f_sum,
+    rows, info, sums, cum, out, z, gn, vc, st, par, e_scale, e8, f_sum,
     gz_o, gb_o, gc_o, n2_o, a_o, gs_o, start_o, misc_o,
     run,
 ):
     step_id = pl.program_id(0)
     blocks = pl.num_programs(0)
     i = blocks - 1 - step_id
-    starts, base, _end_start, flag = read_info(info, i)
+    starts, base, _end_start, flag = read_info(rows, info, i)
     inner = z.shape[1]
+    gain = par[2:3, :inner]
+    dskip = lanes_of(par[8:16, 2:3], e8[...])
 
     @pl.when(step_id == 0)
     def _():
@@ -261,17 +268,17 @@
     gated = o * act
     g_n = gn[...]
     unit = gated * alpha_c
-    g_gated = alpha_c * (g_n * gain[...]) - beta_c * gated
+    g_gated = alpha_c * (g_n * gain) - beta_c * gated
     g_out = g_gated * act
     gz_o[...] = (g_gated * o * (sig + act * (1.0 - sig))).astype(bf16)
     gb = g_out.astype(bf16)
     gb_o[...] = gb
-    n2_o[...] = (unit * gain[...]).astype(bf16)
+    n2_o[...] = (unit * gain).astype(bf16)
     misc_o[0:1, :] += jnp.sum(g_n * unit, axis=0, keepdims=True)
     misc_o[1:2, :] += jnp.sum(g_out * v, axis=0, keepdims=True)
     gf = gb.astype(f32)
     carried = nn(c, st[0]) * scale_x
-    prod = gf * (o - dskip[...] * v) + (g_out - gf) * carried
+    prod = gf * (o - dskip * v) + (g_out - gf) * carried
     high, low = halves(prod)
     sums_c = nn(jnp.concatenate([high, low], axis=1), f_sum[...])
     a_o[...] = jnp.transpose(sums_c)[0:HEAD_ROWS]
@@ -285,7 +292,7 @@
 
 
 def scan_kernel(
-    info, vbc, gb, gc, step, cum, pre, a_sum, st, gs_in, outg, sx, sb, jx, jb, cw, dskip, rate,
+    rows, info, vbc, gb, gc, step, cum, pre, a_sum, st, gs_in, outg, sx, sb, jx, jb, par,
     e_step, e_w, e8, f_one, f_two, f_three, tril,
     gcat_o, tail_o, head_o, misc_o, dt_o,
     run, ext, gram, acc,
@@ -293,9 +300,12 @@
     step_id = pl.program_id(0)
     blocks = pl.num_programs(0)
     i = blocks - 1 - step_id
-    starts, base, end_start, flag = read_info(info, i)
+    starts, base, end_start, flag = read_info(rows, info, i)
     inner = gb.shape[1]
-    taps, width = cw.shape
+    width = inner + jb.shape[1]
+    cw, taps = par[4:8, :], TAPS
+    rate = jnp.exp(par[8:16, 1:2])
+    dskip = lanes_of(par[8:16, 2:3], e8[...])
 
     @pl.when(step_id == 0)
     def _():
@@ -358,7 +368,7 @@
     wv = (v * w_x).astype(bf16)
     ext[0:STRETCH, inner : inner + 128] = (nn(g_gram, c) + nt(wv, low_after)) * sb[:, :128]
     ext[0:STRETCH, inner + 128 :] = (tn(g_gram, b) + nt(gc[...], state)) * sb[:, 128:]
-    gv = dskip[...] * gf + step_x * u + w_x * y
+    gv = dskip * gf + step_x * u + w_x * y
     h1, l1 = halves(v * u)
     h2, l2 = halves(v * y)
     h3, l3 = halves(jnp.concatenate(svs, axis=1) * u)
@@ -374,9 +384,9 @@
     g_cum = a_sum[...] - sums_r[2 * HEAD_ROWS : 3 * HEAD_ROWS] - ends
     end_add = jnp.sum(ends, axis=1, keepdims=True) + end_more
     g_log = exact_rows(g_cum, tril[...]) + end_add
-    g_step = g_step0 + g_end * end_decay - g_log * rate[...]
+    g_step = g_step0 + g_end * end_decay - g_log * rate
     g_pre_dt = g_step * jax.nn.sigmoid(pre[...])
-    dt_o[0:HEAD_ROWS, :] += g_log * (-step_v * rate[...])
+    dt_o[0:HEAD_ROWS, :] += g_log * (-step_v * rate)
     dt_o[HEAD_ROWS:, :] += g_pre_dt
     pad = jnp.zeros((128 - HEAD_ROWS, STRETCH), f32)
     gcat_o[:, width:] = jnp.transpose(jnp.concatenate([g_pre_dt, pad], axis=0)).astype(bf16)
@@ -412,20 +422,40 @@
 
 
 def exit_kernel(
-    info, tok, gout, mine, gz, gcat, tail, nxt, last_j, cw, gain, wz_out, wj,
-    gr_o, rim_o, rim_w_o, gain_o,
-    fix,
+    rows, blocks, rim_side, info, tok, gout, mine, gz, gcat, par, wz_out, wj, *rest
 ):
     step_id = pl.program_id(0)
-    blocks = pl.num_programs(0)
     i = blocks - 1 - step_id
-    starts, base, _end_start, _flag = read_info(info, i)
-    taps, width = cw.shape
+    starts, base, _end_start, _flag = read_info(rows, info, i)
     inner = gz.shape[1]
+    if rim_side:
+        tail, nxt, last_j, gr_o, gain_o, rim_o, rim_w_o, fix = rest
+        taps, width = TAPS, tail.shape[1]
+        cw = par[4:8, :width]
+    else:
+        gr_o, gain_o = rest
+    gain = par[0:1, :]
+
+    g_normed = nt(gz[...], wz_out[:, :inner]) + nt(gcat[...], wj[...])
+
+    def finish(g_normed):
+        unit, inverse = norm_rows(tok[...])
+        scaled = g_normed * gain
+        mean = jnp.mean(scaled * unit, axis=1, keepdims=True)
+        own = gout[...].astype(f32) * mine[...]
+        gr_o[...] = jnp.transpose(own + inverse * (scaled - unit * mean)).astype(bf16)
+        gain_o[...] += jnp.sum(g_normed * unit, axis=0, keepdims=True)
 
     @pl.when(step_id == 0)
     def _():
         gain_o[...] = jnp.zeros_like(gain_o)
+
+    if not rim_side:
+        finish(g_normed)
+        return
+
+    @pl.when(step_id == 0)
+    def _():
         fix[0:8, :] = jnp.zeros((8, width), f32)
         fix[8:16, :] = nxt[...]
         places = base + STRETCH - 8 + iota((8, 128), 0)
@@ -443,16 +473,6 @@
         fix[8:16, :] = total.astype(bf16).astype(f32) - tail[...].astype(bf16).astype(f32)
         rim_o[...] = fix[...].astype(bf16)
 
-    g_normed = nt(gz[...], wz_out[:, :inner]) + nt(gcat[...], wj[...])
-
-    def finish(g_normed):
-        unit, inverse = norm_rows(tok[...])
-        scaled = g_normed * gain[...]
-        mean = jnp.mean(scaled * unit, axis=1, keepdims=True)
-        own = gout[...].astype(f32) * mine[...]
-        gr_o[...] = jnp.transpose(own + inverse * (scaled - unit * mean)).astype(bf16)
-        gain_o[...] += jnp.sum(g_normed * unit, axis=0, keepdims=True)
-
     @pl.when(step_id == 0)
     def _():
         more = nt(rim_o[...], wj[:, :width])
@@ -499,12 +519,15 @@
     return parity, index + 1 - 2 * parity
 
 
-def gather_kernel(n, x, bc, dt, out, sent, came, passed, relayed, own):
+def gather_kernel(n, chain, x, bc, dt, tok, out, halo, sent, came, passed, relayed, own, hop):
     f = lax.axis_index("fsdp")
     parity, twin = twin_of(lax.axis_index("ctx"))
     rows = x.shape[0]
     half = rows // 2
-    start_together([{"fsdp": turned(f, d, n)} for d in range(1, n)] + [{"ctx": twin}])
+    here = lax.axis_index("ctx")
+    following = turned(here, 1, chain)
+    sides = [{"ctx": twin}] if chain == 2 else [{"ctx": following}, {"ctx": turned(here, -1, chain)}]
+    start_together([{"fsdp": turned(f, d, n)} for d in range(1, n)] + sides)
     pieces = []
     at = 0
     for ref in (x, bc, dt):
@@ -524,7 +547,12 @@
             )
             copy.start()
             copies.append(copy)
-    locals_ = []
+    edge = halo.shape[0]
+    copy = remote(
+        tok.at[pl.ds(tok.shape[0] - edge, edge), :], halo, hop.at[0], hop.at[1], {"ctx": following}
+    )
+    copy.start()
+    locals_ = [copy]
     for p, (ref, cols) in enumerate(pieces):
         copy = pltpu.make_async_copy(
             ref, out.at[pl.ds(pl.multiple_of(f * rows, 16), rows), cols], own.at[p]
@@ -548,18 +576,22 @@
         copy.wait()
 
 
-def gathered(x, bc, dt):
+def gathered(x, bc, dt, tok):
     n = lax.axis_size("fsdp")
     pieces = (n - 1, 3)
     width = x.shape[1] + bc.shape[1] + dt.shape[1]
     return pl.pallas_call(
-        functools.partial(gather_kernel, n),
-        out_shape=jax.ShapeDtypeStruct((n * x.shape[0], width), bf16),
-        in_specs=[pl.BlockSpec(memory_space=pltpu.VMEM)] * 3,
-        out_specs=pl.BlockSpec(memory_space=pltpu.VMEM),
-        scratch_shapes=[pltpu.SemaphoreType.DMA(pieces)] * 4 + [pltpu.SemaphoreType.DMA((3,))],
+        functools.partial(gather_kernel, n, lax.axis_size("ctx")),
+        out_shape=[
+            jax.ShapeDtypeStruct((n * x.shape[0], width), bf16),
+            jax.ShapeDtypeStruct((16, tok.shape[1]), bf16),
+        ],
+        in_specs=[pl.BlockSpec(memory_space=pltpu.VMEM)] * 3 + [pl.BlockSpec(memory_space=pl.ANY)],
+        out_specs=[pl.BlockSpec(memory_space=pltpu.VMEM)] * 2,
+        scratch_shapes=[pltpu.SemaphoreType.DMA(pieces)] * 4
+        + [pltpu.SemaphoreType.DMA((3,)), pltpu.SemaphoreType.DMA((2,))],
         compiler_params=pltpu.CompilerParams(collective_id=1, has_side_effects=True),
-    )(x, bc, dt)
+    )(x, bc, dt, tok)
 
 
 def total_kernel(n, part, out, slots, sent, came):
@@ -675,7 +707,7 @@
         whole = whole + slots[q].astype(f32)
     final[...] = whole
     bc_at = slice(3 * inner, 3 * inner + bc_cols)
-    bc_slots[pl.ds(t, 1)] = whole[:, bc_at][None]
+    bc_slots[pl.ds(t, 1)] = whole[:, bc_at].astype(bf16)[None]
     wide = jnp.concatenate([small_sum[:, conv_bc:w_scan], small_sum[:, at:]], axis=1)
     wide_slots[pl.ds(t, 1)] = wide[None]
     o_small[...] = small_sum[:, :at]
@@ -688,10 +720,10 @@
             thirds_.append(copy)
     for copy in thirds_:
         copy.wait()
-    bc_sum = bc_slots[0]
+    bc_sum = bc_slots[0].astype(f32)
     wide_sum = wide_slots[0]
     for q in range(1, m):
-        bc_sum = bc_sum + bc_slots[q]
+        bc_sum = bc_sum + bc_slots[q].astype(f32)
         wide_sum = wide_sum + wide_slots[q]
     o_wide[...] = wide_sum
     final[:, bc_at] = bc_sum
@@ -743,7 +775,7 @@
             pltpu.VMEM((n, half, wide), bf16),
             pltpu.VMEM((n, half, wide), bf16),
             pltpu.VMEM((half, wide), f32),
-            pltpu.VMEM((m, half, bc_cols), f32),
+            pltpu.VMEM((m, half, bc_cols), bf16),
             pltpu.VMEM((8, small), f32),
             pltpu.VMEM((2, max(n, 2), 8, small), f32),
             pltpu.VMEM((m, 8, crossing), f32),
@@ -799,28 +831,28 @@
     return lax.fori_loop(0, size, lap, jnp.zeros(state.shape, f32)).astype(bf16)
 
 
-def call(kernel, blocks, ins, outs, scratch, micros=0):
+def call(kernel, blocks, ins, outs, scratch, kept=()):
     def spec(shape, how):
         if how == "smem":
             return pl.BlockSpec(memory_space=pltpu.SMEM)
         return pl.BlockSpec(shape, how)
 
+    def body(*refs):
+        kernel(*refs[: len(ins)], *refs[len(ins) + len(kept) :])
+
     return pl.pallas_call(
-        kernel,
+        body,
         grid=(blocks,),
-        in_specs=[spec(shape, how) for _a, shape, how in ins],
+        in_specs=[spec(shape, how) for _a, shape, how in ins]
+        + [pl.BlockSpec(memory_space=pl.ANY)] * len(kept),
         out_specs=[spec(shape, how) for _s, shape, how in outs],
         out_shape=[s for s, _sh, _h in outs],
         scratch_shapes=scratch,
-        cost_estimate=pl.CostEstimate(
-            flops=0, transcendentals=0, bytes_accessed=3_000_000 * micros
-        )
-        if micros
-        else None,
+        input_output_aliases={len(ins) + k: k for k in range(len(kept))},
         compiler_params=pltpu.CompilerParams(
             dimension_semantics=("arbitrary",), vmem_limit_bytes=56 * 1024 * 1024
         ),
-    )(*[a for a, _s, _h in ins])
+    )(*[a for a, _s, _h in ins], *kept)
 
 
 def local(
@@ -840,24 +872,26 @@
     ctx_index = lax.axis_index("ctx")
     e8, spread, gather, upper, lower = constants(inner, heads)
 
-    w_joined = gathered(w_x, w_bc, jnp.pad(w_dt, ((0, 0), (0, 128 - heads))))
-    wz_out = lax.all_gather(jnp.concatenate([w_z, w_out.T], axis=1), "fsdp", axis=0, tiled=True)
-
-    starts = jnp.cumsum(lengths[0]) - lengths[0]
-    info = jnp.concatenate([(ctx_index * rows).astype(jnp.int32)[None], starts.astype(jnp.int32)])
-    halo = passed_along(tokens[rows - 16 :], "ctx", 1)
-    gain = norm_gain[None, :]
-    conv_w = jnp.concatenate([conv_x_w, conv_bc_w], axis=1)
-    conv_b = jnp.concatenate([conv_x_b, conv_bc_b])[None, :]
-
-    def head_rows(x):
-        return jnp.broadcast_to(jnp.pad(x, (0, HEAD_ROWS - heads))[:, None], (HEAD_ROWS, STRETCH))
-
-    bias = head_rows(dt_bias)
-    rate = head_rows(jnp.exp(a_log))
+    w_joined, halo = gathered(w_x, w_bc, jnp.pad(w_dt, ((0, 0), (0, 128 - heads))), tokens)
+    second = jnp.concatenate([w_z, w_out.T], axis=1)
+    second, w_joined = lax.optimization_barrier((second, w_joined))
+    wz_out = lax.all_gather(second, "fsdp", axis=0, tiled=True)
     per_head = inner // heads
-    dskip = jnp.repeat(d_skip, per_head)[None, :]
-    ggain = gate_gain[None, :]
+
+    def line(*vectors):
+        joint = jnp.concatenate(vectors) if len(vectors) > 1 else vectors[0]
+        return jnp.pad(joint, (0, model - joint.shape[0]))[None, :]
+
+    per_heads = jnp.stack([dt_bias, a_log, d_skip], axis=1)
+    params = jnp.concatenate(
+        [
+            line(norm_gain), line(conv_x_b, conv_bc_b), line(gate_gain), jnp.zeros((1, model), f32),
+            jnp.pad(conv_x_w, ((0, 0), (0, model - inner)))
+            + jnp.pad(conv_bc_w, ((0, 0), (inner, model - width))),
+            jnp.pad(per_heads, ((0, HEAD_ROWS - heads), (0, model - 3))),
+        ],
+        axis=0,
+    )
 
     def shape(dims, kind):
         return jax.ShapeDtypeStruct(dims, kind)
@@ -883,14 +917,13 @@
     def fixed(x):
         return (x, x.shape, lambda i: (0,) * len(x.shape))
 
-    info_in = (info, None, "smem")
+    info_in = (lengths, None, "smem")
     state_dims = (blocks, states, inner)
     normed, joined_x, joined_bc, vbc, slope_x, slope_bc, pre, step, cum, s_part, end_state, decay = call(
-        entry_kernel,
+        functools.partial(entry_kernel, rows),
         blocks,
         [
-            info_in, by_rows(tokens), whole(halo), whole(gain), whole(w_joined),
-            whole(conv_w), whole(conv_b), whole(bias), whole(rate), whole(upper),
+            info_in, by_rows(tokens), whole(halo), whole(params), whole(w_joined), whole(upper),
             whole(spread(0)), whole(e8),
         ],
         [
@@ -914,33 +947,33 @@
         ],
     )
     incoming = entering(decay, end_state, "ctx", False)
-    z_part, out, gn, branch, sums, state_in = call(
-        mix_kernel,
+    z_part, out, gn, sums, state_in, branch = call(
+        functools.partial(mix_kernel, rows),
         blocks,
         [
             info_in, by_rows(vbc), by_lanes(step), by_lanes(cum), by_block(s_part),
-            whole(incoming), by_rows(normed), by_rows(grad_out), whole(wz_out), whole(dskip),
-            whole(ggain), whole(spread(1)), whole(spread(2)), whole(e8),
+            whole(incoming), by_rows(normed), by_rows(grad_out), whole(wz_out), whole(params),
+            whole(spread(1)), whole(spread(2)), whole(e8),
         ],
         [
             by_rows(shape((rows, inner), f32)),
             by_rows(shape((rows, inner), f32)),
             by_rows(shape((rows, inner), f32)),
-            by_lanes(shape((model, rows), bf16)),
             by_lanes(shape((2, rows), f32)),
             by_block(shape(state_dims, bf16)),
+            by_lanes(shape((model, rows), bf16)),
         ],
         [pltpu.VMEM((states, inner), f32), pltpu.VMEM((STRETCH, STRETCH), f32)],
     )
+    branch = lax.psum_scatter(branch, "tp", scatter_dimension=0, tiled=True)
     sums = total_over_tp(sums)
-    branch = lax.psum_scatter(branch, "tp", scatter_dimension=0, tiled=True)
     g_z, g_b, g_c, normed_two, a_sum, gs_part, start_state, misc_gate = call(
-        gate_kernel,
+        functools.partial(gate_kernel, rows),
         blocks,
         [
             info_in, by_lanes(sums, True), by_lanes(cum, True), by_rows(out, True),
             by_rows(z_part, True), by_rows(gn, True), by_rows(vbc, True), by_block(state_in, True),
-            whole(dskip), whole(ggain), whole(spread(2)), whole(e8), whole(gather(0)),
+            whole(params), whole(spread(2)), whole(e8), whole(gather(0)),
         ],
         [
             by_rows(shape((rows, inner), bf16), True),
@@ -956,14 +989,14 @@
     )
     outgoing = entering(decay, start_state, "ctx", True)
     g_cat, tail, head, misc_scan, misc_dt = call(
-        scan_kernel,
+        functools.partial(scan_kernel, rows),
         blocks,
         [
             info_in, by_rows(vbc, True), by_rows(g_b, True), by_rows(g_c, True),
             by_lanes(step, True), by_lanes(cum, True), by_lanes(pre, True), by_lanes(a_sum, True),
             by_block(state_in, True), by_block(gs_part, True), whole(outgoing),
             by_rows(slope_x, True), by_rows(slope_bc, True), by_rows(joined_x, True),
-            by_rows(joined_bc, True), whole(conv_w), whole(dskip), whole(rate), whole(spread(1)),
+            by_rows(joined_bc, True), whole(params), whole(spread(1)),
             whole(spread(2)), whole(e8), whole(gather(0)), whole(gather(1)),
             whole(gather(2)), whole(lower),
         ],
@@ -985,20 +1018,36 @@
     feature = jnp.arange(model, dtype=jnp.int32) // slice_width
     mine = (feature == tp_index).astype(f32)[None, :]
     last_joined = jnp.concatenate([joined_x[rows - 16 :], joined_bc[rows - 16 :]], axis=1)
-    g_resid, rim, rim_w, gain_part = call(
-        exit_kernel,
-        blocks,
-        [
-            info_in, by_rows(tokens, True), by_rows(grad_out, True), whole(mine),
-            by_rows(g_z, True), by_rows(g_cat, True), whole(tail), whole(next_rows), whole(last_joined), whole(conv_w), whole(gain),
-            whole(wz_out), whole(w_joined),
-        ],
-        [
-            by_lanes(shape((model, rows), bf16), True),
-            fixed(shape((16, width), bf16)),
-            fixed(shape((8, width), f32)),
-            fixed(shape((1, model), f32)),
-        ],
+    def exit_call(first, extra_in, extra_out, scratch):
+        top = count = blocks
+
+        def flipped(x):
+            return (x, (STRETCH, x.shape[1]), lambda i: (top - 1 - i, 0))
+
+        return call(
+            functools.partial(exit_kernel, rows, top, first),
+            count,
+            [
+                info_in, flipped(tokens), flipped(grad_out), whole(mine), flipped(g_z),
+                flipped(g_cat), whole(params), whole(wz_out), whole(w_joined),
+            ]
+            + extra_in,
+            [
+                (
+                    shape((model, count * STRETCH), bf16),
+                    (model, STRETCH),
+                    lambda i: (0, count - 1 - i),
+                ),
+                fixed(shape((1, model), f32)),
+            ]
+            + extra_out,
+            scratch,
+        )
+
+    g_resid, gain_part, rim, rim_w = exit_call(
+        True,
+        [whole(tail), whole(next_rows), whole(last_joined)],
+        [fixed(shape((16, width), bf16)), fixed(shape((8, width), f32))],
         [pltpu.VMEM((16, width), f32)],
     )
     g_resid = lax.psum_scatter(g_resid, "tp", scatter_dimension=0, tiled=True)
@@ -1035,16 +1084,17 @@
     grad_norm_gain = lax.dynamic_slice_in_dim(s_wide[0, 2 * states :], here, slice_width, 0)
     place = tp_index.astype(jnp.int32)[None]
 
+    wide = 2 * STRETCH
     layer_out = call(
         functools.partial(finish_kernel, tp_size),
         blocks // 2,
         [
             (place, None, "smem"),
-            (branch, (slice_width, 2 * STRETCH), lambda i: (0, i)),
-            (tokens, (2 * STRETCH, model), lambda i: (i, 0)),
-            (sums, (2, 2 * STRETCH), lambda i: (0, i)),
-        ],
-        [(shape((slice_width, rows), bf16), (slice_width, 2 * STRETCH), lambda i: (0, i))],
+            (branch, (slice_width, wide), lambda i: (0, i)),
+            (tokens, (wide, model), lambda i: (i, 0)),
+            (sums, (2, wide), lambda i: (0, i)),
+        ],
+        [(shape((slice_width, rows), bf16), (slice_width, wide), lambda i: (0, i))],
         [],
     )[0].T
     grad_tokens = g_resid.T

time: 287 us -> 278 us (0.969)
  waiting for transfers between devices: 21.9 us -> 28.3 us
  local copies, waits for them, and re-layouts: 21 us -> 14.6 us
  Pallas kernels: 198 us -> 195 us
    pallas_call x1, Pallas kernels: 45.3 us -> 39.1 us  [reduced(): pl.pallas_call(functools.partial(reduce_kernel, n, m, bc_cols, inner), ou...]
    reduce_scatter x1, waiting for transfers between devices: 20.5 us -> 24.4 us  [local(): g_resid = lax.psum_scatter(g_resid, 'tp', scatter_dimension=0, tiled=True)]
    broadcast_in_dim x6 -> x4, local copies, waits for them, and re-layouts: 3.82 us -> 0.02 us  [the longest x3 0.01 us: line(): return jnp.pad(joint, (0, model - joint.shape[0]))[None, :]]
    ppermute x4 -> x3, starting transfers between devices: 7.43 us -> 5.04 us  [passed_along(): return lax.ppermute(block, axis, route)]
    unnamed x39 -> x48, local copies, waits for them, and re-layouts: 7.2 us -> 6.53 us
  transfers between devices with their start and end apart: 7 -> 6, of which waited for: 3 -> 4; matrix products, arithmetic and copies ran while one was open for 12% -> 9% of each run, Pallas kernels for 62% -> 58%
where the time goes in v3:
time: 278 us; the launch traced here: 276 us
  Pallas kernels  195 us (70%)
  waiting for transfers between devices  28.3 us (10%)
  local copies, waits for them, and re-layouts  14.6 us (5%)
  matrix products  14.1 us (5%)
  between operations  14.1 us (5%)
  starting transfers between devices  5.16 us (2%)
  other arithmetic  4.29 us (2%)
    pallas_call x6, Pallas kernels, call(): pl.pallas_call(body, grid=(blocks,), in_specs=[spec(shape, how) for _a, s...  133 us
    pallas_call x1, Pallas kernels, reduced(): pl.pallas_call(functools.partial(reduce_kernel, n, m, bc_cols, inner), ou...  39.1 us
    reduce_scatter x1, waiting for transfers between devices, local(): g_resid = lax.psum_scatter(g_resid, 'tp', scatter_dimension=0, tiled=True)  24.4 us
    pallas_call x1, Pallas kernels, gathered(): pl.pallas_call(functools.partial(gather_kernel, n, lax.axis_size('ctx')),...  14.7 us
    dot_general x4, matrix products, tn(): lax.dot_general(left, right, (((0,), (0,)), ((), ())), preferred_element_...  14.1 us
    pallas_call x1, Pallas kernels, total_over_tp(): pl.pallas_call(functools.partial(total_kernel, n), out_shape=jax.ShapeDty...  8.6 us
    unnamed x48, local copies, waits for them, and re-layouts  6.53 us
  transfers between devices with their start and end apart: 6, of which 4 were waited for; matrix products, arithmetic and copies ran while one was open for 9% of the time, Pallas kernels for 58%

profile of v3, /device:TPU:0, one launch (start us, length us, event | category | flops | bytes accessed | tf_op | source)
XLA Modules:
  0.0 276.0 jit_solution(2133665948451698748)
XLA Ops:
  7.2 0.8 copy.46
  8.1 0.6 pad.28.dt
  8.7 1.7 pad_maximum_fusion
  10.5 14.7 %shard_map.405 = (bf16[768,768]{1,0:T(8,128)(2,1)}, bf16[16,768]{1,0:T(8,128)(2,1)}) custom-call(bf16[192,384]{1,0:T(8,128)(2,1)} %x.15, bf16[192,256]{1,0:T(8,128)(2,1)} %bc.1, bf16[192,128]{1,0:T(8,128)(2,1)} %pad.28.dt, bf16[3072,768]{1,0:T(8,128)(2,1)} %refs_1_.3), custom_call_target="tpu_custom_call" | custom-call | tf_op jit(solution)/shard_map/pallas_call | solution.py:583
  25.7 1.2 concatenate.13.refs_3_.refs_9_.refs_8_.refs_15_.refs_6_
  27.0 24.0 %shard_map.406 = (bf16[3072,768]{1,0:T(8,128)(2,1)}, bf16[3072,384]{1,0:T(8,128)(2,1)}, bf16[3072,256]{1,0:T(8,128)(2,1)}, bf16[3072,640]{1,0:T(8,128)(2,1)}, bf...) custom-call(s32[1,4]{1,0:T(1,128)} %refs_0_.9, ...), custom_call_target="tpu_custom_call" | custom-call | tf_op jit(solution)/shard_map/pallas_call | solution.py:843
  50.9 2.3 collective-permute-start
  53.2 1.1 collective-permute-done.refs_5_
  55.0 21.9 %shard_map.407 = (f32[3072,384]{1,0:T(8,128)}, f32[3072,384]{1,0:T(8,128)}, f32[3072,384]{1,0:T(8,128)}, f32[2,3072]{1,0:T(2,128)}, bf16[12,128,384]{2,1,0:T(8,128)(2,1)}, /*index=5*/bf16[768,3072]{1,0:T(8,128)(2,1)}) custom-call(s32[1,4]{1,0:T(1,128)} %refs_0_.9, bf16[3072,640]{1,0:T(8,128)(2,1)} %get-tuple-element.62.refs_1_.refs_6_, ...), custom_call_target="tpu_custom_call" | custom-call | tf_op jit(solution)/shard_map/pallas_call | solution.py:843
  77.0 0.7 slice.46
  77.7 0.7 slice.45
  78.4 8.6 %shard_map.408.refs_3_.refs_1_ = f32[2,3072]{1,0:T(2,128)} custom-call(f32[2,3072]{1,0:T(2,128)} %get-tuple-element.70.part), custom_call_target="tpu_custom_call" | custom-call | tf_op jit(solution)/shard_map/pallas_call | solution.py:618
  87.0 17.4 %shard_map.410 = (bf16[3072,384]{1,0:T(8,128)(2,1)}, bf16[3072,384]{1,0:T(8,128)(2,1)}, bf16[3072,384]{1,0:T(8,128)(2,1)}, bf16[3072,384]{1,0:T(8,128)(2,1)}, f3...) custom-call(s32[1,4]{1,0:T(1,128)} %refs_0_.9, ...), custom_call_target="tpu_custom_call" | custom-call | tf_op jit(solution)/shard_map/pallas_call | solution.py:843
  104.3 1.3 collective-permute-start.1
  106.2 1.5 collective-permute-done.1.refs_10_
  108.4 44.7 %shard_map.411 = (bf16[3072,768]{1,0:T(8,128)(2,1)}, f32[8,640]{1,0:T(8,128)}, f32[8,640]{1,0:T(8,128)}, f32[8,640]{1,0:T(8,128)}, f32[16,256]{1,0:T(8,128)}) custom-call(s32[1,4]{1,0:T(1,128)} %refs_0_.9, bf16[3072,640]{1,0:T(8,128)(2,1)} %get-tuple-element.62.refs_1_.refs_6_, bf16[3072,384]{1,0:T(8,128)(2,1)} %get-tuple-element.76.refs_2_, ...), custom_call_target="tpu_custom_call" | custom-call | tf_op jit(solution)/shard_map/pallas_call | solution.py:843
  153.1 1.5 collective-permute-start.2
  155.1 1.2 collective-permute-done.2.refs_10_
  157.0 19.3 %shard_map.412 = (bf16[768,3072]{1,0:T(8,128)(2,1)}, f32[1,768]{1,0:T(1,128)}, bf16[16,640]{1,0:T(8,128)(2,1)}, f32[8,640]{1,0:T(8,128)}) custom-call(s32[1,4]{1,0:T(1,128)} %refs_0_.9, bf16[3072,768]{1,0:T(8,128)(2,1)} %refs_1_.3, bf16[3072,768]{1,0:T(8,128)(2,1)} %refs_2_.3, f32[1,768]{1,0:T(1,128)} %compare_convert_fusion.refs_3_, ...), custom_call_target="tpu_custom_call" | custom-call | tf_op jit(solution)/shard_map/pallas_call | solution.py:843
  176.3 1.6 copy-done.19
  178.0 4.7 %convolution_bitcast_fusion.p_out = f32[768,384]{1,0:T(8,128)S(1)} fusion(bf16[3072,384]{1,0:T(8,128)(2,1)S(1)} %copy-done.19, bf16[3072,768]{1,0:T(8,128)(2,1)} %refs_2_.3), kind=kOutput, calls=%fused_computation.1 | convolution fusion | flops 1811939328 | bytes 8257536 | tf_op jit(solution)/shard_map/dot_general | solution.py:31
  182.7 2.6 fusion.2.p_z
  185.9 6.3 %pad_add_fusion.p_cat = f32[768,768]{1,0:T(8,128)S(1)} fusion(f32[768,640]{1,0:T(8,128)S(1)} %fusion, bf16[3072,768]{1,0:T(8,128)(2,1)S(1)} %bitcast.21, bf16[3072,768]{1,0:T(8,128)(2,1)} %get-tuple-element.86.refs_5_), kind=kOutput, calls=%fused_computation | convolution fusion | flops 3624468480 | bytes 13762560 | tf_op jit(solution)/shard_map/dot_general | solution.py:31
  192.3 39.1 %shard_map.413 = (f32[192,384]{1,0:T(8,128)S(1)}, f32[192,384]{1,0:T(8,128)S(1)}, f32[192,768]{1,0:T(8,128)S(1)}, f32[8,1536]{1,0:T(8,128)S(1)}, f32[8,1024]{1,0:T(8,128)S(1)}) custom-call(f32[768,384]{1,0:T(8,128)S(1)} %convolution_bitcast_fusion.p_out, f32[768,384]{1,0:T(8,128)S(1)} %fusion.2.p_z, f32[768,768]{1,0:T(8,128)S(1)} %pad_add_fusion.p_cat, ...), custom_call_target="tpu_custom_call" | custom-call | tf_op jit(solution)/shard_map/pallas_call | solution.py:764
  231.4 0.7 slice.49
  232.1 0.7 slice.50
  234.0 0.7 copy.51
  237.2 0.7 slice_reduce_fusion
  237.9 5.7 %shard_map.409 = bf16[192,3072]{1,0:T(8,128)(2,1)} custom-call(s32[1]{0:T(128)} %bitcast.refs_0_, bf16[192,3072]{1,0:T(8,128)(2,1)} %reduce-scatter.3.cloned.1.call-done.refs_1_, bf16[3072,768]{1,0:T(8,128)(2,1)} %refs_1_.3, f32[2,3072]{1,0:T(2,128)} %shard_map.408.refs_3_.refs_1_), custom_call_target="tpu_custom_call" | custom-call | tf_op jit(solution)/shard_map/pallas_call | solution.py:843
  243.6 24.4 %reduce-scatter.5.cloned.1.call-done = bf16[192,3072]{1,0:T(8,128)(2,1)} async-done(((bf16[768,3072]{1,0:T(8,128)(2,1)}), bf16[192,3072]{1,0:T(8,128)(2,1)}) %reduce-scatter.5.cloned.1.call-update) | async-done | bytes 1179664 | tf_op jit(solution)/shard_map/reduce_scatter | solution.py:1053
  268.0 0.7 copy.55
  268.7 0.7 copy.56
  (75 shorter events, 7.9 us)
Async XLA Ops:
  7.2 47.2 %all-gather.2.cloned.1.call-start = ((), (), s32[]{:S(2)}) async-start(), calls=%async_computation.2 | async-start | bytes 1474560 | tf_op jit(solution)/shard_map/all_gather | solution.py:878
  10.4 14.8 %copy-start.11 = (f32[768]{0:T(1024)S(1)}, f32[768]{0:T(1024)}, u32[]{:S(2)}) copy-start(f32[768]{0:T(1024)} %param.33) | copy-start | bytes 9220
  10.4 14.8 %copy-start.13 = (f32[384]{0:T(512)S(1)}, f32[384]{0:T(512)}, u32[]{:S(2)}) copy-start(f32[384]{0:T(512)} %param.39) | copy-start | bytes 4612
  10.4 14.8 %copy-start.15 = (f32[256]{0:T(256)S(1)}, f32[256]{0:T(256)}, u32[]{:S(2)}) copy-start(f32[256]{0:T(256)} %param.41) | copy-start | bytes 3076
  10.4 14.9 %copy-start.14 = (f32[384]{0:T(512)S(1)}, f32[384]{0:T(512)}, u32[]{:S(2)}) copy-start(f32[384]{0:T(512)} %param.45) | copy-start | bytes 4612
  10.4 14.9 %copy-start.16 = (f32[6]{0:T(128)S(1)}, f32[6]{0:T(128)}, u32[]{:S(2)}) copy-start(f32[6]{0:T(128)} %param.44) | copy-start | bytes 76
  10.4 15.0 %copy-start.17 = (f32[6]{0:T(128)S(1)}, f32[6]{0:T(128)}, u32[]{:S(2)}) copy-start(f32[6]{0:T(128)} %param.43) | copy-start | bytes 76
  10.5 15.1 %copy-start.18 = (f32[6]{0:T(128)S(1)}, f32[6]{0:T(128)}, u32[]{:S(2)}) copy-start(f32[6]{0:T(128)} %param.42) | copy-start | bytes 76
  10.5 15.2 %copy-start.10 = (f32[4,384]{1,0:T(4,128)S(1)}, f32[4,384]{1,0:T(4,128)}, u32[]{:S(2)}) copy-start(f32[4,384]{1,0:T(4,128)} %param.38) | copy-start | bytes 18436
  10.5 15.2 %copy-start.12 = (f32[4,256]{1,0:T(4,128)S(1)}, f32[4,256]{1,0:T(4,128)}, u32[]{:S(2)}) copy-start(f32[4,256]{1,0:T(4,128)} %param.40) | copy-start | bytes 12292
  25.2 212.7 %reduce-scatter.3.cloned.1.call-start = ((), (), s32[]{:S(2)}) async-start(), calls=%async_computation.3 | async-start | bytes 5898240 | tf_op jit(solution)/shard_map/reduce_scatter | solution.py:968
  50.9 3.4 %collective-permute-start = (bf16[128,384]{1,0:T(8,128)(2,1)}, bf16[128,384]{1,0:T(8,128)(2,1)S(1)}, u32[]{:S(2)}, u32[]{:S(2)}) collective-permute-start(bf16[128,384]{1,0:T(8,128)(2,1)} %get-tuple-element.66), channel_id=1, source_target_pairs={{0,4},{1,5},{2,6},{3,7},{8,12},{9,13},{10,14},{11,15},{16,20},{17,... | collective-permute-start | bytes 294920 | tf_op jit(solution)/shard_map/ppermute | solution.py:814
  54.3 0.6 copy-start.7
  76.9 191.1 %reduce-scatter.5.cloned.1.call-start = ((), (), s32[]{:S(2)}) async-start(), calls=%async_computation.4 | async-start | bytes 5898240 | tf_op jit(solution)/shard_map/reduce_scatter | solution.py:1053
  104.3 3.4 %collective-permute-start.1 = (bf16[128,384]{1,0:T(8,128)(2,1)}, bf16[128,384]{1,0:T(8,128)(2,1)S(1)}, u32[]{:S(2)}, u32[]{:S(2)}) collective-permute-start(bf16[128,384]{1,0:T(8,128)(2,1)} %get-tuple-element.81), channel_id=1, source_target_pairs={{4,0},{5,1},{6,2},{7,3},{12,8},{13,9},{14,10},{15,11},{20,16},{21,... | collective-permute-start | bytes 294920 | tf_op jit(solution)/shard_map/ppermute | solution.py:814
  107.8 0.6 copy-start.6
  153.1 3.3 %collective-permute-start.2 = (f32[8,640]{1,0:T(8,128)}, f32[8,640]{1,0:T(8,128)S(1)}, u32[]{:S(2)}, u32[]{:S(2)}) collective-permute-start(f32[8,640]{1,0:T(8,128)} %get-tuple-element.88), channel_id=1, source_target_pairs={{4,0},{5,1},{6,2},{7,3},{12,8},{13,9},{14,10},{15,11},{20,16},{21,... | collective-permute-start | bytes 61448 | tf_op jit(solution)/shard_map/ppermute | solution.py:814
  156.3 0.6 copy-start.9
  176.3 1.7 copy-start.19
  176.3 6.4 %slice-start = ((s8[4718592]{0:T(1024)(128)(4,1)}), s8[524288]{0:T(1024)(128)(4,1)S(1)}, s32[]{:S(2)}) async-start(s8[4718592]{0:T(1024)(128)(4,1)} %bitcast.20), calls=%async_computation.5 | async-start | bytes 1048576
  178.0 4.7 %slice-start.1 = ((s8[4718592]{0:T(1024)(128)(4,1)}), s8[4194304]{0:T(1024)(128)(4,1)S(1)}, s32[]{:S(2)}) async-start(s8[4718592]{0:T(1024)(128)(4,1)} %bitcast.20), calls=%async_computation.6 | async-start | bytes 8388608
  178.0 4.7 %copy-start.5 = (bf16[3072,384]{1,0:T(8,128)(2,1)S(1)}, bf16[3072,384]{1,0:T(8,128)(2,1)}, u32[]{:S(2)}) copy-start(bf16[3072,384]{1,0:T(8,128)(2,1)} %get-tuple-element.75.refs_4_) | copy-start | bytes 7077892
  182.7 2.6 copy-start.8
  185.8 6.4 %copy-start = (f32[8,640]{1,0:T(8,128)S(1)}, f32[8,640]{1,0:T(8,128)}, u32[]{:S(2)}) copy-start(f32[8,640]{1,0:T(8,128)} %get-tuple-element.92.m_scan) | copy-start | bytes 61444
  185.8 6.4 %copy-start.1 = (f32[8,640]{1,0:T(8,128)S(1)}, f32[8,640]{1,0:T(8,128)}, u32[]{:S(2)}) copy-start(f32[8,640]{1,0:T(8,128)} %get-tuple-element.93.m_rim) | copy-start | bytes 61444
  185.8 6.4 %copy-start.2 = (f32[16,256]{1,0:T(8,128)S(1)}, f32[16,256]{1,0:T(8,128)}, u32[]{:S(2)}) copy-start(f32[16,256]{1,0:T(8,128)} %get-tuple-element.95.m_dt) | copy-start | bytes 49156
  185.8 6.4 %copy-start.3 = (f32[8,384]{1,0:T(8,128)S(1)}, f32[8,384]{1,0:T(8,128)}, u32[]{:S(2)}) copy-start(f32[8,384]{1,0:T(8,128)} %get-tuple-element.94.m_gate) | copy-start | bytes 36868
  185.9 6.4 %copy-start.4 = (f32[1,768]{1,0:T(1,128)S(1)}, f32[1,768]{1,0:T(1,128)}, u32[]{:S(2)}) copy-start(f32[1,768]{1,0:T(1,128)} %get-tuple-element.96.m_gain) | copy-start | bytes 9220
Sparse Core Ops, SparseCore 0:
  25.3 28.5 all-gather.1
  77.0 86.2 reduce-scatter.2
  176.5 91.5 reduce-scatter.4

commit v4 on v3

--- a/solution.py
+++ b/solution.py
@@ -198,26 +198,41 @@
     scale_x = nn(both, e_scale[...])
     b = vbc[:, inner : inner + 128]
     c = vbc[:, inner + 128 : inner + 256]
-    t_at = iota((STRETCH, STRETCH), 0)
-    s_at = iota((STRETCH, STRETCH), 1)
-    t_first = segment_start(t_at + base, starts)
-    mask = (s_at <= t_at) & (s_at + base >= t_first)
-    gram[...] = jnp.where(mask, nt(c, b), 0.0)
     carried = nn(c, st) * scale_x
+    half = STRETCH // 2
+    low, high = slice(0, half), slice(half, STRETCH)
+    t_at = iota((half, STRETCH), 0)
+    s_at = iota((half, STRETCH), 1)
+    causal = (s_at <= t_at)[:, low]
+    first_low = segment_start(iota((half, half), 0) + base, starts)
+    first_high = segment_start(t_at + (base + half), starts)
+    mask_a = causal & ((s_at + base)[:, low] >= first_low)
+    mask_b = (s_at <= t_at + half) & (s_at + base >= first_high)
+    gram[low, low] = jnp.where(mask_a, nt(c[low], b[low]), 0.0)
+    gram[high, :] = jnp.where(mask_b, nt(c[high], b), 0.0)
     lane = iota((STRETCH, 128), 1)
     pieces = []
     for p in range(inner // 128):
         at = slice(128 * p, 128 * (p + 1))
         v = vbc[:, at].astype(f32)
-        sv = v * step_x[:, at]
-        acc = carried[:, at] + dskip[:, at] * v
+        sv = (v * step_x[:, at]).astype(bf16)
+        rest = carried[:, at] + dskip[:, at] * v
+        acc_low, acc_high = rest[low], rest[high]
         for j in range(2):
             h = 2 * p + j
-            half = jnp.where((lane < 64) if j == 0 else (lane >= 64), sv, 0.0).astype(bf16)
-            gap = cols[:, h : h + 1] - cum2[h : h + 1, :]
-            m = (gram[...] * jnp.exp2(jnp.minimum(gap, 0.0))).astype(bf16)
-            acc = acc + nn(m, half)
-        pieces.append(acc)
+            side = (lane < 64) if j == 0 else (lane >= 64)
+            part = jnp.where(side, sv, jnp.zeros_like(sv))
+            row = cum2[h : h + 1, :]
+            first_gap = cols[low, h : h + 1] - row[:, low]
+            cross_gap = cols[high, h : h + 1] - row[:, low]
+            last_gap = cols[high, h : h + 1] - row[:, high]
+            decay_b = jnp.concatenate(
+                [jnp.exp2(cross_gap), jnp.exp2(jnp.minimum(last_gap, 0.0))], axis=1
+            )
+            decay_a = jnp.exp2(jnp.minimum(first_gap, 0.0))
+            acc_low = acc_low + nn((gram[low, low] * decay_a).astype(bf16), part[low])
+            acc_high = acc_high + nn((gram[high, :] * decay_b).astype(bf16), part)
+        pieces.append(jnp.concatenate([acc_low, acc_high], axis=0))
     out = jnp.concatenate(pieces, axis=1)
     out_o[...] = out
     zf = nn(normed[...], wz_out[:, :inner])
@@ -293,9 +308,9 @@
 
 def scan_kernel(
     rows, info, vbc, gb, gc, step, cum, pre, a_sum, st, gs_in, outg, sx, sb, jx, jb, par,
-    e_step, e_w, e8, f_one, f_two, f_three, tril,
+    e_step, e_w, e8, f_all, tril,
     gcat_o, tail_o, head_o, misc_o, dt_o,
-    run, ext, gram, acc,
+    run, ext, gram, acc, prod,
 ):
     step_id = pl.program_id(0)
     blocks = pl.num_programs(0)
@@ -310,7 +325,7 @@
     @pl.when(step_id == 0)
     def _():
         run[...] = outg[...].astype(f32)
-        ext[STRETCH : STRETCH + 8, :] = jnp.zeros((8, width), f32)
+        ext[...] = jnp.zeros((8, width), f32)
         misc_o[...] = jnp.zeros_like(misc_o)
         dt_o[...] = jnp.zeros_like(dt_o)
 
@@ -330,95 +345,111 @@
     end_decay = jnp.exp(cum_e - cum_v) * jnp.where(where_s >= end_start, 1.0, 0.0).astype(f32)
     weight = end_decay * step_v
     cum2 = cum_v * LOG2E
-    cols, both = columns_of([cum2, step_v, weight])
-    step_x = nn(both, e_step[...])
-    w_x = nn(both, e_w[...])
+    ok_rows = [
+        jnp.where(joined_ok(where_s, d, starts), 1.0, 0.0).astype(f32)
+        for d in range(taps - 1, 0, -1)
+    ]
+    cols, both = columns_of([cum2, step_v, weight] + ok_rows)
     b = vbc[:, inner : inner + 128]
     c = vbc[:, inner + 128 : inner + 256]
-    s_at = iota((STRETCH, STRETCH), 0)
-    t_at = iota((STRETCH, STRETCH), 1)
-    mask = (s_at <= t_at) & (s_at + base >= row_first)
-    gram[...] = jnp.where(mask, nt(b, c), 0.0)
+    half = STRETCH // 2
+    low, high = slice(0, half), slice(half, STRETCH)
+    s_at = iota((half, STRETCH), 0)
+    t_at = iota((half, STRETCH), 1)
+    mask_a = (s_at <= t_at) & (s_at + base >= row_first)
+    mask_b = (s_at <= t_at)[:, low] & ((s_at + (base + half)) >= row_first)[:, high]
+    gram[low, :] = jnp.where(mask_a, nt(b[low], c), 0.0)
+    gram[high, low] = jnp.where(mask_b, nt(b[high], c[high]), 0.0)
     acc[...] = jnp.zeros_like(acc)
-    y = nn(b, low_after)
     lane = iota((STRETCH, 128), 1)
-    us = []
-    svs = []
-    for p in range(inner // 128):
-        at = slice(128 * p, 128 * (p + 1))
-        sv = (vbc[:, at].astype(f32) * step_x[:, at]).astype(bf16).astype(f32)
-        svs.append(sv)
-        g_pair = gb[:, at]
-        g_wide = g_pair.astype(f32)
-        u = jnp.zeros((STRETCH, 128), f32)
-        for j in range(2):
-            h = 2 * p + j
-            side = (lane < 64) if j == 0 else (lane >= 64)
-            gap = cum2[h : h + 1, :] - cols[:, h : h + 1]
-            decay = jnp.exp2(jnp.minimum(gap, 0.0))
-            m = (gram[...] * decay).astype(bf16)
-            u = u + nn(m, jnp.where(side, g_wide, 0.0).astype(bf16))
-            g_m = nt(jnp.where(side, sv, 0.0).astype(bf16), g_pair)
-            acc[...] += g_m * decay
-        us.append(u)
-    u = jnp.concatenate(us, axis=1)
-    g_gram = jnp.where(mask, acc[...], 0.0).astype(bf16)
-    v = vbc[:, :inner].astype(f32)
-    gf = gb[...].astype(f32)
-    wv = (v * w_x).astype(bf16)
-    ext[0:STRETCH, inner : inner + 128] = (nn(g_gram, c) + nt(wv, low_after)) * sb[:, :128]
-    ext[0:STRETCH, inner + 128 :] = (tn(g_gram, b) + nt(gc[...], state)) * sb[:, 128:]
-    gv = dskip * gf + step_x * u + w_x * y
-    h1, l1 = halves(v * u)
-    h2, l2 = halves(v * y)
-    h3, l3 = halves(jnp.concatenate(svs, axis=1) * u)
-    sums_c = (
-        nn(jnp.concatenate([h1, l1], axis=1), f_one[...])
-        + nn(jnp.concatenate([h2, l2], axis=1), f_two[...])
-        + nn(jnp.concatenate([h3, l3], axis=1), f_three[...])
-    )
-    sums_r = jnp.transpose(sums_c)
-    g_step0 = sums_r[0:HEAD_ROWS]
-    g_end = sums_r[HEAD_ROWS : 2 * HEAD_ROWS]
-    ends = g_end * weight
-    g_cum = a_sum[...] - sums_r[2 * HEAD_ROWS : 3 * HEAD_ROWS] - ends
-    end_add = jnp.sum(ends, axis=1, keepdims=True) + end_more
-    g_log = exact_rows(g_cum, tril[...]) + end_add
-    g_step = g_step0 + g_end * end_decay - g_log * rate
-    g_pre_dt = g_step * jax.nn.sigmoid(pre[...])
-    dt_o[0:HEAD_ROWS, :] += g_log * (-step_v * rate)
-    dt_o[HEAD_ROWS:, :] += g_pre_dt
-    pad = jnp.zeros((128 - HEAD_ROWS, STRETCH), f32)
-    gcat_o[:, width:] = jnp.transpose(jnp.concatenate([g_pre_dt, pad], axis=0)).astype(bf16)
-
-    ext[0:STRETCH, :inner] = gv * sx[...].astype(f32)
-    pos = base + iota((STRETCH, 128), 0)
     ok = [
-        jnp.where(joined_ok(pos, d, starts), 1.0, 0.0).astype(f32) for d in range(taps - 1, 0, -1)
+        jnp.broadcast_to(cols[:, 3 * HEAD_ROWS + k : 3 * HEAD_ROWS + k + 1], (STRETCH, 128))
+        for k in range(taps - 1)
     ]
-    for g in range(width // 128):
-        at = slice(128 * g, 128 * (g + 1))
-        if 128 * g < inner:
-            j_f = jx[:, at].astype(f32)
-        else:
-            j_f = jb[:, 128 * g - inner : 128 * (g + 1) - inner].astype(f32)
-        own = ext[0:STRETCH, at]
+
+    def convolve(at, own, j_f):
+        following = ext[:, at]
+        joint = jnp.concatenate([own, following], axis=0)
+        ext[:, at] = own[0:8]
         misc_o[taps : taps + 1, at] += jnp.sum(own, axis=0, keepdims=True)
         misc_o[taps - 1 : taps, at] += jnp.sum(own * j_f, axis=0, keepdims=True)
         total = own * cw[taps - 1 : taps, at]
         for k in range(taps - 1):
             d = taps - 1 - k
-            term = ext[d : d + STRETCH, at] * ok[k]
+            term = pltpu.roll(joint, STRETCH + 8 - d, axis=0)[:STRETCH] * ok[k]
             misc_o[k : k + 1, at] += jnp.sum(term * j_f, axis=0, keepdims=True)
             total = total + term * cw[k : k + 1, at]
         gcat_o[:, at] = total.astype(bf16)
-
-        @pl.when(step_id == 0)
-        def _():
-            tail_o[:, at] = total[STRETCH - 8 :]
-
-    head_o[...] = ext[0:8, :]
-    ext[STRETCH : STRETCH + 8, :] = ext[0:8, :]
+        tail_o[:, at] = jnp.where(step_id == 0, total[STRETCH - 8 :], tail_o[:, at])
+
+    g_b = jnp.zeros((STRETCH, 128), f32)
+    g_c = jnp.zeros((STRETCH, 128), f32)
+    for p in range(inner // 128):
+        at = slice(128 * p, 128 * (p + 1))
+        step_x = nn(both, e_step[:, at])
+        v = vbc[:, at].astype(f32)
+        sv = (v * step_x).astype(bf16)
+        g_pair = gb[:, at]
+        u_low = jnp.zeros((half, 128), f32)
+        u_high = jnp.zeros((half, 128), f32)
+        for j in range(2):
+            h = 2 * p + j
+            side = (lane < 64) if j == 0 else (lane >= 64)
+            g_side = jnp.where(side, g_pair, jnp.zeros_like(g_pair))
+            sv_side = jnp.where(side, sv, jnp.zeros_like(sv))
+            row = cum2[h : h + 1, :]
+            first_gap = row[:, low] - cols[low, h : h + 1]
+            cross_gap = row[:, high] - cols[low, h : h + 1]
+            last_gap = row[:, high] - cols[high, h : h + 1]
+            decay_a = jnp.concatenate(
+                [jnp.exp2(jnp.minimum(first_gap, 0.0)), jnp.exp2(cross_gap)], axis=1
+            )
+            decay_b = jnp.exp2(jnp.minimum(last_gap, 0.0))
+            u_low = u_low + nn((gram[low, :] * decay_a).astype(bf16), g_side)
+            u_high = u_high + nn((gram[high, low] * decay_b).astype(bf16), g_side[high])
+            acc[low, :] += nt(sv_side[low], g_pair) * decay_a
+            acc[high, low] += nt(sv_side[high], g_pair[high]) * decay_b
+        u = jnp.concatenate([u_low, u_high], axis=0)
+        w_x = nn(both, e_w[:, at])
+        y = nn(b, low_after[:, at])
+        h1, l1 = halves(sv.astype(f32) * u)
+        prod[:, at] = h1
+        prod[:, inner + 128 * p : inner + 128 * (p + 1)] = l1
+        prod[:, 2 * inner + 128 * p : 2 * inner + 128 * (p + 1)] = (v * y).astype(bf16)
+        g_b = g_b + nt((v * w_x).astype(bf16), low_after[:, at])
+        g_c = g_c + nt(gc[:, at], state[:, at])
+        gv = dskip[:, at] * g_pair.astype(f32) + step_x * u + w_x * y
+        convolve(at, gv * sx[:, at].astype(f32), jx[:, at].astype(f32))
+
+    gg_a = jnp.where(mask_a, acc[low, :], 0.0).astype(bf16)
+    gg_b = jnp.where(mask_b, acc[high, low], 0.0).astype(bf16)
+    g_b = g_b + jnp.concatenate([nn(gg_a, c), nn(gg_b, c[high])], axis=0)
+    g_c = g_c + tn(gg_a, b[low])
+    g_c = g_c + jnp.concatenate([jnp.zeros((half, 128), f32), tn(gg_b, b[high])], axis=0)
+    for k, part in enumerate((g_b, g_c)):
+        here = slice(128 * k, 128 * (k + 1))
+        convolve(
+            slice(inner + 128 * k, inner + 128 * (k + 1)),
+            part * sb[:, here],
+            jb[:, here].astype(f32),
+        )
+
+    sums_r = jnp.transpose(nn(prod[...], f_all[...]))
+    g_mixed = sums_r[0:HEAD_ROWS]
+    g_end = sums_r[HEAD_ROWS : 2 * HEAD_ROWS]
+    ends = g_end * weight
+    g_cum = a_sum[...] - g_mixed - ends
+    end_add = jnp.sum(ends, axis=1, keepdims=True) + end_more
+    g_log = exact_rows(g_cum, tril[...]) + end_add
+    slope_dt = jax.nn.sigmoid(pre[...])
+    ratio = jnp.where(step_v > 0.0, slope_dt / step_v, 1.0)
+    g_pre_dt = (g_end * end_decay - g_log * rate) * slope_dt + g_mixed * ratio
+    dt_o[0:HEAD_ROWS, :] += g_log * (-step_v * rate)
+    dt_o[HEAD_ROWS:, :] += g_pre_dt
+    pad = jnp.zeros((128 - HEAD_ROWS, STRETCH), f32)
+    gcat_o[:, width:] = jnp.transpose(jnp.concatenate([g_pre_dt, pad], axis=0)).astype(bf16)
+
+    head_o[...] = ext[...]
 
 
 def exit_kernel(
@@ -987,6 +1018,7 @@
         ],
         [pltpu.VMEM((states, inner), f32)],
     )
+    sum_all = jnp.concatenate([gather(0), gather(1)[:inner]], axis=0)
     outgoing = entering(decay, start_state, "ctx", True)
     g_cat, tail, head, misc_scan, misc_dt = call(
         functools.partial(scan_kernel, rows),
@@ -997,8 +1029,7 @@
             by_block(state_in, True), by_block(gs_part, True), whole(outgoing),
             by_rows(slope_x, True), by_rows(slope_bc, True), by_rows(joined_x, True),
             by_rows(joined_bc, True), whole(params), whole(spread(1)),
-            whole(spread(2)), whole(e8), whole(gather(0)), whole(gather(1)),
-            whole(gather(2)), whole(lower),
+            whole(spread(2)), whole(e8), whole(sum_all), whole(lower),
         ],
         [
             by_rows(shape((rows, width + 128), bf16), True),
@@ -1009,9 +1040,10 @@
         ],
         [
             pltpu.VMEM((states, inner), f32),
-            pltpu.VMEM((STRETCH + 8, width), f32),
+            pltpu.VMEM((8, width), f32),
             pltpu.VMEM((STRETCH, STRETCH), f32),
             pltpu.VMEM((STRETCH, STRETCH), f32),
+            pltpu.VMEM((STRETCH, 3 * inner), bf16),
         ],
     )
     next_rows = passed_along(head, "ctx", -1)

time: 278 us -> 267 us (0.960)
  Pallas kernels: 195 us -> 183 us
    pallas_call x6, Pallas kernels: 133 us -> 120 us  [call(): pl.pallas_call(body, grid=(blocks,), in_specs=[spec(shape, how) for _a, s...]
  transfers between devices with their start and end apart: 6 -> 6, of which waited for: 4 -> 4; matrix products, arithmetic and copies ran while one was open for 9% -> 9% of each run, Pallas kernels for 58% -> 56%
where the time goes in v4:
time: 267 us; the launch traced here: 265 us
  Pallas kernels  183 us (69%)
  waiting for transfers between devices  29.6 us (11%)
  local copies, waits for them, and re-layouts  14.6 us (5%)
  matrix products  14.2 us (5%)
  between operations  14.1 us (5%)
  starting transfers between devices  5.16 us (2%)
  other arithmetic  4.29 us (2%)
    pallas_call x6, Pallas kernels, call(): pl.pallas_call(body, grid=(blocks,), in_specs=[spec(shape, how) for _a, s...  120 us
    pallas_call x1, Pallas kernels, reduced(): pl.pallas_call(functools.partial(reduce_kernel, n, m, bc_cols, inner), ou...  39.6 us
    reduce_scatter x1, waiting for transfers between devices, local(): g_resid = lax.psum_scatter(g_resid, 'tp', scatter_dimension=0, tiled=True)  25.7 us
    pallas_call x1, Pallas kernels, gathered(): pl.pallas_call(functools.partial(gather_kernel, n, lax.axis_size('ctx')),...  14.7 us
    dot_general x4, matrix products, tn(): lax.dot_general(left, right, (((0,), (0,)), ((), ())), preferred_element_...  14.2 us
    pallas_call x1, Pallas kernels, total_over_tp(): pl.pallas_call(functools.partial(total_kernel, n), out_shape=jax.ShapeDty...  8.6 us
    unnamed x48, local copies, waits for them, and re-layouts  6.53 us
  transfers between devices with their start and end apart: 6, of which 4 were waited for; matrix products, arithmetic and copies ran while one was open for 9% of the time, Pallas kernels for 56%

profile of v4, /device:TPU:0, one launch (start us, length us, event | category | flops | bytes accessed | tf_op | source)
XLA Modules:
  0.0 265.0 jit_solution(17455252200795155099)
XLA Ops:
  7.2 0.8 copy.45
  8.1 0.6 pad.28.dt
  8.7 1.7 pad_maximum_fusion
  10.5 14.7 %shard_map.396 = (bf16[768,768]{1,0:T(8,128)(2,1)}, bf16[16,768]{1,0:T(8,128)(2,1)}) custom-call(bf16[192,384]{1,0:T(8,128)(2,1)} %x.15, bf16[192,256]{1,0:T(8,128)(2,1)} %bc.1, bf16[192,128]{1,0:T(8,128)(2,1)} %pad.28.dt, bf16[3072,768]{1,0:T(8,128)(2,1)} %refs_1_.3), custom_call_target="tpu_custom_call" | custom-call | tf_op jit(solution)/shard_map/pallas_call | solution.py:614
  25.7 1.2 concatenate.16.refs_3_.refs_9_.refs_8_.refs_15_.refs_6_
  27.0 24.0 %shard_map.397 = (bf16[3072,768]{1,0:T(8,128)(2,1)}, bf16[3072,384]{1,0:T(8,128)(2,1)}, bf16[3072,256]{1,0:T(8,128)(2,1)}, bf16[3072,640]{1,0:T(8,128)(2,1)}, bf...) custom-call(s32[1,4]{1,0:T(1,128)} %refs_0_.9, ...), custom_call_target="tpu_custom_call" | custom-call | tf_op jit(solution)/shard_map/pallas_call | solution.py:874
  50.9 2.3 collective-permute-start
  53.2 1.1 collective-permute-done.refs_5_
  55.0 21.3 %shard_map.398 = (f32[3072,384]{1,0:T(8,128)}, f32[3072,384]{1,0:T(8,128)}, f32[3072,384]{1,0:T(8,128)}, f32[2,3072]{1,0:T(2,128)}, bf16[12,128,384]{2,1,0:T(8,128)(2,1)}, /*index=5*/bf16[768,3072]{1,0:T(8,128)(2,1)}) custom-call(s32[1,4]{1,0:T(1,128)} %refs_0_.9, bf16[3072,640]{1,0:T(8,128)(2,1)} %get-tuple-element.62.refs_1_.refs_6_, ...), custom_call_target="tpu_custom_call" | custom-call | tf_op jit(solution)/shard_map/pallas_call | solution.py:874
  76.4 0.7 slice.50
  77.1 0.7 slice.49
  77.8 8.6 %shard_map.399.refs_3_.refs_1_ = f32[2,3072]{1,0:T(2,128)} custom-call(f32[2,3072]{1,0:T(2,128)} %get-tuple-element.70.part), custom_call_target="tpu_custom_call" | custom-call | tf_op jit(solution)/shard_map/pallas_call | solution.py:649
  86.4 17.4 %shard_map.401 = (bf16[3072,384]{1,0:T(8,128)(2,1)}, bf16[3072,384]{1,0:T(8,128)(2,1)}, bf16[3072,384]{1,0:T(8,128)(2,1)}, bf16[3072,384]{1,0:T(8,128)(2,1)}, f3...) custom-call(s32[1,4]{1,0:T(1,128)} %refs_0_.9, ...), custom_call_target="tpu_custom_call" | custom-call | tf_op jit(solution)/shard_map/pallas_call | solution.py:874
  103.8 1.3 collective-permute-start.1
  105.7 1.5 collective-permute-done.1.refs_10_
  107.8 32.5 %shard_map.402 = (bf16[3072,768]{1,0:T(8,128)(2,1)}, f32[8,640]{1,0:T(8,128)}, f32[8,640]{1,0:T(8,128)}, f32[8,640]{1,0:T(8,128)}, f32[16,256]{1,0:T(8,128)}) custom-call(s32[1,4]{1,0:T(1,128)} %refs_0_.9, bf16[3072,640]{1,0:T(8,128)(2,1)} %get-tuple-element.62.refs_1_.refs_6_, bf16[3072,384]{1,0:T(8,128)(2,1)} %get-tuple-element.76.refs_2_, ...), custom_call_target="tpu_custom_call" | custom-call | tf_op jit(solution)/shard_map/pallas_call | solution.py:874
  140.3 1.5 collective-permute-start.2
  142.4 1.2 collective-permute-done.2.refs_10_
  144.2 19.4 %shard_map.403 = (bf16[768,3072]{1,0:T(8,128)(2,1)}, f32[1,768]{1,0:T(1,128)}, bf16[16,640]{1,0:T(8,128)(2,1)}, f32[8,640]{1,0:T(8,128)}) custom-call(s32[1,4]{1,0:T(1,128)} %refs_0_.9, bf16[3072,768]{1,0:T(8,128)(2,1)} %refs_1_.3, bf16[3072,768]{1,0:T(8,128)(2,1)} %refs_2_.3, f32[1,768]{1,0:T(1,128)} %compare_convert_fusion.refs_3_, ...), custom_call_target="tpu_custom_call" | custom-call | tf_op jit(solution)/shard_map/pallas_call | solution.py:874
  163.6 1.6 copy-done.19
  165.2 4.7 %convolution_bitcast_fusion.p_out = f32[768,384]{1,0:T(8,128)S(1)} fusion(bf16[3072,384]{1,0:T(8,128)(2,1)S(1)} %copy-done.19, bf16[3072,768]{1,0:T(8,128)(2,1)} %refs_2_.3), kind=kOutput, calls=%fused_computation.1 | convolution fusion | flops 1811939328 | bytes 8257536 | tf_op jit(solution)/shard_map/dot_general | solution.py:31
  170.0 2.6 fusion.2.p_z
  173.1 6.4 %pad_add_fusion.p_cat = f32[768,768]{1,0:T(8,128)S(1)} fusion(f32[768,640]{1,0:T(8,128)S(1)} %fusion, bf16[3072,768]{1,0:T(8,128)(2,1)S(1)} %bitcast.21, bf16[3072,768]{1,0:T(8,128)(2,1)} %get-tuple-element.86.refs_5_), kind=kOutput, calls=%fused_computation | convolution fusion | flops 3624468480 | bytes 13762560 | tf_op jit(solution)/shard_map/dot_general | solution.py:31
  179.6 39.6 %shard_map.404 = (f32[192,384]{1,0:T(8,128)S(1)}, f32[192,384]{1,0:T(8,128)S(1)}, f32[192,768]{1,0:T(8,128)S(1)}, f32[8,1536]{1,0:T(8,128)S(1)}, f32[8,1024]{1,0:T(8,128)S(1)}) custom-call(f32[768,384]{1,0:T(8,128)S(1)} %convolution_bitcast_fusion.p_out, f32[768,384]{1,0:T(8,128)S(1)} %fusion.2.p_z, f32[768,768]{1,0:T(8,128)S(1)} %pad_add_fusion.p_cat, ...), custom_call_target="tpu_custom_call" | custom-call | tf_op jit(solution)/shard_map/pallas_call | solution.py:795
  219.2 0.7 slice.53
  220.0 0.7 slice.54
  221.8 0.7 copy.50
  225.0 0.7 slice_reduce_fusion
  225.7 5.7 %shard_map.400 = bf16[192,3072]{1,0:T(8,128)(2,1)} custom-call(s32[1]{0:T(128)} %bitcast.refs_0_, bf16[192,3072]{1,0:T(8,128)(2,1)} %reduce-scatter.3.cloned.1.call-done.refs_1_, bf16[3072,768]{1,0:T(8,128)(2,1)} %refs_1_.3, f32[2,3072]{1,0:T(2,128)} %shard_map.399.refs_3_.refs_1_), custom_call_target="tpu_custom_call" | custom-call | tf_op jit(solution)/shard_map/pallas_call | solution.py:874
  231.4 25.7 %reduce-scatter.5.cloned.1.call-done = bf16[192,3072]{1,0:T(8,128)(2,1)} async-done(((bf16[768,3072]{1,0:T(8,128)(2,1)}), bf16[192,3072]{1,0:T(8,128)(2,1)}) %reduce-scatter.5.cloned.1.call-update) | async-done | bytes 1179664 | tf_op jit(solution)/shard_map/reduce_scatter | solution.py:1085
  257.1 0.7 copy.54
  257.8 0.7 copy.55
  (75 shorter events, 7.9 us)
Async XLA Ops:
  7.2 47.2 %all-gather.2.cloned.1.call-start = ((), (), s32[]{:S(2)}) async-start(), calls=%async_computation.2 | async-start | bytes 1474560 | tf_op jit(solution)/shard_map/all_gather | solution.py:909
  10.4 14.8 %copy-start.11 = (f32[768]{0:T(1024)S(1)}, f32[768]{0:T(1024)}, u32[]{:S(2)}) copy-start(f32[768]{0:T(1024)} %param.32) | copy-start | bytes 9220
  10.4 14.8 %copy-start.13 = (f32[384]{0:T(512)S(1)}, f32[384]{0:T(512)}, u32[]{:S(2)}) copy-start(f32[384]{0:T(512)} %param.38) | copy-start | bytes 4612
  10.4 14.8 %copy-start.15 = (f32[256]{0:T(256)S(1)}, f32[256]{0:T(256)}, u32[]{:S(2)}) copy-start(f32[256]{0:T(256)} %param.40) | copy-start | bytes 3076
  10.4 14.9 %copy-start.14 = (f32[384]{0:T(512)S(1)}, f32[384]{0:T(512)}, u32[]{:S(2)}) copy-start(f32[384]{0:T(512)} %param.44) | copy-start | bytes 4612
  10.4 14.9 %copy-start.16 = (f32[6]{0:T(128)S(1)}, f32[6]{0:T(128)}, u32[]{:S(2)}) copy-start(f32[6]{0:T(128)} %param.43) | copy-start | bytes 76
  10.4 15.0 %copy-start.17 = (f32[6]{0:T(128)S(1)}, f32[6]{0:T(128)}, u32[]{:S(2)}) copy-start(f32[6]{0:T(128)} %param.42) | copy-start | bytes 76
  10.5 15.1 %copy-start.18 = (f32[6]{0:T(128)S(1)}, f32[6]{0:T(128)}, u32[]{:S(2)}) copy-start(f32[6]{0:T(128)} %param.41) | copy-start | bytes 76
  10.5 15.2 %copy-start.10 = (f32[4,384]{1,0:T(4,128)S(1)}, f32[4,384]{1,0:T(4,128)}, u32[]{:S(2)}) copy-start(f32[4,384]{1,0:T(4,128)} %param.37) | copy-start | bytes 18436
  10.5 15.2 %copy-start.12 = (f32[4,256]{1,0:T(4,128)S(1)}, f32[4,256]{1,0:T(4,128)}, u32[]{:S(2)}) copy-start(f32[4,256]{1,0:T(4,128)} %param.39) | copy-start | bytes 12292
  25.2 200.5 %reduce-scatter.3.cloned.1.call-start = ((), (), s32[]{:S(2)}) async-start(), calls=%async_computation.3 | async-start | bytes 5898240 | tf_op jit(solution)/shard_map/reduce_scatter | solution.py:999
  50.9 3.4 %collective-permute-start = (bf16[128,384]{1,0:T(8,128)(2,1)}, bf16[128,384]{1,0:T(8,128)(2,1)S(1)}, u32[]{:S(2)}, u32[]{:S(2)}) collective-permute-start(bf16[128,384]{1,0:T(8,128)(2,1)} %get-tuple-element.66), channel_id=1, source_target_pairs={{0,4},{1,5},{2,6},{3,7},{8,12},{9,13},{10,14},{11,15},{16,20},{17,... | collective-permute-start | bytes 294920 | tf_op jit(solution)/shard_map/ppermute | solution.py:845
  54.3 0.6 copy-start.7
  76.3 180.8 %reduce-scatter.5.cloned.1.call-start = ((), (), s32[]{:S(2)}) async-start(), calls=%async_computation.4 | async-start | bytes 5898240 | tf_op jit(solution)/shard_map/reduce_scatter | solution.py:1085
  103.8 3.4 %collective-permute-start.1 = (bf16[128,384]{1,0:T(8,128)(2,1)}, bf16[128,384]{1,0:T(8,128)(2,1)S(1)}, u32[]{:S(2)}, u32[]{:S(2)}) collective-permute-start(bf16[128,384]{1,0:T(8,128)(2,1)} %get-tuple-element.81), channel_id=1, source_target_pairs={{4,0},{5,1},{6,2},{7,3},{12,8},{13,9},{14,10},{15,11},{20,16},{21,... | collective-permute-start | bytes 294920 | tf_op jit(solution)/shard_map/ppermute | solution.py:845
  107.2 0.6 copy-start.6
  140.3 3.3 %collective-permute-start.2 = (f32[8,640]{1,0:T(8,128)}, f32[8,640]{1,0:T(8,128)S(1)}, u32[]{:S(2)}, u32[]{:S(2)}) collective-permute-start(f32[8,640]{1,0:T(8,128)} %get-tuple-element.88), channel_id=1, source_target_pairs={{4,0},{5,1},{6,2},{7,3},{12,8},{13,9},{14,10},{15,11},{20,16},{21,... | collective-permute-start | bytes 61448 | tf_op jit(solution)/shard_map/ppermute | solution.py:845
  143.6 0.6 copy-start.9
  163.5 1.7 copy-start.19
  163.6 6.4 %slice-start = ((s8[4718592]{0:T(1024)(128)(4,1)}), s8[524288]{0:T(1024)(128)(4,1)S(1)}, s32[]{:S(2)}) async-start(s8[4718592]{0:T(1024)(128)(4,1)} %bitcast.20), calls=%async_computation.5 | async-start | bytes 1048576
  165.2 4.7 %slice-start.1 = ((s8[4718592]{0:T(1024)(128)(4,1)}), s8[4194304]{0:T(1024)(128)(4,1)S(1)}, s32[]{:S(2)}) async-start(s8[4718592]{0:T(1024)(128)(4,1)} %bitcast.20), calls=%async_computation.6 | async-start | bytes 8388608
  165.2 4.7 %copy-start.5 = (bf16[3072,384]{1,0:T(8,128)(2,1)S(1)}, bf16[3072,384]{1,0:T(8,128)(2,1)}, u32[]{:S(2)}) copy-start(bf16[3072,384]{1,0:T(8,128)(2,1)} %get-tuple-element.75.refs_4_) | copy-start | bytes 7077892
  170.0 2.6 copy-start.8
  173.1 6.5 %copy-start = (f32[8,640]{1,0:T(8,128)S(1)}, f32[8,640]{1,0:T(8,128)}, u32[]{:S(2)}) copy-start(f32[8,640]{1,0:T(8,128)} %get-tuple-element.92.m_scan) | copy-start | bytes 61444
  173.1 6.5 %copy-start.1 = (f32[8,640]{1,0:T(8,128)S(1)}, f32[8,640]{1,0:T(8,128)}, u32[]{:S(2)}) copy-start(f32[8,640]{1,0:T(8,128)} %get-tuple-element.93.m_rim) | copy-start | bytes 61444
  173.1 6.5 %copy-start.2 = (f32[16,256]{1,0:T(8,128)S(1)}, f32[16,256]{1,0:T(8,128)}, u32[]{:S(2)}) copy-start(f32[16,256]{1,0:T(8,128)} %get-tuple-element.95.m_dt) | copy-start | bytes 49156
  173.1 6.5 %copy-start.3 = (f32[8,384]{1,0:T(8,128)S(1)}, f32[8,384]{1,0:T(8,128)}, u32[]{:S(2)}) copy-start(f32[8,384]{1,0:T(8,128)} %get-tuple-element.94.m_gate) | copy-start | bytes 36868
  173.1 6.5 %copy-start.4 = (f32[1,768]{1,0:T(1,128)S(1)}, f32[1,768]{1,0:T(1,128)}, u32[]{:S(2)}) copy-start(f32[1,768]{1,0:T(1,128)} %get-tuple-element.96.m_gain) | copy-start | bytes 9220
Sparse Core Ops, SparseCore 0:
  25.3 28.5 all-gather.1
  76.4 86.2 reduce-scatter.2
  165.6 91.4 reduce-scatter.4

commit v5 on v4

--- a/solution.py
+++ b/solution.py
@@ -97,12 +97,60 @@
     return jnp.sum(column * e8, axis=0, keepdims=True)
 
 
+MESH = pl.DeviceIdType.MESH
+
+
+def start_together(peers):
+    barrier = pltpu.get_barrier_semaphore()
+    for peer in peers:
+        pl.semaphore_signal(barrier, inc=1, device_id=peer, device_id_type=MESH)
+    pl.semaphore_wait(barrier, len(peers))
+
+
+def remote(src, dst, sent, came, peer):
+    return pltpu.make_async_remote_copy(
+        src_ref=src, dst_ref=dst, send_sem=sent, recv_sem=came, device_id=peer, device_id_type=MESH
+    )
+
+
+def turned(index, distance, size):
+    return lax.rem(index + distance + size, size)
+
+
+def twin_of(index):
+    parity = lax.rem(index, 2)
+    return parity, index + 1 - 2 * parity
+
+
 def entry_kernel(
-    rows, info, tok, halo, par, wj, tri, ew, e8,
-    nrm_o, jx_o, jb_o, vbc_o, sx_o, sb_o, pre_o, step_o, cum_o, s_o, end_o, dec_o,
-    ext, run, dec,
+    rows, n, chain, info, nrm, halo, par, wj, tri, ew, e8, w_z, w_out_t,
+    jx_o, jb_o, vbc_o, sx_o, sb_o, pre_o, step_o, cum_o, s_o, end_o, dec_o, inc_o, wz_o,
+    ext, run, dec, got, sent, came, own, hop,
 ):
     i = pl.program_id(0)
+    f = lax.axis_index("fsdp")
+    here = lax.axis_index("ctx")
+    _parity, twin = twin_of(here)
+    peers = [{"fsdp": turned(f, d, n)} for d in range(1, n)] + [{"ctx": twin}]
+    barrier = pltpu.get_barrier_semaphore()
+    slab = w_z.shape[0]
+
+    @pl.when(i == 0)
+    def _():
+        for peer in peers:
+            pl.semaphore_signal(barrier, inc=1, device_id=peer, device_id_type=MESH)
+
+    def weight_copies():
+        at = pl.ds(pl.multiple_of(f * slab, 16), slab)
+        for p, ref in enumerate((w_z, w_out_t)):
+            cols = slice(p * ref.shape[1], (p + 1) * ref.shape[1])
+            target = wz_o.at[at, cols]
+            yield pltpu.make_async_copy(ref, target, own.at[p])
+            for d in range(1, n):
+                yield remote(
+                    ref, target, sent.at[d - 1, p], came.at[d - 1, p], {"fsdp": turned(f, d, n)}
+                )
+
     starts, base, end_start, flag = read_info(rows, info, i)
     inner = jx_o.shape[1]
     width = inner + jb_o.shape[1]
@@ -116,9 +164,7 @@
         run[...] = jnp.zeros_like(run)
         dec[...] = jnp.ones_like(dec)
 
-    unit, _inv = norm_rows(tok[...])
-    normed = (unit * gain).astype(bf16)
-    nrm_o[...] = normed
+    normed = nrm[...]
     product = nn(normed, wj[...])
     joined = product[:, :width].astype(bf16)
     jx_o[...] = joined[:, :inner]
@@ -166,6 +212,24 @@
     dec[...] = dec[...] * through
     end_o[...] = run[...].astype(bf16)
     dec_o[...] = dec[...]
+
+    @pl.when(i == 0)
+    def _():
+        pl.semaphore_wait(barrier, len(peers))
+        for copy in weight_copies():
+            copy.start()
+
+    @pl.when(i == pl.num_programs(0) - 1)
+    def _():
+        if chain == 2:
+            copy = remote(end_o, got, hop.at[0], hop.at[1], {"ctx": twin})
+            copy.start()
+            copy.wait()
+            inc_o[...] = jnp.where(here > 0, got[...], jnp.zeros_like(got))
+        else:
+            inc_o[...] = jnp.zeros_like(inc_o)
+        for copy in weight_copies():
+            copy.wait()
 
 
 def mix_kernel(
@@ -525,32 +589,9 @@
             out[...] = (wide + add).astype(bf16)
 
 
-MESH = pl.DeviceIdType.MESH
-
-
-def start_together(peers):
-    barrier = pltpu.get_barrier_semaphore()
-    for peer in peers:
-        pl.semaphore_signal(barrier, inc=1, device_id=peer, device_id_type=MESH)
-    pl.semaphore_wait(barrier, len(peers))
-
-
-def remote(src, dst, sent, came, peer):
-    return pltpu.make_async_remote_copy(
-        src_ref=src, dst_ref=dst, send_sem=sent, recv_sem=came, device_id=peer, device_id_type=MESH
-    )
-
-
-def turned(index, distance, size):
-    return lax.rem(index + distance + size, size)
-
-
-def twin_of(index):
-    parity = lax.rem(index, 2)
-    return parity, index + 1 - 2 * parity
-
-
-def gather_kernel(n, chain, x, bc, dt, tok, out, halo, sent, came, passed, relayed, own, hop):
+def gather_kernel(
+    n, chain, x, bc, dt, par, tok, out, halo, nrm, sent, came, passed, relayed, own, hop
+):
     f = lax.axis_index("fsdp")
     parity, twin = twin_of(lax.axis_index("ctx"))
     rows = x.shape[0]
@@ -590,13 +631,24 @@
         )
         copy.start()
         locals_.append(copy)
+    gain = par[...][None, :]
+
+    def norm_block(tok_block, nrm_block):
+        unit, _inverse = norm_rows(tok_block[...])
+        nrm_block[...] = (unit * gain).astype(bf16)
+
+    block = pl.BlockSpec((2 * STRETCH, tok.shape[1]), lambda i: (i, 0))
+    pltpu.emit_pipeline(
+        norm_block, grid=(tok.shape[0] // (2 * STRETCH),), in_specs=[block], out_specs=[block]
+    )(tok, nrm)
+
     relays = []
     for d in range(1, n):
         source = turned(f, -d, n)
         for p, (ref, cols) in enumerate(pieces):
             copies[(d - 1) * len(pieces) + p].wait_recv()
-            block = out.at[place(source, parity), cols]
-            copy = remote(block, block, passed.at[d - 1, p], relayed.at[d - 1, p], {"ctx": twin})
+            piece = out.at[place(source, parity), cols]
+            copy = remote(piece, piece, passed.at[d - 1, p], relayed.at[d - 1, p], {"ctx": twin})
             copy.start()
             relays.append(copy)
     for copy in copies:
@@ -607,7 +659,7 @@
         copy.wait()
 
 
-def gathered(x, bc, dt, tok):
+def gathered(x, bc, dt, par, tok):
     n = lax.axis_size("fsdp")
     pieces = (n - 1, 3)
     width = x.shape[1] + bc.shape[1] + dt.shape[1]
@@ -616,13 +668,15 @@
         out_shape=[
             jax.ShapeDtypeStruct((n * x.shape[0], width), bf16),
             jax.ShapeDtypeStruct((16, tok.shape[1]), bf16),
-        ],
-        in_specs=[pl.BlockSpec(memory_space=pltpu.VMEM)] * 3 + [pl.BlockSpec(memory_space=pl.ANY)],
-        out_specs=[pl.BlockSpec(memory_space=pltpu.VMEM)] * 2,
+            jax.ShapeDtypeStruct(tok.shape, bf16),
+        ],
+        in_specs=[pl.BlockSpec(memory_space=pltpu.VMEM)] * 4 + [pl.BlockSpec(memory_space=pl.ANY)],
+        out_specs=[pl.BlockSpec(memory_space=pltpu.VMEM)] * 2
+        + [pl.BlockSpec(memory_space=pl.ANY)],
         scratch_shapes=[pltpu.SemaphoreType.DMA(pieces)] * 4
         + [pltpu.SemaphoreType.DMA((3,)), pltpu.SemaphoreType.DMA((2,))],
         compiler_params=pltpu.CompilerParams(collective_id=1, has_side_effects=True),
-    )(x, bc, dt, tok)
+    )(x, bc, dt, par, tok)
 
 
 def total_kernel(n, part, out, slots, sent, came):
@@ -862,28 +916,72 @@
     return lax.fori_loop(0, size, lap, jnp.zeros(state.shape, f32)).astype(bf16)
 
 
-def call(kernel, blocks, ins, outs, scratch, kept=()):
+def fill_params(raw, par):
+    gain, gate, x_w, bc_w, x_b, bc_b, bias, rate, skip = raw
+    inner = x_w.shape[1]
+    width = inner + bc_w.shape[1]
+    heads = bias.shape[0]
+
+    @pl.when(pl.program_id(0) == 0)
+    def _():
+        par[0:1, :] = gain[...][None, :]
+        par[1:2, :inner] = x_b[...][None, :]
+        par[1:2, inner:width] = bc_b[...][None, :]
+        par[2:3, :inner] = gate[...][None, :]
+        par[4:8, :inner] = x_w[...]
+        par[4:8, inner:width] = bc_w[...]
+        row, lane = iota((HEAD_ROWS, 128), 0), iota((HEAD_ROWS, 128), 1)
+        table = jnp.zeros((HEAD_ROWS, 128), f32)
+        for h in range(heads):
+            for k, ref in enumerate((bias, rate, skip)):
+                table = jnp.where((row == h) & (lane == k), ref[h], table)
+        par[8:16, 0:128] = table
+
+
+def call(kernel, blocks, ins, outs, scratch, remote_id=None, raw=None):
     def spec(shape, how):
         if how == "smem":
             return pl.BlockSpec(memory_space=pltpu.SMEM)
+        if how == "any":
+            return pl.BlockSpec(memory_space=pl.ANY)
         return pl.BlockSpec(shape, how)
 
-    def body(*refs):
-        kernel(*refs[: len(ins)], *refs[len(ins) + len(kept) :])
+    places = [k for k, (_a, _s, how) in enumerate(ins) if how == "par"]
+    ins = [entry for entry in ins if entry[2] != "par"]
+    body = kernel
+    if places:
+        count = len(raw)
+        model = raw[0].shape[0]
+        scratch = list(scratch) + [pltpu.VMEM((16, model), f32)]
+
+        def body(*refs):
+            par = refs[-1]
+            fill_params(refs[:count], par)
+            rest = list(refs[count:-1])
+            rest.insert(places[0], par)
+            kernel(*rest)
+
+        def fixed_at(x):
+            if x.ndim == 1 and x.shape[0] < 128:
+                return (x, None, "smem")
+            return (x, x.shape, lambda i: (0,) * x.ndim)
+
+        ins = [fixed_at(x) for x in raw] + ins
 
     return pl.pallas_call(
         body,
         grid=(blocks,),
-        in_specs=[spec(shape, how) for _a, shape, how in ins]
-        + [pl.BlockSpec(memory_space=pl.ANY)] * len(kept),
+        in_specs=[spec(shape, how) for _a, shape, how in ins],
         out_specs=[spec(shape, how) for _s, shape, how in outs],
         out_shape=[s for s, _sh, _h in outs],
         scratch_shapes=scratch,
-        input_output_aliases={len(ins) + k: k for k in range(len(kept))},
         compiler_params=pltpu.CompilerParams(
-            dimension_semantics=("arbitrary",), vmem_limit_bytes=56 * 1024 * 1024
+            dimension_semantics=("arbitrary",),
+            vmem_limit_bytes=56 * 1024 * 1024,
+            collective_id=remote_id,
+            has_side_effects=remote_id is not None,
         ),
-    )(*[a for a, _s, _h in ins], *kept)
+    )(*[a for a, _s, _h in ins])
 
 
 def local(
@@ -903,26 +1001,13 @@
     ctx_index = lax.axis_index("ctx")
     e8, spread, gather, upper, lower = constants(inner, heads)
 
-    w_joined, halo = gathered(w_x, w_bc, jnp.pad(w_dt, ((0, 0), (0, 128 - heads))), tokens)
-    second = jnp.concatenate([w_z, w_out.T], axis=1)
-    second, w_joined = lax.optimization_barrier((second, w_joined))
-    wz_out = lax.all_gather(second, "fsdp", axis=0, tiled=True)
     per_head = inner // heads
 
-    def line(*vectors):
-        joint = jnp.concatenate(vectors) if len(vectors) > 1 else vectors[0]
-        return jnp.pad(joint, (0, model - joint.shape[0]))[None, :]
-
-    per_heads = jnp.stack([dt_bias, a_log, d_skip], axis=1)
-    params = jnp.concatenate(
-        [
-            line(norm_gain), line(conv_x_b, conv_bc_b), line(gate_gain), jnp.zeros((1, model), f32),
-            jnp.pad(conv_x_w, ((0, 0), (0, model - inner)))
-            + jnp.pad(conv_bc_w, ((0, 0), (inner, model - width))),
-            jnp.pad(per_heads, ((0, HEAD_ROWS - heads), (0, model - 3))),
-        ],
-        axis=0,
-    )
+    w_joined, halo, normed = gathered(
+        w_x, w_bc, jnp.pad(w_dt, ((0, 0), (0, 128 - heads))), norm_gain, tokens
+    )
+    n = lax.axis_size("fsdp")
+    chain = lax.axis_size("ctx")
 
     def shape(dims, kind):
         return jax.ShapeDtypeStruct(dims, kind)
@@ -949,16 +1034,24 @@
         return (x, x.shape, lambda i: (0,) * len(x.shape))
 
     info_in = (lengths, None, "smem")
+    params_in = (None, None, "par")
+    raw = (
+        norm_gain, gate_gain, conv_x_w, conv_bc_w, conv_x_b, conv_bc_b, dt_bias, a_log, d_skip
+    )
+    run = functools.partial(call, raw=raw)
     state_dims = (blocks, states, inner)
-    normed, joined_x, joined_bc, vbc, slope_x, slope_bc, pre, step, cum, s_part, end_state, decay = call(
-        functools.partial(entry_kernel, rows),
+    dma = pltpu.SemaphoreType.DMA
+    (
+        joined_x, joined_bc, vbc, slope_x, slope_bc, pre, step, cum, s_part, end_state, decay,
+        incoming, wz_out,
+    ) = run(
+        functools.partial(entry_kernel, rows, n, chain),
         blocks,
         [
-            info_in, by_rows(tokens), whole(halo), whole(params), whole(w_joined), whole(upper),
-            whole(spread(0)), whole(e8),
+            info_in, by_rows(normed), whole(halo), params_in, whole(w_joined), whole(upper),
+            whole(spread(0)), whole(e8), (w_z, None, "any"), (w_out.T, None, "any"),
         ],
         [
-            by_rows(shape((rows, model), bf16)),
             by_rows(shape((rows, inner), bf16)),
             by_rows(shape((rows, 2 * states), bf16)),
             by_rows(shape((rows, width), bf16)),
@@ -970,20 +1063,29 @@
             by_block(shape(state_dims, f32)),
             fixed(shape((states, inner), bf16)),
             fixed(shape((1, inner), f32)),
+            fixed(shape((states, inner), bf16)),
+            (shape((model, 2 * inner), bf16), None, "any"),
         ],
         [
             pltpu.VMEM((STRETCH + 8, width), f32),
             pltpu.VMEM((states, inner), f32),
             pltpu.VMEM((1, inner), f32),
-        ],
-    )
-    incoming = entering(decay, end_state, "ctx", False)
-    z_part, out, gn, sums, state_in, branch = call(
+            pltpu.VMEM((states, inner), bf16),
+            dma((n - 1, 2)),
+            dma((n - 1, 2)),
+            dma((2,)),
+            dma((2,)),
+        ],
+        remote_id=4,
+    )
+    if chain > 2:
+        incoming = entering(decay, end_state, "ctx", False)
+    z_part, out, gn, sums, state_in, branch = run(
         functools.partial(mix_kernel, rows),
         blocks,
         [
             info_in, by_rows(vbc), by_lanes(step), by_lanes(cum), by_block(s_part),
-            whole(incoming), by_rows(normed), by_rows(grad_out), whole(wz_out), whole(params),
+            whole(incoming), by_rows(normed), by_rows(grad_out), whole(wz_out), params_in,
             whole(spread(1)), whole(spread(2)), whole(e8),
         ],
         [
@@ -998,13 +1100,13 @@
     )
     branch = lax.psum_scatter(branch, "tp", scatter_dimension=0, tiled=True)
     sums = total_over_tp(sums)
-    g_z, g_b, g_c, normed_two, a_sum, gs_part, start_state, misc_gate = call(
+    g_z, g_b, g_c, normed_two, a_sum, gs_part, start_state, misc_gate = run(
         functools.partial(gate_kernel, rows),
         blocks,
         [
             info_in, by_lanes(sums, True), by_lanes(cum, True), by_rows(out, True),
             by_rows(z_part, True), by_rows(gn, True), by_rows(vbc, True), by_block(state_in, True),
-            whole(params), whole(spread(2)), whole(e8), whole(gather(0)),
+            params_in, whole(spread(2)), whole(e8), whole(gather(0)),
         ],
         [
             by_rows(shape((rows, inner), bf16), True),
@@ -1020,7 +1122,7 @@
     )
     sum_all = jnp.concatenate([gather(0), gather(1)[:inner]], axis=0)
     outgoing = entering(decay, start_state, "ctx", True)
-    g_cat, tail, head, misc_scan, misc_dt = call(
+    g_cat, tail, head, misc_scan, misc_dt = run(
         functools.partial(scan_kernel, rows),
         blocks,
         [
@@ -1028,7 +1130,7 @@
             by_lanes(step, True), by_lanes(cum, True), by_lanes(pre, True), by_lanes(a_sum, True),
             by_block(state_in, True), by_block(gs_part, True), whole(outgoing),
             by_rows(slope_x, True), by_rows(slope_bc, True), by_rows(joined_x, True),
-            by_rows(joined_bc, True), whole(params), whole(spread(1)),
+            by_rows(joined_bc, True), params_in, whole(spread(1)),
             whole(spread(2)), whole(e8), whole(sum_all), whole(lower),
         ],
         [
@@ -1056,12 +1158,12 @@
         def flipped(x):
             return (x, (STRETCH, x.shape[1]), lambda i: (top - 1 - i, 0))
 
-        return call(
+        return run(
             functools.partial(exit_kernel, rows, top, first),
             count,
             [
                 info_in, flipped(tokens), flipped(grad_out), whole(mine), flipped(g_z),
-                flipped(g_cat), whole(params), whole(wz_out), whole(w_joined),
+                flipped(g_cat), params_in, whole(wz_out), whole(w_joined),
             ]
             + extra_in,
             [
@@ -1117,7 +1219,7 @@
     place = tp_index.astype(jnp.int32)[None]
 
     wide = 2 * STRETCH
-    layer_out = call(
+    layer_out = run(
         functools.partial(finish_kernel, tp_size),
         blocks // 2,
         [

time: 267 us -> 260 us (0.974)
    unnamed x48 -> x28, local copies, waits for them, and re-layouts: 6.53 us -> 5.94 us
  transfers between devices with their start and end apart: 6 -> 4, of which waited for: 4 -> 3; matrix products, arithmetic and copies ran while one was open for 9% -> 9% of each run, Pallas kernels for 56% -> 47%
where the time goes in v5:
time: 260 us; the launch traced here: 258 us
  Pallas kernels  182 us (70%)
  waiting for transfers between devices  29.3 us (11%)
  matrix products  14.9 us (6%)
  between operations  14.3 us (6%)
  local copies, waits for them, and re-layouts  12.5 us (5%)
  starting transfers between devices  2.84 us (1%)
    pallas_call x6, Pallas kernels, call(): pl.pallas_call(body, grid=(blocks,), in_specs=[spec(shape, how) for _a, s...  121 us
    pallas_call x1, Pallas kernels, reduced(): pl.pallas_call(functools.partial(reduce_kernel, n, m, bc_cols, inner), ou...  38.1 us
    reduce_scatter x1, waiting for transfers between devices, local(): g_resid = lax.psum_scatter(g_resid, 'tp', scatter_dimension=0, tiled=True)  28 us
    dot_general x4, matrix products, tn(): lax.dot_general(left, right, (((0,), (0,)), ((), ())), preferred_element_...  14.9 us
    pallas_call x1, Pallas kernels, gathered(): pl.pallas_call(functools.partial(gather_kernel, n, lax.axis_size('ctx')),...  14.6 us
    pallas_call x1, Pallas kernels, total_over_tp(): pl.pallas_call(functools.partial(total_kernel, n), out_shape=jax.ShapeDty...  8.12 us
    unnamed x28, local copies, waits for them, and re-layouts  5.94 us
  transfers between devices with their start and end apart: 4, of which 3 were waited for; matrix products, arithmetic and copies ran while one was open for 9% of the time, Pallas kernels for 47%

profile of v5, /device:TPU:0, one launch (start us, length us, event | category | flops | bytes accessed | tf_op | source)
XLA Modules:
  0.0 258.5 jit_solution(17451959536074936350)
XLA Ops:
  7.2 0.8 copy.45
  8.1 0.6 pad.8.dt
  8.7 14.6 %shard_map.396 = (bf16[768,768]{1,0:T(8,128)(2,1)}, bf16[16,768]{1,0:T(8,128)(2,1)}, bf16[3072,768]{1,0:T(8,128)(2,1)}) custom-call(bf16[192,384]{1,0:T(8,128)(2,1)} %x.5, bf16[192,256]{1,0:T(8,128)(2,1)} %bc.1, bf16[192,128]{1,0:T(8,128)(2,1)} %pad.8.dt, f32[768]{0:T(1024)} %refs_0_.9, bf16[3072,768]{1,0:T(8,128)(2,1)} %refs_10_.1), custom_call_target="tpu_custom_call" | custom-call | tf_op jit(solution)/shard_map/pallas_call | solution.py:666
  23.3 24.8 %shard_map.397 = (bf16[3072,384]{1,0:T(8,128)(2,1)}, bf16[3072,256]{1,0:T(8,128)(2,1)}, bf16[3072,640]{1,0:T(8,128)(2,1)}, bf16[3072,384]{1,0:T(8,128)(2,1)}, f3...) custom-call(f32[768]{0:T(1024)} %refs_0_.9, ...), custom_call_target="tpu_custom_call" | custom-call | tf_op jit(solution)/shard_map/pallas_call | solution.py:971
  48.1 21.7 %shard_map.398 = (f32[3072,384]{1,0:T(8,128)}, f32[3072,384]{1,0:T(8,128)}, f32[3072,384]{1,0:T(8,128)}, f32[2,3072]{1,0:T(2,128)}, bf16[12,128,384]{2,1,0:T(8,128)(2,1)}, /*index=5*/bf16[768,3072]{1,0:T(8,128)(2,1)}) custom-call(f32[768]{0:T(1024)} %refs_0_.9, f32[384]{0:T(512)} %refs_1_.9, f32[4,384]{1,0:T(4,128)} %refs_2_.9, f32[4,256]{1,0:T(4,128)} %refs_3_.9, ...), custom_call_target="tpu_custom_call" | custom-call | tf_op jit(solution)/shard_map/pallas_call | solution.py:971
  69.9 8.1 %shard_map.399.sums.refs_10_ = f32[2,3072]{1,0:T(2,128)} custom-call(f32[2,3072]{1,0:T(2,128)} %get-tuple-element.68.part), custom_call_target="tpu_custom_call" | custom-call | tf_op jit(solution)/shard_map/pallas_call | solution.py:703
  78.0 16.8 %shard_map.401 = (bf16[3072,384]{1,0:T(8,128)(2,1)}, bf16[3072,384]{1,0:T(8,128)(2,1)}, bf16[3072,384]{1,0:T(8,128)(2,1)}, bf16[3072,384]{1,0:T(8,128)(2,1)}, f3...) custom-call(f32[768]{0:T(1024)} %refs_0_.9, f32[384]{0:T(512)} %refs_1_.9, ...), custom_call_target="tpu_custom_call" | custom-call | tf_op jit(solution)/shard_map/pallas_call | solution.py:971
  94.8 1.3 collective-permute-start
  96.1 0.7 slice.50
  96.8 0.7 slice.49
  97.5 0.6 pad_maximum_fusion.refs_19_
  98.2 0.6 copy-done.6
  98.9 32.8 %shard_map.402 = (bf16[3072,768]{1,0:T(8,128)(2,1)}, f32[8,640]{1,0:T(8,128)}, f32[8,640]{1,0:T(8,128)}, f32[8,640]{1,0:T(8,128)}, f32[16,256]{1,0:T(8,128)}) custom-call(f32[768]{0:T(1024)} %refs_0_.9, f32[384]{0:T(512)} %refs_1_.9, f32[4,384]{1,0:T(4,128)} %refs_2_.9, f32[4,256]{1,0:T(4,128)} %refs_3_.9, f32[384]{0:T(512)} %refs_4_.9, f32[256]{0:T(256)} %refs_5_.9, ...), custom_call_target="tpu_custom_call" | custom-call | tf_op jit(solution)/shard_map/pallas_call | solution.py:971
  131.7 1.5 collective-permute-start.1
  133.8 1.2 collective-permute-done.1.refs_18_
  135.0 0.6 copy-done.8
  135.6 19.5 %shard_map.403 = (bf16[768,3072]{1,0:T(8,128)(2,1)}, f32[1,768]{1,0:T(1,128)}, bf16[16,640]{1,0:T(8,128)(2,1)}, f32[8,640]{1,0:T(8,128)}) custom-call(f32[768]{0:T(1024)} %refs_0_.9, f32[384]{0:T(512)} %refs_1_.9, f32[4,384]{1,0:T(4,128)} %refs_2_.9, f32[4,256]{1,0:T(4,128)} %refs_3_.9, f32[384]{0:T(512)} %refs_4_.9, f32[256]{0:T(256)} %refs_5_.9, ...), custom_call_target="tpu_custom_call" | custom-call | tf_op jit(solution)/shard_map/pallas_call | solution.py:971
  155.2 1.7 copy-done.9
  156.9 4.7 %convolution_bitcast_fusion.p_out = f32[768,384]{1,0:T(8,128)S(1)} fusion(bf16[3072,384]{1,0:T(8,128)(2,1)S(1)} %copy-done.9, bf16[3072,768]{1,0:T(8,128)(2,1)} %refs_11_.1), kind=kOutput, calls=%fused_computation.1 | convolution fusion | flops 1811939328 | bytes 8257536 | tf_op jit(solution)/shard_map/dot_general | solution.py:31
  161.7 2.6 %fusion.2.p_z = f32[768,384]{1,0:T(8,128)S(1)} fusion(bf16[3072,768]{1,0:T(8,128)(2,1)S(1)} %bitcast.18, bf16[3072,384]{1,0:T(8,128)(2,1)S(1)} %copy-done.5), kind=kOutput, calls=%fused_computation.16 | convolution fusion | flops 1811939328 | bytes 8257536 | tf_op jit(solution)/shard_map/dot_general | solution.py:31
  164.8 7.1 %pad_add_fusion.p_cat = f32[768,768]{1,0:T(8,128)S(1)} fusion(f32[768,640]{1,0:T(8,128)S(1)} %fusion, bf16[3072,768]{1,0:T(8,128)(2,1)S(1)} %bitcast.18, bf16[3072,768]{1,0:T(8,128)(2,1)} %get-tuple-element.84.refs_14_), kind=kOutput, calls=%fused_computation | convolution fusion | flops 3624468480 | bytes 13762560 | tf_op jit(solution)/shard_map/dot_general | solution.py:31
  172.0 38.1 %shard_map.404 = (f32[192,384]{1,0:T(8,128)S(1)}, f32[192,384]{1,0:T(8,128)S(1)}, f32[192,768]{1,0:T(8,128)S(1)}, f32[8,1536]{1,0:T(8,128)S(1)}, f32[8,1024]{1,0:T(8,128)S(1)}) custom-call(f32[768,384]{1,0:T(8,128)S(1)} %convolution_bitcast_fusion.p_out, f32[768,384]{1,0:T(8,128)S(1)} %fusion.2.p_z, f32[768,768]{1,0:T(8,128)S(1)} %pad_add_fusion.p_cat, ...), custom_call_target="tpu_custom_call" | custom-call | tf_op jit(solution)/shard_map/pallas_call | solution.py:849
  210.1 0.7 slice.53
  210.8 0.7 slice.54
  212.7 0.7 copy.47
  214.6 0.6 reduce_sum.29
  215.2 0.6 constant_dynamic-slice_fusion
  215.9 0.7 slice_reduce_fusion
  216.5 5.7 %shard_map.400 = bf16[192,3072]{1,0:T(8,128)(2,1)} custom-call(s32[1]{0:T(128)} %bitcast.place, bf16[192,3072]{1,0:T(8,128)(2,1)} %reduce-scatter.3.cloned.1.call-done.part, bf16[3072,768]{1,0:T(8,128)(2,1)} %refs_10_.1, f32[2,3072]{1,0:T(2,128)} %shard_map.399.sums.refs_10_), custom_call_target="tpu_custom_call" | custom-call | tf_op jit(solution)/shard_map/pallas_call | solution.py:971
  222.2 28.0 %reduce-scatter.5.cloned.1.call-done = bf16[192,3072]{1,0:T(8,128)(2,1)} async-done(((bf16[768,3072]{1,0:T(8,128)(2,1)}), bf16[192,3072]{1,0:T(8,128)(2,1)}) %reduce-scatter.5.cloned.1.call-update) | async-done | bytes 1179664 | tf_op jit(solution)/shard_map/reduce_scatter | solution.py:1187
  250.2 0.7 copy.51
  250.9 0.7 copy.52
  (37 shorter events, 3.7 us)
Async XLA Ops:
  7.2 209.4 %reduce-scatter.3.cloned.1.call-start = ((), (), s32[]{:S(2)}) async-start(), calls=%async_computation.2 | async-start | bytes 5898240 | tf_op jit(solution)/shard_map/reduce_scatter | solution.py:1101
  69.8 180.4 %reduce-scatter.5.cloned.1.call-start = ((), (), s32[]{:S(2)}) async-start(), calls=%async_computation.3 | async-start | bytes 5898240 | tf_op jit(solution)/shard_map/reduce_scatter | solution.py:1187
  94.8 3.4 %collective-permute-start = (bf16[128,384]{1,0:T(8,128)(2,1)}, bf16[128,384]{1,0:T(8,128)(2,1)S(1)}, u32[]{:S(2)}, u32[]{:S(2)}) collective-permute-start(bf16[128,384]{1,0:T(8,128)(2,1)} %get-tuple-element.79), channel_id=1, source_target_pairs={{4,0},{5,1},{6,2},{7,3},{12,8},{13,9},{14,10},{15,11},{20,16},{21,... | collective-permute-start | bytes 294920 | tf_op jit(solution)/shard_map/ppermute | solution.py:899
  98.2 0.6 copy-start.6
  131.7 3.3 %collective-permute-start.1 = (f32[8,640]{1,0:T(8,128)}, f32[8,640]{1,0:T(8,128)S(1)}, u32[]{:S(2)}, u32[]{:S(2)}) collective-permute-start(f32[8,640]{1,0:T(8,128)} %get-tuple-element.86), channel_id=1, source_target_pairs={{4,0},{5,1},{6,2},{7,3},{12,8},{13,9},{14,10},{15,11},{20,16},{21,... | collective-permute-start | bytes 61448 | tf_op jit(solution)/shard_map/ppermute | solution.py:899
  135.0 0.6 copy-start.8
  155.1 1.8 copy-start.9
  155.1 6.5 %slice-start = ((s8[4718592]{0:T(1024)(128)(4,1)}), s8[524288]{0:T(1024)(128)(4,1)S(1)}, s32[]{:S(2)}) async-start(s8[4718592]{0:T(1024)(128)(4,1)} %bitcast.17), calls=%async_computation.4 | async-start | bytes 1048576
  156.9 4.7 %slice-start.1 = ((s8[4718592]{0:T(1024)(128)(4,1)}), s8[4194304]{0:T(1024)(128)(4,1)S(1)}, s32[]{:S(2)}) async-start(s8[4718592]{0:T(1024)(128)(4,1)} %bitcast.17), calls=%async_computation.5 | async-start | bytes 8388608
  156.9 4.7 %copy-start.5 = (bf16[3072,384]{1,0:T(8,128)(2,1)S(1)}, bf16[3072,384]{1,0:T(8,128)(2,1)}, u32[]{:S(2)}) copy-start(bf16[3072,384]{1,0:T(8,128)(2,1)} %get-tuple-element.73.refs_13_) | copy-start | bytes 7077892
  161.7 2.6 %copy-start.7 = (bf16[16,640]{1,0:T(8,128)(2,1)S(1)}, bf16[16,640]{1,0:T(8,128)(2,1)}, u32[]{:S(2)}) copy-start(bf16[16,640]{1,0:T(8,128)(2,1)} %get-tuple-element.89) | copy-start | bytes 61444
  164.8 7.2 %copy-start = (f32[8,640]{1,0:T(8,128)S(1)}, f32[8,640]{1,0:T(8,128)}, u32[]{:S(2)}) copy-start(f32[8,640]{1,0:T(8,128)} %get-tuple-element.90.m_scan) | copy-start | bytes 61444
  164.8 7.2 %copy-start.1 = (f32[8,640]{1,0:T(8,128)S(1)}, f32[8,640]{1,0:T(8,128)}, u32[]{:S(2)}) copy-start(f32[8,640]{1,0:T(8,128)} %get-tuple-element.91.m_rim) | copy-start | bytes 61444
  164.8 7.2 %copy-start.2 = (f32[16,256]{1,0:T(8,128)S(1)}, f32[16,256]{1,0:T(8,128)}, u32[]{:S(2)}) copy-start(f32[16,256]{1,0:T(8,128)} %get-tuple-element.93.m_dt) | copy-start | bytes 49156
  164.8 7.2 %copy-start.3 = (f32[8,384]{1,0:T(8,128)S(1)}, f32[8,384]{1,0:T(8,128)}, u32[]{:S(2)}) copy-start(f32[8,384]{1,0:T(8,128)} %get-tuple-element.92.m_gate) | copy-start | bytes 36868
  164.8 7.2 %copy-start.4 = (f32[1,768]{1,0:T(1,128)S(1)}, f32[1,768]{1,0:T(1,128)}, u32[]{:S(2)}) copy-start(f32[1,768]{1,0:T(1,128)} %get-tuple-element.94.m_gain) | copy-start | bytes 9220
Sparse Core Ops, SparseCore 0:
  69.9 86.2 reduce-scatter.2
  159.1 91.0 reduce-scatter.4

commit v6 on v5

--- a/solution.py
+++ b/solution.py
@@ -123,11 +123,12 @@
 
 
 def entry_kernel(
-    rows, n, chain, info, nrm, halo, par, wj, tri, ew, e8, w_z, w_out_t,
+    rows, n, chain, sub, subs, info, nrm, halo, par, wj, tri, ew, e8, w_z, w_out_t,
     jx_o, jb_o, vbc_o, sx_o, sb_o, pre_o, step_o, cum_o, s_o, end_o, dec_o, inc_o, wz_o,
     ext, run, dec, got, sent, came, own, hop,
 ):
-    i = pl.program_id(0)
+    i = pl.program_id(0) * subs + sub
+    skip = STRETCH * sub
     f = lax.axis_index("fsdp")
     here = lax.axis_index("ctx")
     _parity, twin = twin_of(here)
@@ -135,7 +136,15 @@
     barrier = pltpu.get_barrier_semaphore()
     slab = w_z.shape[0]
 
-    @pl.when(i == 0)
+    def at_first(body):
+        if sub == 0:
+            pl.when(pl.program_id(0) == 0)(body)
+
+    def at_last(body):
+        if sub == subs - 1:
+            pl.when(pl.program_id(0) == pl.num_programs(0) - 1)(body)
+
+    @at_first
     def _():
         for peer in peers:
             pl.semaphore_signal(barrier, inc=1, device_id=peer, device_id_type=MESH)
@@ -156,7 +165,7 @@
     width = inner + jb_o.shape[1]
     gain, cb, cw, taps = par[0:1, :], par[1:2, :], par[4:8, :], TAPS
 
-    @pl.when(i == 0)
+    @at_first
     def _():
         unit, _inv = norm_rows(halo[...])
         before = nn((unit * gain).astype(bf16), wj[:, :width])
@@ -169,7 +178,7 @@
     joined = product[:, :width].astype(bf16)
     jx_o[...] = joined[:, :inner]
     jb_o[...] = joined[:, inner:]
-    ext[8 : 8 + STRETCH, :] = joined.astype(f32)
+    ext[8 + skip : 8 + skip + STRETCH, :] = joined.astype(f32)
     pos = base + iota((STRETCH, 128), 0)
     first_of = segment_start(pos, starts)
     valid = [
@@ -177,9 +186,9 @@
     ]
     for g in range(width // 128):
         at = slice(128 * g, 128 * (g + 1))
-        acc = cb[:, at] + cw[taps - 1 : taps, at] * ext[8 : 8 + STRETCH, at]
+        acc = cb[:, at] + cw[taps - 1 : taps, at] * ext[8 + skip : 8 + skip + STRETCH, at]
         for k in range(taps - 1):
-            low = 8 - (taps - 1) + k
+            low = skip + 8 - (taps - 1) + k
             acc = acc + cw[k : k + 1, at] * (ext[low : low + STRETCH, at] * valid[k])
         sig = jax.nn.sigmoid(acc)
         act = acc * sig
@@ -189,7 +198,8 @@
             sx_o[:, at] = slope.astype(bf16)
         else:
             sb_o[:, 128 * g - inner : 128 * (g + 1) - inner] = slope
-    ext[0:8, :] = ext[STRETCH : STRETCH + 8, :]
+    if sub == subs - 1:
+        ext[0:8, :] = ext[skip + STRETCH : skip + STRETCH + 8, :]
     pre = jnp.transpose(product[:, width:])[:HEAD_ROWS] + par[8:16, 0:1]
     step = jax.nn.softplus(pre)
     logd = -step * jnp.exp(par[8:16, 1:2])
@@ -213,13 +223,13 @@
     end_o[...] = run[...].astype(bf16)
     dec_o[...] = dec[...]
 
-    @pl.when(i == 0)
+    @at_first
     def _():
         pl.semaphore_wait(barrier, len(peers))
         for copy in weight_copies():
             copy.start()
 
-    @pl.when(i == pl.num_programs(0) - 1)
+    @at_last
     def _():
         if chain == 2:
             copy = remote(end_o, got, hop.at[0], hop.at[1], {"ctx": twin})
@@ -232,20 +242,40 @@
             copy.wait()
 
 
+def view(ref, kind, sub):
+    if kind == "r":
+        return ref.at[pl.ds(STRETCH * sub, STRETCH), :]
+    if kind == "l":
+        return ref.at[:, pl.ds(STRETCH * sub, STRETCH)]
+    if kind == "b":
+        return ref.at[pl.ds(sub, 1)]
+    return ref
+
+
+def in_turn(kernel, subs, kinds):
+    def body(*refs):
+        for sub in range(subs):
+            kernel(sub, subs, *[view(ref, kind, sub) for ref, kind in zip(refs, kinds)])
+
+    return body
+
+
 def mix_kernel(
-    rows, info, vbc, step, cum, s_in, inc, normed, gout, wz_out, par, e_step, e_scale, e8,
-    z_o, out_o, gn_o, sum_o, st_o, br_o,
+    rows, sub, subs, info, vbc, step, cum, s_in, inc, normed, gout, wz_out, par, e_step, e_scale, e8,
+    z_o, out_o, sum_o, st_o, br_o,
     run, gram,
 ):
-    i = pl.program_id(0)
+    i = pl.program_id(0) * subs + sub
     starts, base, _end_start, flag = read_info(rows, info, i)
     inner = out_o.shape[1]
     gain = par[2:3, :inner]
     dskip = lanes_of(par[8:16, 2:3], e8[...])
 
-    @pl.when(i == 0)
-    def _():
-        run[...] = inc[...].astype(f32)
+    if sub == 0:
+
+        @pl.when(i == 0)
+        def _():
+            run[...] = inc[...].astype(f32)
 
     st = run[...].astype(bf16)
     st_o[0] = st
@@ -302,17 +332,16 @@
     zf = nn(normed[...], wz_out[:, :inner])
     z_o[...] = zf
     gated = out * (zf * jax.nn.sigmoid(zf))
-    gn = nn(gout[...], wz_out[:, inner:])
-    gn_o[...] = gn
     gg = gated * gain
-    br_o[...] = nt(wz_out[:, inner:], gg.astype(bf16)).astype(bf16)
+    branch = nt(wz_out[:, inner:], gg.astype(bf16))
+    br_o[...] = branch.astype(bf16)
     ss = jnp.sum(gated * gated, axis=1, keepdims=True)
-    dq = jnp.sum(gn * gg, axis=1, keepdims=True)
-    sum_o[...] = jnp.transpose(jnp.where(lane == 0, ss, dq))[0:2]
+    sum_o[0:1, :] = jnp.transpose(jnp.broadcast_to(ss, (STRETCH, 128)))[0:1]
+    sum_o[1:2, :] = jnp.sum(jnp.transpose(gout[...]).astype(f32) * branch, axis=0, keepdims=True)
 
 
 def gate_kernel(
-    rows, info, sums, cum, out, z, gn, vc, st, par, e_scale, e8, f_sum,
+    rows, info, sums, cum, out, z, gout, wz_out, vc, st, par, e_scale, e8, f_sum,
     gz_o, gb_o, gc_o, n2_o, a_o, gs_o, start_o, misc_o,
     run,
 ):
@@ -345,7 +374,7 @@
     act = zf * sig
     o = out[...]
     gated = o * act
-    g_n = gn[...]
+    g_n = nn(gout[...], wz_out[:, inner:])
     unit = gated * alpha_c
     g_gated = alpha_c * (g_n * gain) - beta_c * gated
     g_out = g_gated * act
@@ -718,7 +747,7 @@
     n, m, bc_cols, conv_bc,
     p_out, p_z, p_cat, m_scan, m_rim, m_gate, m_dt, m_gain,
     o_out, o_z, o_cat, o_small, o_wide,
-    give, take, mid, slots, final, bc_slots, small, small_slots, wide_slots,
+    give, take, mid, slots, final, bc_slots, small, small_slots, wide_slots, gain_slots,
     s1, r1, s2, r2, s3, r3, s4, r4,
 ):
     f = lax.axis_index("fsdp")
@@ -793,24 +822,27 @@
     final[...] = whole
     bc_at = slice(3 * inner, 3 * inner + bc_cols)
     bc_slots[pl.ds(t, 1)] = whole[:, bc_at].astype(bf16)[None]
-    wide = jnp.concatenate([small_sum[:, conv_bc:w_scan], small_sum[:, at:]], axis=1)
-    wide_slots[pl.ds(t, 1)] = wide[None]
+    wide_slots[pl.ds(t, 1)] = small_sum[:, conv_bc:w_scan][None]
+    gain_slots[pl.ds(t, 1)] = small_sum[0:1, at:][None]
     o_small[...] = small_sum[:, :at]
     thirds_ = []
     for d in range(1, m):
         peer = {"tp": turned(t, d, m)}
-        for p, buf in enumerate((bc_slots, wide_slots)):
-            copy = remote(buf.at[t], buf.at[t], s3.at[2 * (d - 1) + p], r3.at[2 * (d - 1) + p], peer)
+        for p, buf in enumerate((bc_slots, wide_slots, gain_slots)):
+            copy = remote(buf.at[t], buf.at[t], s3.at[3 * (d - 1) + p], r3.at[3 * (d - 1) + p], peer)
             copy.start()
             thirds_.append(copy)
     for copy in thirds_:
         copy.wait()
     bc_sum = bc_slots[0].astype(f32)
     wide_sum = wide_slots[0]
+    gain_sum = gain_slots[0]
     for q in range(1, m):
         bc_sum = bc_sum + bc_slots[q].astype(f32)
         wide_sum = wide_sum + wide_slots[q]
-    o_wide[...] = wide_sum
+        gain_sum = gain_sum + gain_slots[q]
+    o_wide[:, :bc_cols] = wide_sum
+    o_wide[:, bc_cols:] = jnp.broadcast_to(gain_sum, (8, gain_sum.shape[1]))
     final[:, bc_at] = bc_sum
     here = pl.ds(pl.multiple_of(parity * half, 8), half)
     o_out[here, :] = final[:, :inner]
@@ -863,9 +895,10 @@
             pltpu.VMEM((m, half, bc_cols), bf16),
             pltpu.VMEM((8, small), f32),
             pltpu.VMEM((2, max(n, 2), 8, small), f32),
-            pltpu.VMEM((m, 8, crossing), f32),
+            pltpu.VMEM((m, 8, bc_cols), f32),
+            pltpu.VMEM((m, 1, m_gain.shape[1]), f32),
             dma((n + 1,)), dma((n + 1,)), dma((2 * n - 2,)), dma((2 * n - 2,)),
-            dma((2 * m - 2,)), dma((2 * m - 2,)), dma((3,)), dma((3,)),
+            dma((3 * m - 3,)), dma((3 * m - 3,)), dma((3,)), dma((3,)),
         ],
         compiler_params=pltpu.CompilerParams(
             collective_id=3, has_side_effects=True, vmem_limit_bytes=48 * 1024 * 1024
@@ -1040,18 +1073,34 @@
     )
     run = functools.partial(call, raw=raw)
     state_dims = (blocks, states, inner)
+    subs = 2 if blocks % 2 == 0 else 1
+
+    def several(entries, kinds):
+        scales = {"r": (subs, 1), "l": (1, subs), "b": (subs, 1, 1)}
+        grown = []
+        for entry, kind in zip(entries, kinds):
+            if kind == "w":
+                grown.append(entry)
+                continue
+            dims = tuple(d * k for d, k in zip(entry[1], scales[kind]))
+            grown.append((entry[0], dims, entry[2]))
+        return grown
+
     dma = pltpu.SemaphoreType.DMA
+    entry_in, entry_out = "wrwwwwwwww", "rrrrrlllbwwww"
     (
         joined_x, joined_bc, vbc, slope_x, slope_bc, pre, step, cum, s_part, end_state, decay,
         incoming, wz_out,
     ) = run(
-        functools.partial(entry_kernel, rows, n, chain),
+        in_turn(
+            functools.partial(entry_kernel, rows, n, chain), 1, entry_in + entry_out + "w" * 8
+        ),
         blocks,
-        [
+        list([
             info_in, by_rows(normed), whole(halo), params_in, whole(w_joined), whole(upper),
             whole(spread(0)), whole(e8), (w_z, None, "any"), (w_out.T, None, "any"),
-        ],
-        [
+        ]),
+        list([
             by_rows(shape((rows, inner), bf16)),
             by_rows(shape((rows, 2 * states), bf16)),
             by_rows(shape((rows, width), bf16)),
@@ -1065,7 +1114,7 @@
             fixed(shape((1, inner), f32)),
             fixed(shape((states, inner), bf16)),
             (shape((model, 2 * inner), bf16), None, "any"),
-        ],
+        ]),
         [
             pltpu.VMEM((STRETCH + 8, width), f32),
             pltpu.VMEM((states, inner), f32),
@@ -1080,23 +1129,29 @@
     )
     if chain > 2:
         incoming = entering(decay, end_state, "ctx", False)
-    z_part, out, gn, sums, state_in, branch = run(
-        functools.partial(mix_kernel, rows),
-        blocks,
-        [
-            info_in, by_rows(vbc), by_lanes(step), by_lanes(cum), by_block(s_part),
-            whole(incoming), by_rows(normed), by_rows(grad_out), whole(wz_out), params_in,
-            whole(spread(1)), whole(spread(2)), whole(e8),
-        ],
-        [
-            by_rows(shape((rows, inner), f32)),
-            by_rows(shape((rows, inner), f32)),
-            by_rows(shape((rows, inner), f32)),
-            by_lanes(shape((2, rows), f32)),
-            by_block(shape(state_dims, bf16)),
-            by_lanes(shape((model, rows), bf16)),
-        ],
-        [pltpu.VMEM((states, inner), f32), pltpu.VMEM((STRETCH, STRETCH), f32)],
+    mix_in, mix_out = "wrllbwrrwwwww", "rrlbl"
+    z_part, out, sums, state_in, branch = run(
+        in_turn(functools.partial(mix_kernel, rows), subs, mix_in + mix_out + "wr"),
+        blocks // subs,
+        several(
+            [
+                info_in, by_rows(vbc), by_lanes(step), by_lanes(cum), by_block(s_part),
+                whole(incoming), by_rows(normed), by_rows(grad_out), whole(wz_out), params_in,
+                whole(spread(1)), whole(spread(2)), whole(e8),
+            ],
+            mix_in,
+        ),
+        several(
+            [
+                by_rows(shape((rows, inner), f32)),
+                by_rows(shape((rows, inner), f32)),
+                by_lanes(shape((2, rows), f32)),
+                by_block(shape(state_dims, bf16)),
+                by_lanes(shape((model, rows), bf16)),
+            ],
+            mix_out,
+        ),
+        [pltpu.VMEM((states, inner), f32), pltpu.VMEM((subs * STRETCH, STRETCH), f32)],
     )
     branch = lax.psum_scatter(branch, "tp", scatter_dimension=0, tiled=True)
     sums = total_over_tp(sums)
@@ -1105,7 +1160,8 @@
         blocks,
         [
             info_in, by_lanes(sums, True), by_lanes(cum, True), by_rows(out, True),
-            by_rows(z_part, True), by_rows(gn, True), by_rows(vbc, True), by_block(state_in, True),
+            by_rows(z_part, True), by_rows(grad_out, True), whole(wz_out), by_rows(vbc, True),
+            by_block(state_in, True),
             params_in, whole(spread(2)), whole(e8), whole(gather(0)),
         ],
         [

time: 260 us -> 256 us (0.985)
  transfers between devices with their start and end apart: 4 -> 4, of which waited for: 3 -> 3; matrix products, arithmetic and copies ran while one was open for 9% -> 9% of each run, Pallas kernels for 47% -> 48%
where the time goes in v6:
time: 256 us; the launch traced here: 255 us
  Pallas kernels  181 us (71%)
  waiting for transfers between devices  27.9 us (11%)
  between operations  14.3 us (6%)
  matrix products  14.1 us (6%)
  local copies, waits for them, and re-layouts  12.4 us (5%)
  starting transfers between devices  2.84 us (1%)
    pallas_call x6, Pallas kernels, call(): pl.pallas_call(body, grid=(blocks,), in_specs=[spec(shape, how) for _a, s...  121 us
    pallas_call x1, Pallas kernels, reduced(): pl.pallas_call(functools.partial(reduce_kernel, n, m, bc_cols, inner), ou...  36.9 us
    reduce_scatter x1, waiting for transfers between devices, local(): g_resid = lax.psum_scatter(g_resid, 'tp', scatter_dimension=0, tiled=True)  26.6 us
    pallas_call x1, Pallas kernels, gathered(): pl.pallas_call(functools.partial(gather_kernel, n, lax.axis_size('ctx')),...  14.6 us
    dot_general x4, matrix products, tn(): lax.dot_general(left, right, (((0,), (0,)), ((), ())), preferred_element_...  14.1 us
    pallas_call x1, Pallas kernels, total_over_tp(): pl.pallas_call(functools.partial(total_kernel, n), out_shape=jax.ShapeDty...  8.12 us
    unnamed x28, local copies, waits for them, and re-layouts  5.84 us
  transfers between devices with their start and end apart: 4, of which 3 were waited for; matrix products, arithmetic and copies ran while one was open for 9% of the time, Pallas kernels for 48%

profile of v6, /device:TPU:0, one launch (start us, length us, event | category | flops | bytes accessed | tf_op | source)
XLA Modules:
  0.0 254.9 jit_solution(17193989538913015816)
XLA Ops:
  7.2 0.8 copy.45
  8.1 0.6 pad.8.dt
  8.7 14.6 %shard_map.396 = (bf16[768,768]{1,0:T(8,128)(2,1)}, bf16[16,768]{1,0:T(8,128)(2,1)}, bf16[3072,768]{1,0:T(8,128)(2,1)}) custom-call(bf16[192,384]{1,0:T(8,128)(2,1)} %x.5, bf16[192,256]{1,0:T(8,128)(2,1)} %bc.1, bf16[192,128]{1,0:T(8,128)(2,1)} %pad.8.dt, f32[768]{0:T(1024)} %refs_0_.9, bf16[3072,768]{1,0:T(8,128)(2,1)} %refs_10_.1), custom_call_target="tpu_custom_call" | custom-call | tf_op jit(solution)/shard_map/pallas_call | solution.py:695
  23.4 24.8 %shard_map.397 = (bf16[3072,384]{1,0:T(8,128)(2,1)}, bf16[3072,256]{1,0:T(8,128)(2,1)}, bf16[3072,640]{1,0:T(8,128)(2,1)}, bf16[3072,384]{1,0:T(8,128)(2,1)}, f3...) custom-call(f32[768]{0:T(1024)} %refs_0_.9, ...), custom_call_target="tpu_custom_call" | custom-call | tf_op jit(solution)/shard_map/pallas_call | solution.py:1004
  48.2 19.5 %shard_map.398 = (f32[3072,384]{1,0:T(8,128)}, f32[3072,384]{1,0:T(8,128)}, f32[2,3072]{1,0:T(2,128)}, bf16[12,128,384]{2,1,0:T(8,128)(2,1)}, bf16[768,3072]{1,0:T(8,128)(2,1)}) custom-call(f32[768]{0:T(1024)} %refs_0_.9, f32[384]{0:T(512)} %refs_1_.9, f32[4,384]{1,0:T(4,128)} %refs_2_.9, f32[4,256]{1,0:T(4,128)} %refs_3_.9, f32[384]{0:T(512)} %refs_4_.9, ...), custom_call_target="tpu_custom_call" | custom-call | tf_op jit(solution)/shard_map/pallas_call | solution.py:1004
  67.7 8.1 %shard_map.399.sums.refs_10_ = f32[2,3072]{1,0:T(2,128)} custom-call(f32[2,3072]{1,0:T(2,128)} %get-tuple-element.67.part), custom_call_target="tpu_custom_call" | custom-call | tf_op jit(solution)/shard_map/pallas_call | solution.py:732
  75.8 19.0 %shard_map.401 = (bf16[3072,384]{1,0:T(8,128)(2,1)}, bf16[3072,384]{1,0:T(8,128)(2,1)}, bf16[3072,384]{1,0:T(8,128)(2,1)}, bf16[3072,384]{1,0:T(8,128)(2,1)}, f3...) custom-call(f32[768]{0:T(1024)} %refs_0_.9, f32[384]{0:T(512)} %refs_1_.9, ...), custom_call_target="tpu_custom_call" | custom-call | tf_op jit(solution)/shard_map/pallas_call | solution.py:1004
  94.9 1.3 collective-permute-start
  96.2 0.7 slice.50
  96.9 0.7 slice.49
  97.6 0.6 pad_maximum_fusion.refs_19_
  98.3 0.6 copy-done.6
  98.9 32.8 %shard_map.402 = (bf16[3072,768]{1,0:T(8,128)(2,1)}, f32[8,640]{1,0:T(8,128)}, f32[8,640]{1,0:T(8,128)}, f32[8,640]{1,0:T(8,128)}, f32[16,256]{1,0:T(8,128)}) custom-call(f32[768]{0:T(1024)} %refs_0_.9, f32[384]{0:T(512)} %refs_1_.9, f32[4,384]{1,0:T(4,128)} %refs_2_.9, f32[4,256]{1,0:T(4,128)} %refs_3_.9, f32[384]{0:T(512)} %refs_4_.9, f32[256]{0:T(256)} %refs_5_.9, ...), custom_call_target="tpu_custom_call" | custom-call | tf_op jit(solution)/shard_map/pallas_call | solution.py:1004
  131.7 1.5 collective-permute-start.1
  133.8 1.2 collective-permute-done.1.refs_18_
  135.0 0.6 copy-done.8
  135.6 19.4 %shard_map.403 = (bf16[768,3072]{1,0:T(8,128)(2,1)}, f32[1,768]{1,0:T(1,128)}, bf16[16,640]{1,0:T(8,128)(2,1)}, f32[8,640]{1,0:T(8,128)}) custom-call(f32[768]{0:T(1024)} %refs_0_.9, f32[384]{0:T(512)} %refs_1_.9, f32[4,384]{1,0:T(4,128)} %refs_2_.9, f32[4,256]{1,0:T(4,128)} %refs_3_.9, f32[384]{0:T(512)} %refs_4_.9, f32[256]{0:T(256)} %refs_5_.9, ...), custom_call_target="tpu_custom_call" | custom-call | tf_op jit(solution)/shard_map/pallas_call | solution.py:1004
  155.1 1.6 copy-done.9
  156.7 4.7 %convolution_bitcast_fusion.p_out = f32[768,384]{1,0:T(8,128)S(1)} fusion(bf16[3072,384]{1,0:T(8,128)(2,1)S(1)} %copy-done.9, bf16[3072,768]{1,0:T(8,128)(2,1)} %refs_11_.1), kind=kOutput, calls=%fused_computation.1 | convolution fusion | flops 1811939328 | bytes 8257536 | tf_op jit(solution)/shard_map/dot_general | solution.py:31
  161.5 2.6 %fusion.2.p_z = f32[768,384]{1,0:T(8,128)S(1)} fusion(bf16[3072,768]{1,0:T(8,128)(2,1)S(1)} %bitcast.18, bf16[3072,384]{1,0:T(8,128)(2,1)S(1)} %copy-done.5), kind=kOutput, calls=%fused_computation.16 | convolution fusion | flops 1811939328 | bytes 8257536 | tf_op jit(solution)/shard_map/dot_general | solution.py:31
  164.6 6.3 %pad_add_fusion.p_cat = f32[768,768]{1,0:T(8,128)S(1)} fusion(f32[768,640]{1,0:T(8,128)S(1)} %fusion, bf16[3072,768]{1,0:T(8,128)(2,1)S(1)} %bitcast.18, bf16[3072,768]{1,0:T(8,128)(2,1)} %get-tuple-element.82.refs_14_), kind=kOutput, calls=%fused_computation | convolution fusion | flops 3624468480 | bytes 13762560 | tf_op jit(solution)/shard_map/dot_general | solution.py:31
  171.0 36.9 %shard_map.404 = (f32[192,384]{1,0:T(8,128)S(1)}, f32[192,384]{1,0:T(8,128)S(1)}, f32[192,768]{1,0:T(8,128)S(1)}, f32[8,1536]{1,0:T(8,128)S(1)}, f32[8,1024]{1,0:T(8,128)S(1)}) custom-call(f32[768,384]{1,0:T(8,128)S(1)} %convolution_bitcast_fusion.p_out, f32[768,384]{1,0:T(8,128)S(1)} %fusion.2.p_z, f32[768,768]{1,0:T(8,128)S(1)} %pad_add_fusion.p_cat, ...), custom_call_target="tpu_custom_call" | custom-call | tf_op jit(solution)/shard_map/pallas_call | solution.py:881
  207.9 0.7 slice.53
  208.7 0.7 slice.54
  210.5 0.7 copy.47
  212.5 0.6 reduce_sum.29
  213.1 0.6 constant_dynamic-slice_fusion
  213.7 0.7 slice_reduce_fusion
  214.4 5.7 %shard_map.400 = bf16[192,3072]{1,0:T(8,128)(2,1)} custom-call(s32[1]{0:T(128)} %bitcast.place, bf16[192,3072]{1,0:T(8,128)(2,1)} %reduce-scatter.3.cloned.1.call-done.part, bf16[3072,768]{1,0:T(8,128)(2,1)} %refs_10_.1, f32[2,3072]{1,0:T(2,128)} %shard_map.399.sums.refs_10_), custom_call_target="tpu_custom_call" | custom-call | tf_op jit(solution)/shard_map/pallas_call | solution.py:1004
  220.1 26.6 %reduce-scatter.5.cloned.1.call-done = bf16[192,3072]{1,0:T(8,128)(2,1)} async-done(((bf16[768,3072]{1,0:T(8,128)(2,1)}), bf16[192,3072]{1,0:T(8,128)(2,1)}) %reduce-scatter.5.cloned.1.call-update) | async-done | bytes 1179664 | tf_op jit(solution)/shard_map/reduce_scatter | solution.py:1243
  246.7 0.7 copy.51
  247.4 0.7 copy.52
  (37 shorter events, 3.7 us)
Async XLA Ops:
  7.2 207.2 %reduce-scatter.3.cloned.1.call-start = ((), (), s32[]{:S(2)}) async-start(), calls=%async_computation.2 | async-start | bytes 5898240 | tf_op jit(solution)/shard_map/reduce_scatter | solution.py:1156
  67.7 179.0 %reduce-scatter.5.cloned.1.call-start = ((), (), s32[]{:S(2)}) async-start(), calls=%async_computation.3 | async-start | bytes 5898240 | tf_op jit(solution)/shard_map/reduce_scatter | solution.py:1243
  94.9 3.4 %collective-permute-start = (bf16[128,384]{1,0:T(8,128)(2,1)}, bf16[128,384]{1,0:T(8,128)(2,1)S(1)}, u32[]{:S(2)}, u32[]{:S(2)}) collective-permute-start(bf16[128,384]{1,0:T(8,128)(2,1)} %get-tuple-element.77), channel_id=1, source_target_pairs={{4,0},{5,1},{6,2},{7,3},{12,8},{13,9},{14,10},{15,11},{20,16},{21,... | collective-permute-start | bytes 294920 | tf_op jit(solution)/shard_map/ppermute | solution.py:932
  98.3 0.6 copy-start.6
  131.7 3.3 %collective-permute-start.1 = (f32[8,640]{1,0:T(8,128)}, f32[8,640]{1,0:T(8,128)S(1)}, u32[]{:S(2)}, u32[]{:S(2)}) collective-permute-start(f32[8,640]{1,0:T(8,128)} %get-tuple-element.84), channel_id=1, source_target_pairs={{4,0},{5,1},{6,2},{7,3},{12,8},{13,9},{14,10},{15,11},{20,16},{21,... | collective-permute-start | bytes 61448 | tf_op jit(solution)/shard_map/ppermute | solution.py:932
  135.0 0.6 copy-start.8
  155.0 1.7 copy-start.9
  155.0 6.4 %slice-start = ((s8[4718592]{0:T(1024)(128)(4,1)}), s8[524288]{0:T(1024)(128)(4,1)S(1)}, s32[]{:S(2)}) async-start(s8[4718592]{0:T(1024)(128)(4,1)} %bitcast.17), calls=%async_computation.4 | async-start | bytes 1048576
  156.7 4.7 %slice-start.1 = ((s8[4718592]{0:T(1024)(128)(4,1)}), s8[4194304]{0:T(1024)(128)(4,1)S(1)}, s32[]{:S(2)}) async-start(s8[4718592]{0:T(1024)(128)(4,1)} %bitcast.17), calls=%async_computation.5 | async-start | bytes 8388608
  156.7 4.7 %copy-start.5 = (bf16[3072,384]{1,0:T(8,128)(2,1)S(1)}, bf16[3072,384]{1,0:T(8,128)(2,1)}, u32[]{:S(2)}) copy-start(bf16[3072,384]{1,0:T(8,128)(2,1)} %get-tuple-element.71.refs_13_) | copy-start | bytes 7077892
  161.4 2.6 %copy-start.7 = (bf16[16,640]{1,0:T(8,128)(2,1)S(1)}, bf16[16,640]{1,0:T(8,128)(2,1)}, u32[]{:S(2)}) copy-start(bf16[16,640]{1,0:T(8,128)(2,1)} %get-tuple-element.87) | copy-start | bytes 61444
  164.5 6.4 %copy-start = (f32[8,640]{1,0:T(8,128)S(1)}, f32[8,640]{1,0:T(8,128)}, u32[]{:S(2)}) copy-start(f32[8,640]{1,0:T(8,128)} %get-tuple-element.88.m_scan) | copy-start | bytes 61444
  164.6 6.4 %copy-start.1 = (f32[8,640]{1,0:T(8,128)S(1)}, f32[8,640]{1,0:T(8,128)}, u32[]{:S(2)}) copy-start(f32[8,640]{1,0:T(8,128)} %get-tuple-element.89.m_rim) | copy-start | bytes 61444
  164.6 6.4 %copy-start.2 = (f32[16,256]{1,0:T(8,128)S(1)}, f32[16,256]{1,0:T(8,128)}, u32[]{:S(2)}) copy-start(f32[16,256]{1,0:T(8,128)} %get-tuple-element.91.m_dt) | copy-start | bytes 49156
  164.6 6.4 %copy-start.3 = (f32[8,384]{1,0:T(8,128)S(1)}, f32[8,384]{1,0:T(8,128)}, u32[]{:S(2)}) copy-start(f32[8,384]{1,0:T(8,128)} %get-tuple-element.90.m_gate) | copy-start | bytes 36868
  164.6 6.4 %copy-start.4 = (f32[1,768]{1,0:T(1,128)S(1)}, f32[1,768]{1,0:T(1,128)}, u32[]{:S(2)}) copy-start(f32[1,768]{1,0:T(1,128)} %get-tuple-element.92.m_gain) | copy-start | bytes 9220
Sparse Core Ops, SparseCore 0:
  67.8 86.2 reduce-scatter.2
  157.0 89.6 reduce-scatter.4

commit v7 on v6

--- a/solution.py
+++ b/solution.py
@@ -262,7 +262,7 @@
 
 def mix_kernel(
     rows, sub, subs, info, vbc, step, cum, s_in, inc, normed, gout, wz_out, par, e_step, e_scale, e8,
-    z_o, out_o, sum_o, st_o, br_o,
+    z_o, out_o, gn_o, sum_o, st_o, br_o,
     run, gram,
 ):
     i = pl.program_id(0) * subs + sub
@@ -332,16 +332,17 @@
     zf = nn(normed[...], wz_out[:, :inner])
     z_o[...] = zf
     gated = out * (zf * jax.nn.sigmoid(zf))
+    gn = nn(gout[...], wz_out[:, inner:])
+    gn_o[...] = gn
     gg = gated * gain
-    branch = nt(wz_out[:, inner:], gg.astype(bf16))
-    br_o[...] = branch.astype(bf16)
+    br_o[...] = nt(wz_out[:, inner:], gg.astype(bf16)).astype(bf16)
     ss = jnp.sum(gated * gated, axis=1, keepdims=True)
-    sum_o[0:1, :] = jnp.transpose(jnp.broadcast_to(ss, (STRETCH, 128)))[0:1]
-    sum_o[1:2, :] = jnp.sum(jnp.transpose(gout[...]).astype(f32) * branch, axis=0, keepdims=True)
+    dq = jnp.sum(gn * gg, axis=1, keepdims=True)
+    sum_o[...] = jnp.transpose(jnp.where(lane == 0, ss, dq))[0:2]
 
 
 def gate_kernel(
-    rows, info, sums, cum, out, z, gout, wz_out, vc, st, par, e_scale, e8, f_sum,
+    rows, info, sums, cum, out, z, gn, vc, st, par, e_scale, e8, f_sum,
     gz_o, gb_o, gc_o, n2_o, a_o, gs_o, start_o, misc_o,
     run,
 ):
@@ -374,7 +375,7 @@
     act = zf * sig
     o = out[...]
     gated = o * act
-    g_n = nn(gout[...], wz_out[:, inner:])
+    g_n = gn[...]
     unit = gated * alpha_c
     g_gated = alpha_c * (g_n * gain) - beta_c * gated
     g_out = g_gated * act
@@ -743,10 +744,74 @@
     )(part)
 
 
+def share_over_tp(m, t, shares, sent, came):
+    copies = []
+    for p, (buf, own) in enumerate(shares):
+        buf[pl.ds(t, 1)] = own[None]
+    for d in range(1, m):
+        for p, (buf, _own) in enumerate(shares):
+            k = 3 * (d - 1) + p
+            copy = remote(buf.at[t], buf.at[t], sent.at[k], came.at[k], {"tp": turned(t, d, m)})
+            copy.start()
+            copies.append(copy)
+    for copy in copies:
+        copy.wait()
+    totals = []
+    for buf, _own in shares:
+        total = buf[0].astype(f32)
+        for q in range(1, m):
+            total = total + buf[q].astype(f32)
+        totals.append(total)
+    return totals
+
+
+def fold_over_tp(m, t, shares, sent, came):
+    at_edge = (t == 0) | (t == 3)
+    in_middle = jnp.logical_not(at_edge)
+    inward = jnp.where(t == 0, 1, 2)
+    outward = jnp.where(t == 1, 0, 3)
+    across = 3 - t
+
+    def copy_of(phase, p, src, dst, peer):
+        buf = shares[p][0]
+        k = 3 * phase + p
+        return remote(buf.at[src], buf.at[dst], sent.at[k], came.at[k], {"tp": peer})
+
+    every = range(len(shares))
+    for buf, own in shares:
+        buf[0] = own
+
+    @pl.when(at_edge)
+    def _():
+        for p in every:
+            copy_of(0, p, 0, 1, inward).start()
+        for p in every:
+            copy_of(0, p, 0, 1, inward).wait_send()
+        for p in every:
+            copy_of(2, p, 4, 4, inward).wait_recv()
+
+    @pl.when(in_middle)
+    def _():
+        for p in every:
+            buf = shares[p][0]
+            copy_of(0, p, 0, 1, outward).wait_recv()
+            buf[2] = (buf[0].astype(f32) + buf[1].astype(f32)).astype(buf.dtype)
+            copy_of(1, p, 2, 3, across).start()
+        for p in every:
+            buf = shares[p][0]
+            copy_of(1, p, 2, 3, across).wait()
+            buf[4] = (buf[2].astype(f32) + buf[3].astype(f32)).astype(buf.dtype)
+            copy_of(2, p, 4, 4, outward).start()
+        for p in every:
+            copy_of(2, p, 4, 4, outward).wait_send()
+
+    return [buf[4].astype(f32) for buf, _own in shares]
+
+
 def reduce_kernel(
     n, m, bc_cols, conv_bc,
     p_out, p_z, p_cat, m_scan, m_rim, m_gate, m_dt, m_gain,
-    o_out, o_z, o_cat, o_small, o_wide,
+    o_all, o_small, o_wide,
     give, take, mid, slots, final, bc_slots, small, small_slots, wide_slots, gain_slots,
     s1, r1, s2, r2, s3, r3, s4, r4,
 ):
@@ -821,45 +886,21 @@
         whole = whole + slots[q].astype(f32)
     final[...] = whole
     bc_at = slice(3 * inner, 3 * inner + bc_cols)
-    bc_slots[pl.ds(t, 1)] = whole[:, bc_at].astype(bf16)[None]
-    wide_slots[pl.ds(t, 1)] = small_sum[:, conv_bc:w_scan][None]
-    gain_slots[pl.ds(t, 1)] = small_sum[0:1, at:][None]
     o_small[...] = small_sum[:, :at]
-    thirds_ = []
-    for d in range(1, m):
-        peer = {"tp": turned(t, d, m)}
-        for p, buf in enumerate((bc_slots, wide_slots, gain_slots)):
-            copy = remote(buf.at[t], buf.at[t], s3.at[3 * (d - 1) + p], r3.at[3 * (d - 1) + p], peer)
-            copy.start()
-            thirds_.append(copy)
-    for copy in thirds_:
-        copy.wait()
-    bc_sum = bc_slots[0].astype(f32)
-    wide_sum = wide_slots[0]
-    gain_sum = gain_slots[0]
-    for q in range(1, m):
-        bc_sum = bc_sum + bc_slots[q].astype(f32)
-        wide_sum = wide_sum + wide_slots[q]
-        gain_sum = gain_sum + gain_slots[q]
+    shares = (
+        (bc_slots, whole[:, bc_at].astype(bf16)),
+        (wide_slots, small_sum[:, conv_bc:w_scan]),
+        (gain_slots, small_sum[0:1, at:]),
+    )
+    bc_sum, wide_sum, gain_sum = (fold_over_tp if m == 4 else share_over_tp)(m, t, shares, s3, r3)
     o_wide[:, :bc_cols] = wide_sum
     o_wide[:, bc_cols:] = jnp.broadcast_to(gain_sum, (8, gain_sum.shape[1]))
     final[:, bc_at] = bc_sum
     here = pl.ds(pl.multiple_of(parity * half, 8), half)
-    o_out[here, :] = final[:, :inner]
-    o_z[here, :] = final[:, inner : 2 * inner]
-    o_cat[here, :] = final[:, 2 * inner :]
-    lasts = []
-    for p, (out, cols) in enumerate(
-        ((o_out, slice(0, inner)), (o_z, slice(inner, 2 * inner)), (o_cat, slice(2 * inner, None)))
-    ):
-        copy = remote(
-            final.at[:, cols] if cols.stop else final.at[:, 2 * inner : final.shape[1]],
-            out.at[here, :], s4.at[p], r4.at[p], {"ctx": twin},
-        )
-        copy.start()
-        lasts.append(copy)
-    for copy in lasts:
-        copy.wait()
+    o_all[here, :] = final[...]
+    copy = remote(final, o_all.at[here, :], s4.at[0], r4.at[0], {"ctx": twin})
+    copy.start()
+    copy.wait()
 
 
 def reduced(parts, miscs, bc_cols):
@@ -881,24 +922,23 @@
     return pl.pallas_call(
         functools.partial(reduce_kernel, n, m, bc_cols, inner),
         out_shape=[
-            shape(rows, inner), shape(rows, inner), shape(rows, p_cat.shape[1]),
-            shape(8, kept), shape(8, crossing),
+            shape(rows, wide), shape(8, kept), shape(8, crossing),
         ],
         in_specs=[pl.BlockSpec(memory_space=pltpu.VMEM)] * 8,
-        out_specs=[pl.BlockSpec(memory_space=pltpu.VMEM)] * 5,
+        out_specs=[pl.BlockSpec(memory_space=pltpu.VMEM)] * 3,
         scratch_shapes=[
             pltpu.VMEM((n, half, wide), bf16),
             pltpu.VMEM((n, half, wide), bf16),
             pltpu.VMEM((n, half, wide), bf16),
             pltpu.VMEM((n, half, wide), bf16),
             pltpu.VMEM((half, wide), f32),
-            pltpu.VMEM((m, half, bc_cols), bf16),
+            pltpu.VMEM((max(m, 5), half, bc_cols), bf16),
             pltpu.VMEM((8, small), f32),
             pltpu.VMEM((2, max(n, 2), 8, small), f32),
-            pltpu.VMEM((m, 8, bc_cols), f32),
-            pltpu.VMEM((m, 1, m_gain.shape[1]), f32),
+            pltpu.VMEM((max(m, 5), 8, bc_cols), f32),
+            pltpu.VMEM((max(m, 5), 1, m_gain.shape[1]), f32),
             dma((n + 1,)), dma((n + 1,)), dma((2 * n - 2,)), dma((2 * n - 2,)),
-            dma((3 * m - 3,)), dma((3 * m - 3,)), dma((3,)), dma((3,)),
+            dma((3 * m,)), dma((3 * m,)), dma((1,)), dma((1,)),
         ],
         compiler_params=pltpu.CompilerParams(
             collective_id=3, has_side_effects=True, vmem_limit_bytes=48 * 1024 * 1024
@@ -1129,8 +1169,8 @@
     )
     if chain > 2:
         incoming = entering(decay, end_state, "ctx", False)
-    mix_in, mix_out = "wrllbwrrwwwww", "rrlbl"
-    z_part, out, sums, state_in, branch = run(
+    mix_in, mix_out = "wrllbwrrwwwww", "rrrlbl"
+    z_part, out, gn, sums, state_in, branch = run(
         in_turn(functools.partial(mix_kernel, rows), subs, mix_in + mix_out + "wr"),
         blocks // subs,
         several(
@@ -1145,6 +1185,7 @@
             [
                 by_rows(shape((rows, inner), f32)),
                 by_rows(shape((rows, inner), f32)),
+                by_rows(shape((rows, inner), f32)),
                 by_lanes(shape((2, rows), f32)),
                 by_block(shape(state_dims, bf16)),
                 by_lanes(shape((model, rows), bf16)),
@@ -1160,8 +1201,7 @@
         blocks,
         [
             info_in, by_lanes(sums, True), by_lanes(cum, True), by_rows(out, True),
-            by_rows(z_part, True), by_rows(grad_out, True), whole(wz_out), by_rows(vbc, True),
-            by_block(state_in, True),
+            by_rows(z_part, True), by_rows(gn, True), by_rows(vbc, True), by_block(state_in, True),
             params_in, whole(spread(2)), whole(e8), whole(gather(0)),
         ],
         [
@@ -1247,17 +1287,18 @@
     part_cat = tn(normed, g_cat)
     part_rim = tn(normed[rows - 16 :], rim)
     part_cat = part_cat + jnp.pad(part_rim, ((0, 0), (0, 128)))
-    s_out, s_z, s_cat, s_small, s_wide = reduced(
+    s_all, s_small, s_wide = reduced(
         (part_out, part_z, part_cat),
         (misc_scan, rim_w, misc_gate, misc_dt, gain_part),
         2 * states,
     )
     if lax.axis_size("ctx") > 2:
-        s_out, s_z, s_cat, s_small, s_wide = jax.tree.map(
-            lambda part: lax.psum(0.5 * part, "ctx"), (s_out, s_z, s_cat, s_small, s_wide)
+        s_all, s_small, s_wide = jax.tree.map(
+            lambda part: lax.psum(0.5 * part, "ctx"), (s_all, s_small, s_wide)
         )
-    grad_w_out = s_out.T
-    grad_w_z = s_z
+    grad_w_out = s_all[:, :inner].T
+    grad_w_z = s_all[:, inner : 2 * inner]
+    s_cat = s_all[:, 2 * inner :]
     grad_w_x = s_cat[:, :inner]
     grad_w_bc = s_cat[:, inner : inner + 2 * states]
     grad_w_dt = s_cat[:, inner + 2 * states : inner + 2 * states + heads]

time: 256 us -> 253 us (0.988)
  waiting for transfers between devices: 27.9 us -> 18.1 us
  Pallas kernels: 181 us -> 187 us
    reduce_scatter x1, waiting for transfers between devices: 26.6 us -> 16.8 us  [local(): g_resid = lax.psum_scatter(g_resid, 'tp', scatter_dimension=0, tiled=True)]
    pallas_call x1, Pallas kernels: 36.9 us -> 45.1 us  [reduced(): pl.pallas_call(functools.partial(reduce_kernel, n, m, bc_cols, inner), ou...]
    unnamed x28 -> x26, local copies, waits for them, and re-layouts: 5.84 us -> 4.5 us
  transfers between devices with their start and end apart: 4 -> 4, of which waited for: 3 -> 3; matrix products, arithmetic and copies ran while one was open for 9% -> 10% of each run, Pallas kernels for 48% -> 51%
where the time goes in v7:
time: 253 us; the launch traced here: 251 us
  Pallas kernels  187 us (74%)
  waiting for transfers between devices  18.1 us (7%)
  matrix products  14.9 us (6%)
  between operations  14.3 us (6%)
  local copies, waits for them, and re-layouts  11.3 us (4%)
  starting transfers between devices  2.84 us (1%)
    pallas_call x6, Pallas kernels, call(): pl.pallas_call(body, grid=(blocks,), in_specs=[spec(shape, how) for _a, s...  120 us
    pallas_call x1, Pallas kernels, reduced(): pl.pallas_call(functools.partial(reduce_kernel, n, m, bc_cols, inner), ou...  45.1 us
    reduce_scatter x1, waiting for transfers between devices, local(): g_resid = lax.psum_scatter(g_resid, 'tp', scatter_dimension=0, tiled=True)  16.8 us
    dot_general x4, matrix products, tn(): lax.dot_general(left, right, (((0,), (0,)), ((), ())), preferred_element_...  14.9 us
    pallas_call x1, Pallas kernels, gathered(): pl.pallas_call(functools.partial(gather_kernel, n, lax.axis_size('ctx')),...  14.6 us
    pallas_call x1, Pallas kernels, total_over_tp(): pl.pallas_call(functools.partial(total_kernel, n), out_shape=jax.ShapeDty...  8.11 us
  transfers between devices with their start and end apart: 4, of which 3 were waited for; matrix products, arithmetic and copies ran while one was open for 10% of the time, Pallas kernels for 51%

profile of v7, /device:TPU:0, one launch (start us, length us, event | category | flops | bytes accessed | tf_op | source)
XLA Modules:
  0.0 251.4 jit_solution(899712046979875904)
XLA Ops:
  7.2 0.8 copy.45
  8.1 0.6 pad.8.dt
  8.7 14.6 %shard_map.396 = (bf16[768,768]{1,0:T(8,128)(2,1)}, bf16[16,768]{1,0:T(8,128)(2,1)}, bf16[3072,768]{1,0:T(8,128)(2,1)}) custom-call(bf16[192,384]{1,0:T(8,128)(2,1)} %x.5, bf16[192,256]{1,0:T(8,128)(2,1)} %bc.1, bf16[192,128]{1,0:T(8,128)(2,1)} %pad.8.dt, f32[768]{0:T(1024)} %refs_0_.9, bf16[3072,768]{1,0:T(8,128)(2,1)} %refs_10_.1), custom_call_target="tpu_custom_call" | custom-call | tf_op jit(solution)/shard_map/pallas_call | solution.py:696
  23.3 24.8 %shard_map.397 = (bf16[3072,384]{1,0:T(8,128)(2,1)}, bf16[3072,256]{1,0:T(8,128)(2,1)}, bf16[3072,640]{1,0:T(8,128)(2,1)}, bf16[3072,384]{1,0:T(8,128)(2,1)}, f3...) custom-call(f32[768]{0:T(1024)} %refs_0_.9, ...), custom_call_target="tpu_custom_call" | custom-call | tf_op jit(solution)/shard_map/pallas_call | solution.py:1044
  48.2 20.0 %shard_map.398 = (f32[3072,384]{1,0:T(8,128)}, f32[3072,384]{1,0:T(8,128)}, f32[3072,384]{1,0:T(8,128)}, f32[2,3072]{1,0:T(2,128)}, bf16[12,128,384]{2,1,0:T(8,128)(2,1)}, /*index=5*/bf16[768,3072]{1,0:T(8,128)(2,1)}) custom-call(f32[768]{0:T(1024)} %refs_0_.9, f32[384]{0:T(512)} %refs_1_.9, f32[4,384]{1,0:T(4,128)} %refs_2_.9, f32[4,256]{1,0:T(4,128)} %refs_3_.9, ...), custom_call_target="tpu_custom_call" | custom-call | tf_op jit(solution)/shard_map/pallas_call | solution.py:1044
  68.2 8.1 %shard_map.399.sums.refs_10_ = f32[2,3072]{1,0:T(2,128)} custom-call(f32[2,3072]{1,0:T(2,128)} %get-tuple-element.66.part), custom_call_target="tpu_custom_call" | custom-call | tf_op jit(solution)/shard_map/pallas_call | solution.py:733
  76.4 16.8 %shard_map.401 = (bf16[3072,384]{1,0:T(8,128)(2,1)}, bf16[3072,384]{1,0:T(8,128)(2,1)}, bf16[3072,384]{1,0:T(8,128)(2,1)}, bf16[3072,384]{1,0:T(8,128)(2,1)}, f3...) custom-call(f32[768]{0:T(1024)} %refs_0_.9, f32[384]{0:T(512)} %refs_1_.9, ...), custom_call_target="tpu_custom_call" | custom-call | tf_op jit(solution)/shard_map/pallas_call | solution.py:1044
  93.2 1.3 collective-permute-start
  94.5 0.7 slice.60
  95.2 0.7 slice.59
  95.9 0.6 pad_maximum_fusion.refs_19_
  96.6 0.6 copy-done.6
  97.2 32.8 %shard_map.402 = (bf16[3072,768]{1,0:T(8,128)(2,1)}, f32[8,640]{1,0:T(8,128)}, f32[8,640]{1,0:T(8,128)}, f32[8,640]{1,0:T(8,128)}, f32[16,256]{1,0:T(8,128)}) custom-call(f32[768]{0:T(1024)} %refs_0_.9, f32[384]{0:T(512)} %refs_1_.9, f32[4,384]{1,0:T(4,128)} %refs_2_.9, f32[4,256]{1,0:T(4,128)} %refs_3_.9, f32[384]{0:T(512)} %refs_4_.9, f32[256]{0:T(256)} %refs_5_.9, ...), custom_call_target="tpu_custom_call" | custom-call | tf_op jit(solution)/shard_map/pallas_call | solution.py:1044
  130.1 1.5 collective-permute-start.1
  132.1 1.2 collective-permute-done.1.refs_18_
  133.4 0.6 copy-done.8
  134.0 19.5 %shard_map.403 = (bf16[768,3072]{1,0:T(8,128)(2,1)}, f32[1,768]{1,0:T(1,128)}, bf16[16,640]{1,0:T(8,128)(2,1)}, f32[8,640]{1,0:T(8,128)}) custom-call(f32[768]{0:T(1024)} %refs_0_.9, f32[384]{0:T(512)} %refs_1_.9, f32[4,384]{1,0:T(4,128)} %refs_2_.9, f32[4,256]{1,0:T(4,128)} %refs_3_.9, f32[384]{0:T(512)} %refs_4_.9, f32[256]{0:T(256)} %refs_5_.9, ...), custom_call_target="tpu_custom_call" | custom-call | tf_op jit(solution)/shard_map/pallas_call | solution.py:1044
  153.5 1.7 copy-done.9
  155.2 4.7 %convolution_bitcast_fusion.p_out = f32[768,384]{1,0:T(8,128)S(1)} fusion(bf16[3072,384]{1,0:T(8,128)(2,1)S(1)} %copy-done.9, bf16[3072,768]{1,0:T(8,128)(2,1)} %refs_11_.1), kind=kOutput, calls=%fused_computation.1 | convolution fusion | flops 1811939328 | bytes 8257536 | tf_op jit(solution)/shard_map/dot_general | solution.py:31
  160.0 2.6 %fusion.2.p_z = f32[768,384]{1,0:T(8,128)S(1)} fusion(bf16[3072,768]{1,0:T(8,128)(2,1)S(1)} %bitcast.18, bf16[3072,384]{1,0:T(8,128)(2,1)S(1)} %copy-done.5), kind=kOutput, calls=%fused_computation.17 | convolution fusion | flops 1811939328 | bytes 8257536 | tf_op jit(solution)/shard_map/dot_general | solution.py:31
  163.1 7.2 %pad_add_fusion.p_cat = f32[768,768]{1,0:T(8,128)S(1)} fusion(f32[768,640]{1,0:T(8,128)S(1)} %fusion, bf16[3072,768]{1,0:T(8,128)(2,1)S(1)} %bitcast.18, bf16[3072,768]{1,0:T(8,128)(2,1)} %get-tuple-element.82.refs_14_), kind=kOutput, calls=%fused_computation | convolution fusion | flops 3624468480 | bytes 13762560 | tf_op jit(solution)/shard_map/dot_general | solution.py:31
  170.3 45.1 %shard_map.404 = (f32[192,1536]{1,0:T(8,128)S(1)}, f32[8,1536]{1,0:T(8,128)S(1)}, f32[8,1024]{1,0:T(8,128)S(1)}) custom-call(f32[768,384]{1,0:T(8,128)S(1)} %convolution_bitcast_fusion.p_out, f32[768,384]{1,0:T(8,128)S(1)} %fusion.2.p_z, f32[768,768]{1,0:T(8,128)S(1)} %pad_add_fusion.p_cat, f32[8,640]{1,0:T(8,128)S(1)} %copy-done, f32[8,640]{1,0:T(8,128)S(1)} %copy-done.1, ...), custom_call_target="tpu_custom_call" | custom-call | tf_op jit(solution)/shard_map/pallas_call | solution.py:922
  215.4 0.7 slice.65
  216.1 0.6 slice.69
  217.3 0.7 copy.47
  218.5 0.6 slice_reduce_fusion.2
  219.2 0.6 reduce_sum.29
  219.9 0.6 constant_dynamic-slice_fusion
  220.5 0.7 slice_reduce_fusion
  221.1 0.9 slice_bitcast_fusion
  222.1 5.7 %shard_map.400 = bf16[192,3072]{1,0:T(8,128)(2,1)} custom-call(s32[1]{0:T(128)} %bitcast.place, bf16[192,3072]{1,0:T(8,128)(2,1)} %reduce-scatter.3.cloned.1.call-done.part, bf16[3072,768]{1,0:T(8,128)(2,1)} %refs_10_.1, f32[2,3072]{1,0:T(2,128)} %shard_map.399.sums.refs_10_), custom_call_target="tpu_custom_call" | custom-call | tf_op jit(solution)/shard_map/pallas_call | solution.py:1044
  227.8 16.8 %reduce-scatter.5.cloned.1.call-done = bf16[192,3072]{1,0:T(8,128)(2,1)} async-done(((bf16[768,3072]{1,0:T(8,128)(2,1)}), bf16[192,3072]{1,0:T(8,128)(2,1)}) %reduce-scatter.5.cloned.1.call-update) | async-done | bytes 1179664 | tf_op jit(solution)/shard_map/reduce_scatter | solution.py:1283
  (35 shorter events, 2.5 us)
Async XLA Ops:
  7.2 214.9 %reduce-scatter.3.cloned.1.call-start = ((), (), s32[]{:S(2)}) async-start(), calls=%async_computation.2 | async-start | bytes 5898240 | tf_op jit(solution)/shard_map/reduce_scatter | solution.py:1197
  68.2 176.4 %reduce-scatter.5.cloned.1.call-start = ((), (), s32[]{:S(2)}) async-start(), calls=%async_computation.3 | async-start | bytes 5898240 | tf_op jit(solution)/shard_map/reduce_scatter | solution.py:1283
  93.2 3.4 %collective-permute-start = (bf16[128,384]{1,0:T(8,128)(2,1)}, bf16[128,384]{1,0:T(8,128)(2,1)S(1)}, u32[]{:S(2)}, u32[]{:S(2)}) collective-permute-start(bf16[128,384]{1,0:T(8,128)(2,1)} %get-tuple-element.77), channel_id=1, source_target_pairs={{4,0},{5,1},{6,2},{7,3},{12,8},{13,9},{14,10},{15,11},{20,16},{21,... | collective-permute-start | bytes 294920 | tf_op jit(solution)/shard_map/ppermute | solution.py:972
  96.6 0.6 copy-start.6
  130.1 3.3 %collective-permute-start.1 = (f32[8,640]{1,0:T(8,128)}, f32[8,640]{1,0:T(8,128)S(1)}, u32[]{:S(2)}, u32[]{:S(2)}) collective-permute-start(f32[8,640]{1,0:T(8,128)} %get-tuple-element.84), channel_id=1, source_target_pairs={{4,0},{5,1},{6,2},{7,3},{12,8},{13,9},{14,10},{15,11},{20,16},{21,... | collective-permute-start | bytes 61448 | tf_op jit(solution)/shard_map/ppermute | solution.py:972
  133.4 0.6 copy-start.8
  153.4 1.8 copy-start.9
  153.4 6.5 %slice-start = ((s8[4718592]{0:T(1024)(128)(4,1)}), s8[524288]{0:T(1024)(128)(4,1)S(1)}, s32[]{:S(2)}) async-start(s8[4718592]{0:T(1024)(128)(4,1)} %bitcast.17), calls=%async_computation.4 | async-start | bytes 1048576
  155.2 4.7 %slice-start.1 = ((s8[4718592]{0:T(1024)(128)(4,1)}), s8[4194304]{0:T(1024)(128)(4,1)S(1)}, s32[]{:S(2)}) async-start(s8[4718592]{0:T(1024)(128)(4,1)} %bitcast.17), calls=%async_computation.5 | async-start | bytes 8388608
  155.2 4.7 %copy-start.5 = (bf16[3072,384]{1,0:T(8,128)(2,1)S(1)}, bf16[3072,384]{1,0:T(8,128)(2,1)}, u32[]{:S(2)}) copy-start(bf16[3072,384]{1,0:T(8,128)(2,1)} %get-tuple-element.71.refs_13_) | copy-start | bytes 7077892
  159.9 2.6 %copy-start.7 = (bf16[16,640]{1,0:T(8,128)(2,1)S(1)}, bf16[16,640]{1,0:T(8,128)(2,1)}, u32[]{:S(2)}) copy-start(bf16[16,640]{1,0:T(8,128)(2,1)} %get-tuple-element.87) | copy-start | bytes 61444
  163.0 7.2 %copy-start = (f32[8,640]{1,0:T(8,128)S(1)}, f32[8,640]{1,0:T(8,128)}, u32[]{:S(2)}) copy-start(f32[8,640]{1,0:T(8,128)} %get-tuple-element.88.m_scan) | copy-start | bytes 61444
  163.1 7.2 %copy-start.1 = (f32[8,640]{1,0:T(8,128)S(1)}, f32[8,640]{1,0:T(8,128)}, u32[]{:S(2)}) copy-start(f32[8,640]{1,0:T(8,128)} %get-tuple-element.89.m_rim) | copy-start | bytes 61444
  163.1 7.2 %copy-start.2 = (f32[16,256]{1,0:T(8,128)S(1)}, f32[16,256]{1,0:T(8,128)}, u32[]{:S(2)}) copy-start(f32[16,256]{1,0:T(8,128)} %get-tuple-element.91.m_dt) | copy-start | bytes 49156
  163.1 7.2 %copy-start.3 = (f32[8,384]{1,0:T(8,128)S(1)}, f32[8,384]{1,0:T(8,128)}, u32[]{:S(2)}) copy-start(f32[8,384]{1,0:T(8,128)} %get-tuple-element.90.m_gate) | copy-start | bytes 36868
  163.1 7.2 %copy-start.4 = (f32[1,768]{1,0:T(1,128)S(1)}, f32[1,768]{1,0:T(1,128)}, u32[]{:S(2)}) copy-start(f32[1,768]{1,0:T(1,128)} %get-tuple-element.92.m_gain) | copy-start | bytes 9220
Sparse Core Ops, SparseCore 0:
  68.3 86.2 reduce-scatter.2
  157.5 87.0 reduce-scatter.4

commit v8 on v7

--- a/solution.py
+++ b/solution.py
@@ -125,10 +125,9 @@
 def entry_kernel(
     rows, n, chain, sub, subs, info, nrm, halo, par, wj, tri, ew, e8, w_z, w_out_t,
     jx_o, jb_o, vbc_o, sx_o, sb_o, pre_o, step_o, cum_o, s_o, end_o, dec_o, inc_o, wz_o,
-    ext, run, dec, got, sent, came, own, hop,
+    ext, run, dec, shifts, got, sent, came, own, hop,
 ):
     i = pl.program_id(0) * subs + sub
-    skip = STRETCH * sub
     f = lax.axis_index("fsdp")
     here = lax.axis_index("ctx")
     _parity, twin = twin_of(here)
@@ -172,24 +171,45 @@
         ext[0:8, :] = before.astype(bf16).astype(f32)[8:16]
         run[...] = jnp.zeros_like(run)
         dec[...] = jnp.ones_like(dec)
+        gap = iota((STRETCH, STRETCH), 0) - iota((STRETCH, STRETCH), 1)
+        for k in range(taps - 1):
+            moves = jnp.where(gap == taps - 1 - k, 1.0, 0.0).astype(bf16)
+            shifts[STRETCH * k : STRETCH * (k + 1), :] = moves
 
     normed = nrm[...]
     product = nn(normed, wj[...])
     joined = product[:, :width].astype(bf16)
     jx_o[...] = joined[:, :inner]
     jb_o[...] = joined[:, inner:]
-    ext[8 + skip : 8 + skip + STRETCH, :] = joined.astype(f32)
     pos = base + iota((STRETCH, 128), 0)
     first_of = segment_start(pos, starts)
     valid = [
         jnp.where(pos - (taps - 1 - k) >= first_of, 1.0, 0.0).astype(f32) for k in range(taps - 1)
     ]
+    row_at = iota((8, 128), 0)
+    masked = jnp.concatenate(
+        [
+            shifts[STRETCH * k : STRETCH * (k + 1), :]
+            * jnp.concatenate([ok.astype(bf16)] * (STRETCH // 128), axis=1)
+            for k, ok in enumerate(valid)
+        ],
+        axis=0,
+    )
     for g in range(width // 128):
         at = slice(128 * g, 128 * (g + 1))
-        acc = cb[:, at] + cw[taps - 1 : taps, at] * ext[8 + skip : 8 + skip + STRETCH, at]
+        if g % 2 == 0:
+            tile = nn(masked, joined[:, 128 * g : min(128 * (g + 2), width)])
+        fresh = joined[:, at].astype(f32)
+        before = ext[:, at]
+        ext[:, at] = fresh[STRETCH - 8 :]
+        acc = cb[:, at] + cw[taps - 1 : taps, at] * fresh
+        part = slice(128 * (g % 2), 128 * (g % 2 + 1))
         for k in range(taps - 1):
-            low = skip + 8 - (taps - 1) + k
-            acc = acc + cw[k : k + 1, at] * (ext[low : low + STRETCH, at] * valid[k])
+            d = taps - 1 - k
+            moved = tile[STRETCH * k : STRETCH * (k + 1), part]
+            edge = jnp.where(row_at < d, pltpu.roll(before, d, axis=0), 0.0) * valid[k][0:8]
+            moved = jnp.concatenate([moved[0:8] + edge, moved[8:]], axis=0)
+            acc = acc + cw[k : k + 1, at] * moved
         sig = jax.nn.sigmoid(acc)
         act = acc * sig
         vbc_o[:, at] = act.astype(bf16)
@@ -198,8 +218,6 @@
             sx_o[:, at] = slope.astype(bf16)
         else:
             sb_o[:, 128 * g - inner : 128 * (g + 1) - inner] = slope
-    if sub == subs - 1:
-        ext[0:8, :] = ext[skip + STRETCH : skip + STRETCH + 8, :]
     pre = jnp.transpose(product[:, width:])[:HEAD_ROWS] + par[8:16, 0:1]
     step = jax.nn.softplus(pre)
     logd = -step * jnp.exp(par[8:16, 1:2])
@@ -620,16 +638,22 @@
 
 
 def gather_kernel(
-    n, chain, x, bc, dt, par, tok, out, halo, nrm, sent, came, passed, relayed, own, hop
+    n, chain, x, bc, dt_t, par, tok, out, halo, nrm, dt, sent, came, passed, relayed, own, hop
 ):
     f = lax.axis_index("fsdp")
     parity, twin = twin_of(lax.axis_index("ctx"))
-    rows = x.shape[0]
-    half = rows // 2
+    half = x.shape[0] // 2
     here = lax.axis_index("ctx")
     following = turned(here, 1, chain)
     sides = [{"ctx": twin}] if chain == 2 else [{"ctx": following}, {"ctx": turned(here, -1, chain)}]
     start_together([{"fsdp": turned(f, d, n)} for d in range(1, n)] + sides)
+    heads, rows = dt_t.shape
+    wide = -(-rows // 128) * 128
+    flat = jnp.concatenate(
+        [dt_t[...].astype(f32), jnp.zeros((heads, wide - rows), f32)], axis=1
+    )
+    flat = jnp.concatenate([flat, jnp.zeros((128 - heads, wide), f32)], axis=0)
+    dt[...] = jnp.transpose(flat)[:rows].astype(bf16)
     pieces = []
     at = 0
     for ref in (x, bc, dt):
@@ -667,13 +691,17 @@
         unit, _inverse = norm_rows(tok_block[...])
         nrm_block[...] = (unit * gain).astype(bf16)
 
-    block = pl.BlockSpec((2 * STRETCH, tok.shape[1]), lambda i: (i, 0))
-    pltpu.emit_pipeline(
-        norm_block, grid=(tok.shape[0] // (2 * STRETCH),), in_specs=[block], out_specs=[block]
-    )(tok, nrm)
+    steps = tok.shape[0] // (2 * STRETCH)
+
+    def normalise(first, count):
+        block = pl.BlockSpec((2 * STRETCH, tok.shape[1]), lambda i: (i + first, 0))
+        pltpu.emit_pipeline(norm_block, grid=(count,), in_specs=[block], out_specs=[block])(
+            tok, nrm
+        )
 
     relays = []
-    for d in range(1, n):
+
+    def relay(d):
         source = turned(f, -d, n)
         for p, (ref, cols) in enumerate(pieces):
             copies[(d - 1) * len(pieces) + p].wait_recv()
@@ -681,6 +709,10 @@
             copy = remote(piece, piece, passed.at[d - 1, p], relayed.at[d - 1, p], {"ctx": twin})
             copy.start()
             relays.append(copy)
+
+    normalise(0, steps)
+    for d in range(1, n):
+        relay(d)
     for copy in copies:
         copy.wait_send()
     for copy in locals_:
@@ -689,10 +721,10 @@
         copy.wait()
 
 
-def gathered(x, bc, dt, par, tok):
+def gathered(x, bc, dt_t, par, tok):
     n = lax.axis_size("fsdp")
     pieces = (n - 1, 3)
-    width = x.shape[1] + bc.shape[1] + dt.shape[1]
+    width = x.shape[1] + bc.shape[1] + 128
     return pl.pallas_call(
         functools.partial(gather_kernel, n, lax.axis_size("ctx")),
         out_shape=[
@@ -703,10 +735,11 @@
         in_specs=[pl.BlockSpec(memory_space=pltpu.VMEM)] * 4 + [pl.BlockSpec(memory_space=pl.ANY)],
         out_specs=[pl.BlockSpec(memory_space=pltpu.VMEM)] * 2
         + [pl.BlockSpec(memory_space=pl.ANY)],
-        scratch_shapes=[pltpu.SemaphoreType.DMA(pieces)] * 4
+        scratch_shapes=[pltpu.VMEM((x.shape[0], 128), bf16)]
+        + [pltpu.SemaphoreType.DMA(pieces)] * 4
         + [pltpu.SemaphoreType.DMA((3,)), pltpu.SemaphoreType.DMA((2,))],
         compiler_params=pltpu.CompilerParams(collective_id=1, has_side_effects=True),
-    )(x, bc, dt, par, tok)
+    )(x, bc, dt_t, par, tok)
 
 
 def total_kernel(n, part, out, slots, sent, came):
@@ -1077,7 +1110,7 @@
     per_head = inner // heads
 
     w_joined, halo, normed = gathered(
-        w_x, w_bc, jnp.pad(w_dt, ((0, 0), (0, 128 - heads))), norm_gain, tokens
+        w_x, w_bc, w_dt.T, norm_gain, tokens
     )
     n = lax.axis_size("fsdp")
     chain = lax.axis_size("ctx")
@@ -1133,7 +1166,7 @@
         incoming, wz_out,
     ) = run(
         in_turn(
-            functools.partial(entry_kernel, rows, n, chain), 1, entry_in + entry_out + "w" * 8
+            functools.partial(entry_kernel, rows, n, chain), 1, entry_in + entry_out + "w" * 9
         ),
         blocks,
         list([
@@ -1156,9 +1189,10 @@
             (shape((model, 2 * inner), bf16), None, "any"),
         ]),
         [
-            pltpu.VMEM((STRETCH + 8, width), f32),
+            pltpu.VMEM((8, width), f32),
             pltpu.VMEM((states, inner), f32),
             pltpu.VMEM((1, inner), f32),
+            pltpu.VMEM(((taps - 1) * STRETCH, STRETCH), bf16),
             pltpu.VMEM((states, inner), bf16),
             dma((n - 1, 2)),
             dma((n - 1, 2)),

time: 253 us -> 250 us (0.988)
  transfers between devices with their start and end apart: 4 -> 4, of which waited for: 3 -> 3; matrix products, arithmetic and copies ran while one was open for 10% -> 10% of each run, Pallas kernels for 51% -> 52%
where the time goes in v8:
time: 250 us; the launch traced here: 248 us
  Pallas kernels  186 us (74%)
  waiting for transfers between devices  18.2 us (7%)
  matrix products  14.9 us (6%)
  between operations  14.3 us (6%)
  local copies, waits for them, and re-layouts  9.8 us (4%)
  starting transfers between devices  2.84 us (1%)
    pallas_call x6, Pallas kernels, call(): pl.pallas_call(body, grid=(blocks,), in_specs=[spec(shape, how) for _a, s...  118 us
    pallas_call x1, Pallas kernels, reduced(): pl.pallas_call(functools.partial(reduce_kernel, n, m, bc_cols, inner), ou...  45 us
    reduce_scatter x1, waiting for transfers between devices, local(): g_resid = lax.psum_scatter(g_resid, 'tp', scatter_dimension=0, tiled=True)  16.8 us
    dot_general x4, matrix products, tn(): lax.dot_general(left, right, (((0,), (0,)), ((), ())), preferred_element_...  14.9 us
    pallas_call x1, Pallas kernels, gathered(): pl.pallas_call(functools.partial(gather_kernel, n, lax.axis_size('ctx')),...  14.8 us
    pallas_call x1, Pallas kernels, total_over_tp(): pl.pallas_call(functools.partial(total_kernel, n), out_shape=jax.ShapeDty...  8.12 us
  transfers between devices with their start and end apart: 4, of which 3 were waited for; matrix products, arithmetic and copies ran while one was open for 10% of the time, Pallas kernels for 52%

profile of v8, /device:TPU:0, one launch (start us, length us, event | category | flops | bytes accessed | tf_op | source)
XLA Modules:
  0.0 248.3 jit_solution(2684555040503895781)
XLA Ops:
  7.2 14.8 %shard_map.396 = (bf16[768,768]{1,0:T(8,128)(2,1)}, bf16[16,768]{1,0:T(8,128)(2,1)}, bf16[3072,768]{1,0:T(8,128)(2,1)}) custom-call(bf16[192,384]{1,0:T(8,128)(2,1)} %x.3, bf16[192,256]{1,0:T(8,128)(2,1)} %bc.1, bf16[6,192]{1,0:T(8,128)(2,1)} %bitcast.22, f32[768]{0:T(1024)} %refs_0_.9, bf16[3072,768]{1,0:T(8,128)(2,1)} %refs_10_.1), custom_call_target="tpu_custom_call" | custom-call | tf_op jit(solution)/shard_map/pallas_call | solution.py:728
  22.0 23.1 %shard_map.397 = (bf16[3072,384]{1,0:T(8,128)(2,1)}, bf16[3072,256]{1,0:T(8,128)(2,1)}, bf16[3072,640]{1,0:T(8,128)(2,1)}, bf16[3072,384]{1,0:T(8,128)(2,1)}, f3...) custom-call(f32[768]{0:T(1024)} %refs_0_.9, ...), custom_call_target="tpu_custom_call" | custom-call | tf_op jit(solution)/shard_map/pallas_call | solution.py:1077
  45.1 20.0 %shard_map.398 = (f32[3072,384]{1,0:T(8,128)}, f32[3072,384]{1,0:T(8,128)}, f32[3072,384]{1,0:T(8,128)}, f32[2,3072]{1,0:T(2,128)}, bf16[12,128,384]{2,1,0:T(8,128)(2,1)}, /*index=5*/bf16[768,3072]{1,0:T(8,128)(2,1)}) custom-call(f32[768]{0:T(1024)} %refs_0_.9, f32[384]{0:T(512)} %refs_1_.9, f32[4,384]{1,0:T(4,128)} %refs_2_.9, f32[4,256]{1,0:T(4,128)} %refs_3_.9, ...), custom_call_target="tpu_custom_call" | custom-call | tf_op jit(solution)/shard_map/pallas_call | solution.py:1077
  65.2 8.1 %shard_map.399.sums.refs_10_ = f32[2,3072]{1,0:T(2,128)} custom-call(f32[2,3072]{1,0:T(2,128)} %get-tuple-element.66.part), custom_call_target="tpu_custom_call" | custom-call | tf_op jit(solution)/shard_map/pallas_call | solution.py:766
  73.3 16.8 %shard_map.401 = (bf16[3072,384]{1,0:T(8,128)(2,1)}, bf16[3072,384]{1,0:T(8,128)(2,1)}, bf16[3072,384]{1,0:T(8,128)(2,1)}, bf16[3072,384]{1,0:T(8,128)(2,1)}, f3...) custom-call(f32[768]{0:T(1024)} %refs_0_.9, f32[384]{0:T(512)} %refs_1_.9, ...), custom_call_target="tpu_custom_call" | custom-call | tf_op jit(solution)/shard_map/pallas_call | solution.py:1077
  90.1 1.3 collective-permute-start
  91.4 0.7 slice.60
  92.1 0.7 slice.59
  92.8 0.6 pad_maximum_fusion.refs_19_
  93.5 0.6 copy-done.6
  94.2 32.8 %shard_map.402 = (bf16[3072,768]{1,0:T(8,128)(2,1)}, f32[8,640]{1,0:T(8,128)}, f32[8,640]{1,0:T(8,128)}, f32[8,640]{1,0:T(8,128)}, f32[16,256]{1,0:T(8,128)}) custom-call(f32[768]{0:T(1024)} %refs_0_.9, f32[384]{0:T(512)} %refs_1_.9, f32[4,384]{1,0:T(4,128)} %refs_2_.9, f32[4,256]{1,0:T(4,128)} %refs_3_.9, f32[384]{0:T(512)} %refs_4_.9, f32[256]{0:T(256)} %refs_5_.9, ...), custom_call_target="tpu_custom_call" | custom-call | tf_op jit(solution)/shard_map/pallas_call | solution.py:1077
  127.0 1.5 collective-permute-start.1
  128.5 0.6 compare_convert_fusion.refs_12_
  129.1 1.2 collective-permute-done.1.refs_18_
  130.3 0.6 copy-done.8
  130.9 19.5 %shard_map.403 = (bf16[768,3072]{1,0:T(8,128)(2,1)}, f32[1,768]{1,0:T(1,128)}, bf16[16,640]{1,0:T(8,128)(2,1)}, f32[8,640]{1,0:T(8,128)}) custom-call(f32[768]{0:T(1024)} %refs_0_.9, f32[384]{0:T(512)} %refs_1_.9, f32[4,384]{1,0:T(4,128)} %refs_2_.9, f32[4,256]{1,0:T(4,128)} %refs_3_.9, f32[384]{0:T(512)} %refs_4_.9, f32[256]{0:T(256)} %refs_5_.9, ...), custom_call_target="tpu_custom_call" | custom-call | tf_op jit(solution)/shard_map/pallas_call | solution.py:1077
  150.4 1.7 copy-done.9
  152.2 4.7 %convolution_bitcast_fusion.p_out = f32[768,384]{1,0:T(8,128)S(1)} fusion(bf16[3072,384]{1,0:T(8,128)(2,1)S(1)} %copy-done.9, bf16[3072,768]{1,0:T(8,128)(2,1)} %refs_11_.1), kind=kOutput, calls=%fused_computation.1 | convolution fusion | flops 1811939328 | bytes 8257536 | tf_op jit(solution)/shard_map/dot_general | solution.py:31
  156.9 2.6 %fusion.2.p_z = f32[768,384]{1,0:T(8,128)S(1)} fusion(bf16[3072,768]{1,0:T(8,128)(2,1)S(1)} %bitcast.19, bf16[3072,384]{1,0:T(8,128)(2,1)S(1)} %copy-done.5), kind=kOutput, calls=%fused_computation.17 | convolution fusion | flops 1811939328 | bytes 8257536 | tf_op jit(solution)/shard_map/dot_general | solution.py:31
  160.1 7.1 %pad_add_fusion.p_cat = f32[768,768]{1,0:T(8,128)S(1)} fusion(f32[768,640]{1,0:T(8,128)S(1)} %fusion, bf16[3072,768]{1,0:T(8,128)(2,1)S(1)} %bitcast.19, bf16[3072,768]{1,0:T(8,128)(2,1)} %get-tuple-element.82.refs_14_), kind=kOutput, calls=%fused_computation | convolution fusion | flops 3624468480 | bytes 13762560 | tf_op jit(solution)/shard_map/dot_general | solution.py:31
  167.3 45.0 %shard_map.404 = (f32[192,1536]{1,0:T(8,128)S(1)}, f32[8,1536]{1,0:T(8,128)S(1)}, f32[8,1024]{1,0:T(8,128)S(1)}) custom-call(f32[768,384]{1,0:T(8,128)S(1)} %convolution_bitcast_fusion.p_out, f32[768,384]{1,0:T(8,128)S(1)} %fusion.2.p_z, f32[768,768]{1,0:T(8,128)S(1)} %pad_add_fusion.p_cat, f32[8,640]{1,0:T(8,128)S(1)} %copy-done, f32[8,640]{1,0:T(8,128)S(1)} %copy-done.1, ...), custom_call_target="tpu_custom_call" | custom-call | tf_op jit(solution)/shard_map/pallas_call | solution.py:955
  212.3 0.7 slice.65
  213.0 0.6 slice.69
  214.1 0.7 copy.46
  214.8 0.6 slice.67
  215.4 0.6 slice_reduce_fusion.2
  216.1 0.6 reduce_sum.29
  216.7 0.6 constant_dynamic-slice_fusion
  217.4 0.7 slice_reduce_fusion
  218.0 0.9 slice_bitcast_fusion
  219.0 5.7 %shard_map.400 = bf16[192,3072]{1,0:T(8,128)(2,1)} custom-call(s32[1]{0:T(128)} %bitcast.place, bf16[192,3072]{1,0:T(8,128)(2,1)} %reduce-scatter.3.cloned.1.call-done.part, bf16[3072,768]{1,0:T(8,128)(2,1)} %refs_10_.1, f32[2,3072]{1,0:T(2,128)} %shard_map.399.sums.refs_10_), custom_call_target="tpu_custom_call" | custom-call | tf_op jit(solution)/shard_map/pallas_call | solution.py:1077
  224.7 16.8 %reduce-scatter.5.cloned.1.call-done = bf16[192,3072]{1,0:T(8,128)(2,1)} async-done(((bf16[768,3072]{1,0:T(8,128)(2,1)}), bf16[192,3072]{1,0:T(8,128)(2,1)}) %reduce-scatter.5.cloned.1.call-update) | async-done | bytes 1179664 | tf_op jit(solution)/shard_map/reduce_scatter | solution.py:1317
  (33 shorter events, 1.4 us)
Async XLA Ops:
  7.2 211.8 %reduce-scatter.3.cloned.1.call-start = ((), (), s32[]{:S(2)}) async-start(), calls=%async_computation.2 | async-start | bytes 5898240 | tf_op jit(solution)/shard_map/reduce_scatter | solution.py:1231
  65.1 176.4 %reduce-scatter.5.cloned.1.call-start = ((), (), s32[]{:S(2)}) async-start(), calls=%async_computation.3 | async-start | bytes 5898240 | tf_op jit(solution)/shard_map/reduce_scatter | solution.py:1317
  90.1 3.4 %collective-permute-start = (bf16[128,384]{1,0:T(8,128)(2,1)}, bf16[128,384]{1,0:T(8,128)(2,1)S(1)}, u32[]{:S(2)}, u32[]{:S(2)}) collective-permute-start(bf16[128,384]{1,0:T(8,128)(2,1)} %get-tuple-element.77), channel_id=1, source_target_pairs={{4,0},{5,1},{6,2},{7,3},{12,8},{13,9},{14,10},{15,11},{20,16},{21,... | collective-permute-start | bytes 294920 | tf_op jit(solution)/shard_map/ppermute | solution.py:1005
  93.5 0.6 copy-start.6
  127.0 3.3 %collective-permute-start.1 = (f32[8,640]{1,0:T(8,128)}, f32[8,640]{1,0:T(8,128)S(1)}, u32[]{:S(2)}, u32[]{:S(2)}) collective-permute-start(f32[8,640]{1,0:T(8,128)} %get-tuple-element.84), channel_id=1, source_target_pairs={{4,0},{5,1},{6,2},{7,3},{12,8},{13,9},{14,10},{15,11},{20,16},{21,... | collective-permute-start | bytes 61448 | tf_op jit(solution)/shard_map/ppermute | solution.py:1005
  130.3 0.6 copy-start.8
  150.4 1.8 copy-start.9
  150.4 6.5 %slice-start = ((s8[4718592]{0:T(1024)(128)(4,1)}), s8[524288]{0:T(1024)(128)(4,1)S(1)}, s32[]{:S(2)}) async-start(s8[4718592]{0:T(1024)(128)(4,1)} %bitcast.18), calls=%async_computation.4 | async-start | bytes 1048576
  152.2 4.7 %slice-start.1 = ((s8[4718592]{0:T(1024)(128)(4,1)}), s8[4194304]{0:T(1024)(128)(4,1)S(1)}, s32[]{:S(2)}) async-start(s8[4718592]{0:T(1024)(128)(4,1)} %bitcast.18), calls=%async_computation.5 | async-start | bytes 8388608
  152.2 4.7 %copy-start.5 = (bf16[3072,384]{1,0:T(8,128)(2,1)S(1)}, bf16[3072,384]{1,0:T(8,128)(2,1)}, u32[]{:S(2)}) copy-start(bf16[3072,384]{1,0:T(8,128)(2,1)} %get-tuple-element.71.refs_13_) | copy-start | bytes 7077892
  156.9 2.6 %copy-start.7 = (bf16[16,640]{1,0:T(8,128)(2,1)S(1)}, bf16[16,640]{1,0:T(8,128)(2,1)}, u32[]{:S(2)}) copy-start(bf16[16,640]{1,0:T(8,128)(2,1)} %get-tuple-element.87) | copy-start | bytes 61444
  160.0 7.2 %copy-start = (f32[8,640]{1,0:T(8,128)S(1)}, f32[8,640]{1,0:T(8,128)}, u32[]{:S(2)}) copy-start(f32[8,640]{1,0:T(8,128)} %get-tuple-element.88.m_scan) | copy-start | bytes 61444
  160.0 7.2 %copy-start.1 = (f32[8,640]{1,0:T(8,128)S(1)}, f32[8,640]{1,0:T(8,128)}, u32[]{:S(2)}) copy-start(f32[8,640]{1,0:T(8,128)} %get-tuple-element.89.m_rim) | copy-start | bytes 61444
  160.0 7.2 %copy-start.2 = (f32[16,256]{1,0:T(8,128)S(1)}, f32[16,256]{1,0:T(8,128)}, u32[]{:S(2)}) copy-start(f32[16,256]{1,0:T(8,128)} %get-tuple-element.91.m_dt) | copy-start | bytes 49156
  160.0 7.2 %copy-start.3 = (f32[8,384]{1,0:T(8,128)S(1)}, f32[8,384]{1,0:T(8,128)}, u32[]{:S(2)}) copy-start(f32[8,384]{1,0:T(8,128)} %get-tuple-element.90.m_gate) | copy-start | bytes 36868
  160.1 7.2 %copy-start.4 = (f32[1,768]{1,0:T(1,128)S(1)}, f32[1,768]{1,0:T(1,128)}, u32[]{:S(2)}) copy-start(f32[1,768]{1,0:T(1,128)} %get-tuple-element.92.m_gain) | copy-start | bytes 9220
Sparse Core Ops, SparseCore 0:
  65.3 86.1 reduce-scatter.2
  154.3 87.1 reduce-scatter.4

commit v9 on v8

--- a/solution.py
+++ b/solution.py
@@ -638,7 +638,7 @@
 
 
 def gather_kernel(
-    n, chain, x, bc, dt_t, par, tok, out, halo, nrm, dt, sent, came, passed, relayed, own, hop
+    n, chain, x, bc, dt_t, par, tok, out, halo, nrm, dt, dts, sent, came, passed, relayed, own, hop
 ):
     f = lax.axis_index("fsdp")
     parity, twin = twin_of(lax.axis_index("ctx"))
@@ -652,11 +652,19 @@
     flat = jnp.concatenate(
         [dt_t[...].astype(f32), jnp.zeros((heads, wide - rows), f32)], axis=1
     )
-    flat = jnp.concatenate([flat, jnp.zeros((128 - heads, wide), f32)], axis=0)
-    dt[...] = jnp.transpose(flat)[:rows].astype(bf16)
+    flat = jnp.concatenate([flat, jnp.zeros((HEAD_ROWS - heads, wide), f32)], axis=0)
+    dt[...] = flat.astype(bf16)
+    dts[pl.ds(f, 1)] = dt[...][None]
+    tiny = []
+    for d in range(1, n):
+        copy = remote(
+            dt, dts.at[f], sent.at[d - 1, 2], came.at[d - 1, 2], {"fsdp": turned(f, d, n)}
+        )
+        copy.start()
+        tiny.append(copy)
     pieces = []
     at = 0
-    for ref in (x, bc, dt):
+    for ref in (x, bc):
         pieces.append((ref, slice(at, at + ref.shape[1])))
         at += ref.shape[1]
 
@@ -713,6 +721,11 @@
     normalise(0, steps)
     for d in range(1, n):
         relay(d)
+    for copy in tiny:
+        copy.wait()
+    joint = jnp.concatenate([dts[q].astype(f32)[:, :rows] for q in range(n)], axis=1)
+    joint = jnp.concatenate([joint, jnp.zeros((128 - HEAD_ROWS, n * rows), f32)], axis=0)
+    out[:, at:] = jnp.transpose(joint).astype(bf16)
     for copy in copies:
         copy.wait_send()
     for copy in locals_:
@@ -735,7 +748,10 @@
         in_specs=[pl.BlockSpec(memory_space=pltpu.VMEM)] * 4 + [pl.BlockSpec(memory_space=pl.ANY)],
         out_specs=[pl.BlockSpec(memory_space=pltpu.VMEM)] * 2
         + [pl.BlockSpec(memory_space=pl.ANY)],
-        scratch_shapes=[pltpu.VMEM((x.shape[0], 128), bf16)]
+        scratch_shapes=[
+            pltpu.VMEM((HEAD_ROWS, -(-x.shape[0] // 128) * 128), bf16),
+            pltpu.VMEM((n, HEAD_ROWS, -(-x.shape[0] // 128) * 128), bf16),
+        ]
         + [pltpu.SemaphoreType.DMA(pieces)] * 4
         + [pltpu.SemaphoreType.DMA((3,)), pltpu.SemaphoreType.DMA((2,))],
         compiler_params=pltpu.CompilerParams(collective_id=1, has_side_effects=True),

time: 250 us -> 249 us (level)
  no operation moved by 1% of the time
where the time goes in v9:
time: 249 us; the launch traced here: 247 us
  Pallas kernels  185 us (74%)
  waiting for transfers between devices  18.2 us (7%)
  matrix products  14.7 us (6%)
  between operations  14.3 us (6%)
  local copies, waits for them, and re-layouts  9.76 us (4%)
  starting transfers between devices  2.84 us (1%)
  other arithmetic  2.49 us (1%)
    pallas_call x6, Pallas kernels, call(): pl.pallas_call(body, grid=(blocks,), in_specs=[spec(shape, how) for _a, s...  118 us
    pallas_call x1, Pallas kernels, reduced(): pl.pallas_call(functools.partial(reduce_kernel, n, m, bc_cols, inner), ou...  44.8 us
    reduce_scatter x1, waiting for transfers between devices, local(): g_resid = lax.psum_scatter(g_resid, 'tp', scatter_dimension=0, tiled=True)  16.8 us
    dot_general x4, matrix products, tn(): lax.dot_general(left, right, (((0,), (0,)), ((), ())), preferred_element_...  14.7 us
    pallas_call x1, Pallas kernels, gathered(): pl.pallas_call(functools.partial(gather_kernel, n, lax.axis_size('ctx')),...  14.4 us
    pallas_call x1, Pallas kernels, total_over_tp(): pl.pallas_call(functools.partial(total_kernel, n), out_shape=jax.ShapeDty...  8.03 us
  transfers between devices with their start and end apart: 4, of which 3 were waited for; matrix products, arithmetic and copies ran while one was open for 10% of the time, Pallas kernels for 52%

profile of v9, /device:TPU:0, one launch (start us, length us, event | category | flops | bytes accessed | tf_op | source)
XLA Modules:
  0.0 247.4 jit_solution(14174000267354425360)
XLA Ops:
  7.2 14.4 %shard_map.396 = (bf16[768,768]{1,0:T(8,128)(2,1)}, bf16[16,768]{1,0:T(8,128)(2,1)}, bf16[3072,768]{1,0:T(8,128)(2,1)}) custom-call(bf16[192,384]{1,0:T(8,128)(2,1)} %x.3, bf16[192,256]{1,0:T(8,128)(2,1)} %bc.1, bf16[6,192]{1,0:T(8,128)(2,1)} %bitcast.22, f32[768]{0:T(1024)} %refs_0_.9, bf16[3072,768]{1,0:T(8,128)(2,1)} %refs_10_.1), custom_call_target="tpu_custom_call" | custom-call | tf_op jit(solution)/shard_map/pallas_call | solution.py:741
  21.7 23.0 %shard_map.397 = (bf16[3072,384]{1,0:T(8,128)(2,1)}, bf16[3072,256]{1,0:T(8,128)(2,1)}, bf16[3072,640]{1,0:T(8,128)(2,1)}, bf16[3072,384]{1,0:T(8,128)(2,1)}, f3...) custom-call(f32[768]{0:T(1024)} %refs_0_.9, ...), custom_call_target="tpu_custom_call" | custom-call | tf_op jit(solution)/shard_map/pallas_call | solution.py:1093
  44.7 20.0 %shard_map.398 = (f32[3072,384]{1,0:T(8,128)}, f32[3072,384]{1,0:T(8,128)}, f32[3072,384]{1,0:T(8,128)}, f32[2,3072]{1,0:T(2,128)}, bf16[12,128,384]{2,1,0:T(8,128)(2,1)}, /*index=5*/bf16[768,3072]{1,0:T(8,128)(2,1)}) custom-call(f32[768]{0:T(1024)} %refs_0_.9, f32[384]{0:T(512)} %refs_1_.9, f32[4,384]{1,0:T(4,128)} %refs_2_.9, f32[4,256]{1,0:T(4,128)} %refs_3_.9, ...), custom_call_target="tpu_custom_call" | custom-call | tf_op jit(solution)/shard_map/pallas_call | solution.py:1093
  64.8 8.0 %shard_map.399.sums.refs_10_ = f32[2,3072]{1,0:T(2,128)} custom-call(f32[2,3072]{1,0:T(2,128)} %get-tuple-element.66.part), custom_call_target="tpu_custom_call" | custom-call | tf_op jit(solution)/shard_map/pallas_call | solution.py:782
  72.8 16.8 %shard_map.401 = (bf16[3072,384]{1,0:T(8,128)(2,1)}, bf16[3072,384]{1,0:T(8,128)(2,1)}, bf16[3072,384]{1,0:T(8,128)(2,1)}, bf16[3072,384]{1,0:T(8,128)(2,1)}, f3...) custom-call(f32[768]{0:T(1024)} %refs_0_.9, f32[384]{0:T(512)} %refs_1_.9, ...), custom_call_target="tpu_custom_call" | custom-call | tf_op jit(solution)/shard_map/pallas_call | solution.py:1093
  89.7 1.3 collective-permute-start
  91.0 0.7 slice.60
  91.7 0.7 slice.59
  92.4 0.6 pad_maximum_fusion.refs_19_
  93.1 0.6 copy-done.6
  93.7 32.8 %shard_map.402 = (bf16[3072,768]{1,0:T(8,128)(2,1)}, f32[8,640]{1,0:T(8,128)}, f32[8,640]{1,0:T(8,128)}, f32[8,640]{1,0:T(8,128)}, f32[16,256]{1,0:T(8,128)}) custom-call(f32[768]{0:T(1024)} %refs_0_.9, f32[384]{0:T(512)} %refs_1_.9, f32[4,384]{1,0:T(4,128)} %refs_2_.9, f32[4,256]{1,0:T(4,128)} %refs_3_.9, f32[384]{0:T(512)} %refs_4_.9, f32[256]{0:T(256)} %refs_5_.9, ...), custom_call_target="tpu_custom_call" | custom-call | tf_op jit(solution)/shard_map/pallas_call | solution.py:1093
  126.5 1.5 collective-permute-start.1
  128.0 0.6 compare_convert_fusion.refs_12_
  128.6 1.2 collective-permute-done.1.refs_18_
  129.8 0.6 copy-done.8
  130.4 19.6 %shard_map.403 = (bf16[768,3072]{1,0:T(8,128)(2,1)}, f32[1,768]{1,0:T(1,128)}, bf16[16,640]{1,0:T(8,128)(2,1)}, f32[8,640]{1,0:T(8,128)}) custom-call(f32[768]{0:T(1024)} %refs_0_.9, f32[384]{0:T(512)} %refs_1_.9, f32[4,384]{1,0:T(4,128)} %refs_2_.9, f32[4,256]{1,0:T(4,128)} %refs_3_.9, f32[384]{0:T(512)} %refs_4_.9, f32[256]{0:T(256)} %refs_5_.9, ...), custom_call_target="tpu_custom_call" | custom-call | tf_op jit(solution)/shard_map/pallas_call | solution.py:1093
  150.0 1.7 copy-done.9
  151.7 4.7 %convolution_bitcast_fusion.p_out = f32[768,384]{1,0:T(8,128)S(1)} fusion(bf16[3072,384]{1,0:T(8,128)(2,1)S(1)} %copy-done.9, bf16[3072,768]{1,0:T(8,128)(2,1)} %refs_11_.1), kind=kOutput, calls=%fused_computation.1 | convolution fusion | flops 1811939328 | bytes 8257536 | tf_op jit(solution)/shard_map/dot_general | solution.py:31
  156.4 2.6 %fusion.2.p_z = f32[768,384]{1,0:T(8,128)S(1)} fusion(bf16[3072,768]{1,0:T(8,128)(2,1)S(1)} %bitcast.19, bf16[3072,384]{1,0:T(8,128)(2,1)S(1)} %copy-done.5), kind=kOutput, calls=%fused_computation.17 | convolution fusion | flops 1811939328 | bytes 8257536 | tf_op jit(solution)/shard_map/dot_general | solution.py:31
  159.6 6.9 %pad_add_fusion.p_cat = f32[768,768]{1,0:T(8,128)S(1)} fusion(f32[768,640]{1,0:T(8,128)S(1)} %fusion, bf16[3072,768]{1,0:T(8,128)(2,1)S(1)} %bitcast.19, bf16[3072,768]{1,0:T(8,128)(2,1)} %get-tuple-element.82.refs_14_), kind=kOutput, calls=%fused_computation | convolution fusion | flops 3624468480 | bytes 13762560 | tf_op jit(solution)/shard_map/dot_general | solution.py:31
  166.5 44.8 %shard_map.404 = (f32[192,1536]{1,0:T(8,128)S(1)}, f32[8,1536]{1,0:T(8,128)S(1)}, f32[8,1024]{1,0:T(8,128)S(1)}) custom-call(f32[768,384]{1,0:T(8,128)S(1)} %convolution_bitcast_fusion.p_out, f32[768,384]{1,0:T(8,128)S(1)} %fusion.2.p_z, f32[768,768]{1,0:T(8,128)S(1)} %pad_add_fusion.p_cat, f32[8,640]{1,0:T(8,128)S(1)} %copy-done, f32[8,640]{1,0:T(8,128)S(1)} %copy-done.1, ...), custom_call_target="tpu_custom_call" | custom-call | tf_op jit(solution)/shard_map/pallas_call | solution.py:971
  211.3 0.7 slice.65
  212.0 0.6 slice.69
  213.2 0.7 copy.46
  213.8 0.6 slice.67
  214.4 0.6 slice_reduce_fusion.2
  215.1 0.6 reduce_sum.29
  215.8 0.6 constant_dynamic-slice_fusion
  216.4 0.7 slice_reduce_fusion
  217.0 0.9 slice_bitcast_fusion
  218.0 5.7 %shard_map.400 = bf16[192,3072]{1,0:T(8,128)(2,1)} custom-call(s32[1]{0:T(128)} %bitcast.place, bf16[192,3072]{1,0:T(8,128)(2,1)} %reduce-scatter.3.cloned.1.call-done.part, bf16[3072,768]{1,0:T(8,128)(2,1)} %refs_10_.1, f32[2,3072]{1,0:T(2,128)} %shard_map.399.sums.refs_10_), custom_call_target="tpu_custom_call" | custom-call | tf_op jit(solution)/shard_map/pallas_call | solution.py:1093
  223.7 16.8 %reduce-scatter.5.cloned.1.call-done = bf16[192,3072]{1,0:T(8,128)(2,1)} async-done(((bf16[768,3072]{1,0:T(8,128)(2,1)}), bf16[192,3072]{1,0:T(8,128)(2,1)}) %reduce-scatter.5.cloned.1.call-update) | async-done | bytes 1179664 | tf_op jit(solution)/shard_map/reduce_scatter | solution.py:1333
  (33 shorter events, 1.4 us)
Async XLA Ops:
  7.2 210.8 %reduce-scatter.3.cloned.1.call-start = ((), (), s32[]{:S(2)}) async-start(), calls=%async_computation.2 | async-start | bytes 5898240 | tf_op jit(solution)/shard_map/reduce_scatter | solution.py:1247
  64.8 175.8 %reduce-scatter.5.cloned.1.call-start = ((), (), s32[]{:S(2)}) async-start(), calls=%async_computation.3 | async-start | bytes 5898240 | tf_op jit(solution)/shard_map/reduce_scatter | solution.py:1333
  89.7 3.4 %collective-permute-start = (bf16[128,384]{1,0:T(8,128)(2,1)}, bf16[128,384]{1,0:T(8,128)(2,1)S(1)}, u32[]{:S(2)}, u32[]{:S(2)}) collective-permute-start(bf16[128,384]{1,0:T(8,128)(2,1)} %get-tuple-element.77), channel_id=1, source_target_pairs={{4,0},{5,1},{6,2},{7,3},{12,8},{13,9},{14,10},{15,11},{20,16},{21,... | collective-permute-start | bytes 294920 | tf_op jit(solution)/shard_map/ppermute | solution.py:1021
  93.1 0.6 copy-start.6
  126.5 3.3 %collective-permute-start.1 = (f32[8,640]{1,0:T(8,128)}, f32[8,640]{1,0:T(8,128)S(1)}, u32[]{:S(2)}, u32[]{:S(2)}) collective-permute-start(f32[8,640]{1,0:T(8,128)} %get-tuple-element.84), channel_id=1, source_target_pairs={{4,0},{5,1},{6,2},{7,3},{12,8},{13,9},{14,10},{15,11},{20,16},{21,... | collective-permute-start | bytes 61448 | tf_op jit(solution)/shard_map/ppermute | solution.py:1021
  129.8 0.6 copy-start.8
  150.0 1.7 copy-start.9
  150.0 6.4 %slice-start = ((s8[4718592]{0:T(1024)(128)(4,1)}), s8[524288]{0:T(1024)(128)(4,1)S(1)}, s32[]{:S(2)}) async-start(s8[4718592]{0:T(1024)(128)(4,1)} %bitcast.18), calls=%async_computation.4 | async-start | bytes 1048576
  151.7 4.7 %slice-start.1 = ((s8[4718592]{0:T(1024)(128)(4,1)}), s8[4194304]{0:T(1024)(128)(4,1)S(1)}, s32[]{:S(2)}) async-start(s8[4718592]{0:T(1024)(128)(4,1)} %bitcast.18), calls=%async_computation.5 | async-start | bytes 8388608
  151.7 4.7 %copy-start.5 = (bf16[3072,384]{1,0:T(8,128)(2,1)S(1)}, bf16[3072,384]{1,0:T(8,128)(2,1)}, u32[]{:S(2)}) copy-start(bf16[3072,384]{1,0:T(8,128)(2,1)} %get-tuple-element.71.refs_13_) | copy-start | bytes 7077892
  156.4 2.6 %copy-start.7 = (bf16[16,640]{1,0:T(8,128)(2,1)S(1)}, bf16[16,640]{1,0:T(8,128)(2,1)}, u32[]{:S(2)}) copy-start(bf16[16,640]{1,0:T(8,128)(2,1)} %get-tuple-element.87) | copy-start | bytes 61444
  159.5 6.9 %copy-start = (f32[8,640]{1,0:T(8,128)S(1)}, f32[8,640]{1,0:T(8,128)}, u32[]{:S(2)}) copy-start(f32[8,640]{1,0:T(8,128)} %get-tuple-element.88.m_scan) | copy-start | bytes 61444
  159.5 6.9 %copy-start.1 = (f32[8,640]{1,0:T(8,128)S(1)}, f32[8,640]{1,0:T(8,128)}, u32[]{:S(2)}) copy-start(f32[8,640]{1,0:T(8,128)} %get-tuple-element.89.m_rim) | copy-start | bytes 61444
  159.5 6.9 %copy-start.2 = (f32[16,256]{1,0:T(8,128)S(1)}, f32[16,256]{1,0:T(8,128)}, u32[]{:S(2)}) copy-start(f32[16,256]{1,0:T(8,128)} %get-tuple-element.91.m_dt) | copy-start | bytes 49156
  159.6 6.9 %copy-start.3 = (f32[8,384]{1,0:T(8,128)S(1)}, f32[8,384]{1,0:T(8,128)}, u32[]{:S(2)}) copy-start(f32[8,384]{1,0:T(8,128)} %get-tuple-element.90.m_gate) | copy-start | bytes 36868
  159.6 6.9 %copy-start.4 = (f32[1,768]{1,0:T(1,128)S(1)}, f32[1,768]{1,0:T(1,128)}, u32[]{:S(2)}) copy-start(f32[1,768]{1,0:T(1,128)} %get-tuple-element.92.m_gain) | copy-start | bytes 9220
Sparse Core Ops, SparseCore 0:
  64.9 85.6 reduce-scatter.2
  153.4 87.0 reduce-scatter.4

commit v10 on v9

--- a/solution.py
+++ b/solution.py
@@ -586,7 +586,7 @@
         scaled = g_normed * gain
         mean = jnp.mean(scaled * unit, axis=1, keepdims=True)
         own = gout[...].astype(f32) * mine[...]
-        gr_o[...] = jnp.transpose(own + inverse * (scaled - unit * mean)).astype(bf16)
+        gr_o[...] = jnp.transpose((own + inverse * (scaled - unit * mean)).astype(bf16))
         gain_o[...] += jnp.sum(g_normed * unit, axis=0, keepdims=True)
 
     @pl.when(step_id == 0)

time: 249 us -> 249 us (level)
  no operation moved by 1% of the time
where the time goes in v10:
time: 249 us; the launch traced here: 247 us
  Pallas kernels  185 us (74%)
  waiting for transfers between devices  18.2 us (7%)
  matrix products  14.7 us (6%)
  between operations  14.3 us (6%)
  local copies, waits for them, and re-layouts  9.77 us (4%)
  starting transfers between devices  2.84 us (1%)
  other arithmetic  2.49 us (1%)
    pallas_call x6, Pallas kernels, call(): pl.pallas_call(body, grid=(blocks,), in_specs=[spec(shape, how) for _a, s...  118 us
    pallas_call x1, Pallas kernels, reduced(): pl.pallas_call(functools.partial(reduce_kernel, n, m, bc_cols, inner), ou...  44.8 us
    reduce_scatter x1, waiting for transfers between devices, local(): g_resid = lax.psum_scatter(g_resid, 'tp', scatter_dimension=0, tiled=True)  16.9 us
    dot_general x4, matrix products, tn(): lax.dot_general(left, right, (((0,), (0,)), ((), ())), preferred_element_...  14.7 us
    pallas_call x1, Pallas kernels, gathered(): pl.pallas_call(functools.partial(gather_kernel, n, lax.axis_size('ctx')),...  14.4 us
    pallas_call x1, Pallas kernels, total_over_tp(): pl.pallas_call(functools.partial(total_kernel, n), out_shape=jax.ShapeDty...  8.03 us
  transfers between devices with their start and end apart: 4, of which 3 were waited for; matrix products, arithmetic and copies ran while one was open for 10% of the time, Pallas kernels for 52%

profile of v10, /device:TPU:0, one launch (start us, length us, event | category | flops | bytes accessed | tf_op | source)
XLA Modules:
  0.0 247.4 jit_solution(4290635153556426248)
XLA Ops:
  7.2 14.4 %shard_map.396 = (bf16[768,768]{1,0:T(8,128)(2,1)}, bf16[16,768]{1,0:T(8,128)(2,1)}, bf16[3072,768]{1,0:T(8,128)(2,1)}) custom-call(bf16[192,384]{1,0:T(8,128)(2,1)} %x.3, bf16[192,256]{1,0:T(8,128)(2,1)} %bc.1, bf16[6,192]{1,0:T(8,128)(2,1)} %bitcast.22, f32[768]{0:T(1024)} %refs_0_.9, bf16[3072,768]{1,0:T(8,128)(2,1)} %refs_10_.1), custom_call_target="tpu_custom_call" | custom-call | tf_op jit(solution)/shard_map/pallas_call | solution.py:741
  21.7 23.0 %shard_map.397 = (bf16[3072,384]{1,0:T(8,128)(2,1)}, bf16[3072,256]{1,0:T(8,128)(2,1)}, bf16[3072,640]{1,0:T(8,128)(2,1)}, bf16[3072,384]{1,0:T(8,128)(2,1)}, f3...) custom-call(f32[768]{0:T(1024)} %refs_0_.9, ...), custom_call_target="tpu_custom_call" | custom-call | tf_op jit(solution)/shard_map/pallas_call | solution.py:1093
  44.7 20.0 %shard_map.398 = (f32[3072,384]{1,0:T(8,128)}, f32[3072,384]{1,0:T(8,128)}, f32[3072,384]{1,0:T(8,128)}, f32[2,3072]{1,0:T(2,128)}, bf16[12,128,384]{2,1,0:T(8,128)(2,1)}, /*index=5*/bf16[768,3072]{1,0:T(8,128)(2,1)}) custom-call(f32[768]{0:T(1024)} %refs_0_.9, f32[384]{0:T(512)} %refs_1_.9, f32[4,384]{1,0:T(4,128)} %refs_2_.9, f32[4,256]{1,0:T(4,128)} %refs_3_.9, ...), custom_call_target="tpu_custom_call" | custom-call | tf_op jit(solution)/shard_map/pallas_call | solution.py:1093
  64.8 8.0 %shard_map.399.sums.refs_10_ = f32[2,3072]{1,0:T(2,128)} custom-call(f32[2,3072]{1,0:T(2,128)} %get-tuple-element.66.part), custom_call_target="tpu_custom_call" | custom-call | tf_op jit(solution)/shard_map/pallas_call | solution.py:782
  72.8 16.8 %shard_map.401 = (bf16[3072,384]{1,0:T(8,128)(2,1)}, bf16[3072,384]{1,0:T(8,128)(2,1)}, bf16[3072,384]{1,0:T(8,128)(2,1)}, bf16[3072,384]{1,0:T(8,128)(2,1)}, f3...) custom-call(f32[768]{0:T(1024)} %refs_0_.9, f32[384]{0:T(512)} %refs_1_.9, ...), custom_call_target="tpu_custom_call" | custom-call | tf_op jit(solution)/shard_map/pallas_call | solution.py:1093
  89.7 1.3 collective-permute-start
  91.0 0.7 slice.60
  91.7 0.7 slice.59
  92.4 0.6 pad_maximum_fusion.refs_19_
  93.1 0.6 copy-done.6
  93.7 32.8 %shard_map.402 = (bf16[3072,768]{1,0:T(8,128)(2,1)}, f32[8,640]{1,0:T(8,128)}, f32[8,640]{1,0:T(8,128)}, f32[8,640]{1,0:T(8,128)}, f32[16,256]{1,0:T(8,128)}) custom-call(f32[768]{0:T(1024)} %refs_0_.9, f32[384]{0:T(512)} %refs_1_.9, f32[4,384]{1,0:T(4,128)} %refs_2_.9, f32[4,256]{1,0:T(4,128)} %refs_3_.9, f32[384]{0:T(512)} %refs_4_.9, f32[256]{0:T(256)} %refs_5_.9, ...), custom_call_target="tpu_custom_call" | custom-call | tf_op jit(solution)/shard_map/pallas_call | solution.py:1093
  126.5 1.5 collective-permute-start.1
  128.0 0.6 compare_convert_fusion.refs_12_
  128.6 1.2 collective-permute-done.1.refs_18_
  129.8 0.6 copy-done.8
  130.4 19.4 %shard_map.403 = (bf16[768,3072]{1,0:T(8,128)(2,1)}, f32[1,768]{1,0:T(1,128)}, bf16[16,640]{1,0:T(8,128)(2,1)}, f32[8,640]{1,0:T(8,128)}) custom-call(f32[768]{0:T(1024)} %refs_0_.9, f32[384]{0:T(512)} %refs_1_.9, f32[4,384]{1,0:T(4,128)} %refs_2_.9, f32[4,256]{1,0:T(4,128)} %refs_3_.9, f32[384]{0:T(512)} %refs_4_.9, f32[256]{0:T(256)} %refs_5_.9, ...), custom_call_target="tpu_custom_call" | custom-call | tf_op jit(solution)/shard_map/pallas_call | solution.py:1093
  149.9 1.7 copy-done.9
  151.6 4.7 %convolution_bitcast_fusion.p_out = f32[768,384]{1,0:T(8,128)S(1)} fusion(bf16[3072,384]{1,0:T(8,128)(2,1)S(1)} %copy-done.9, bf16[3072,768]{1,0:T(8,128)(2,1)} %refs_11_.1), kind=kOutput, calls=%fused_computation.1 | convolution fusion | flops 1811939328 | bytes 8257536 | tf_op jit(solution)/shard_map/dot_general | solution.py:31
  156.3 2.6 %fusion.2.p_z = f32[768,384]{1,0:T(8,128)S(1)} fusion(bf16[3072,768]{1,0:T(8,128)(2,1)S(1)} %bitcast.19, bf16[3072,384]{1,0:T(8,128)(2,1)S(1)} %copy-done.5), kind=kOutput, calls=%fused_computation.17 | convolution fusion | flops 1811939328 | bytes 8257536 | tf_op jit(solution)/shard_map/dot_general | solution.py:31
  159.5 6.9 %pad_add_fusion.p_cat = f32[768,768]{1,0:T(8,128)S(1)} fusion(f32[768,640]{1,0:T(8,128)S(1)} %fusion, bf16[3072,768]{1,0:T(8,128)(2,1)S(1)} %bitcast.19, bf16[3072,768]{1,0:T(8,128)(2,1)} %get-tuple-element.82.refs_14_), kind=kOutput, calls=%fused_computation | convolution fusion | flops 3624468480 | bytes 13762560 | tf_op jit(solution)/shard_map/dot_general | solution.py:31
  166.5 44.8 %shard_map.404 = (f32[192,1536]{1,0:T(8,128)S(1)}, f32[8,1536]{1,0:T(8,128)S(1)}, f32[8,1024]{1,0:T(8,128)S(1)}) custom-call(f32[768,384]{1,0:T(8,128)S(1)} %convolution_bitcast_fusion.p_out, f32[768,384]{1,0:T(8,128)S(1)} %fusion.2.p_z, f32[768,768]{1,0:T(8,128)S(1)} %pad_add_fusion.p_cat, f32[8,640]{1,0:T(8,128)S(1)} %copy-done, f32[8,640]{1,0:T(8,128)S(1)} %copy-done.1, ...), custom_call_target="tpu_custom_call" | custom-call | tf_op jit(solution)/shard_map/pallas_call | solution.py:971
  211.3 0.7 slice.65
  212.0 0.6 slice.69
  213.1 0.7 copy.46
  213.8 0.6 slice.67
  214.4 0.6 slice_reduce_fusion.2
  215.1 0.6 reduce_sum.29
  215.7 0.6 constant_dynamic-slice_fusion
  216.4 0.7 slice_reduce_fusion
  217.0 0.9 slice_bitcast_fusion
  217.9 5.7 %shard_map.400 = bf16[192,3072]{1,0:T(8,128)(2,1)} custom-call(s32[1]{0:T(128)} %bitcast.place, bf16[192,3072]{1,0:T(8,128)(2,1)} %reduce-scatter.3.cloned.1.call-done.part, bf16[3072,768]{1,0:T(8,128)(2,1)} %refs_10_.1, f32[2,3072]{1,0:T(2,128)} %shard_map.399.sums.refs_10_), custom_call_target="tpu_custom_call" | custom-call | tf_op jit(solution)/shard_map/pallas_call | solution.py:1093
  223.7 16.9 %reduce-scatter.5.cloned.1.call-done = bf16[192,3072]{1,0:T(8,128)(2,1)} async-done(((bf16[768,3072]{1,0:T(8,128)(2,1)}), bf16[192,3072]{1,0:T(8,128)(2,1)}) %reduce-scatter.5.cloned.1.call-update) | async-done | bytes 1179664 | tf_op jit(solution)/shard_map/reduce_scatter | solution.py:1333
  (33 shorter events, 1.4 us)
Async XLA Ops:
  7.2 210.8 %reduce-scatter.3.cloned.1.call-start = ((), (), s32[]{:S(2)}) async-start(), calls=%async_computation.2 | async-start | bytes 5898240 | tf_op jit(solution)/shard_map/reduce_scatter | solution.py:1247
  64.8 175.8 %reduce-scatter.5.cloned.1.call-start = ((), (), s32[]{:S(2)}) async-start(), calls=%async_computation.3 | async-start | bytes 5898240 | tf_op jit(solution)/shard_map/reduce_scatter | solution.py:1333
  89.7 3.4 %collective-permute-start = (bf16[128,384]{1,0:T(8,128)(2,1)}, bf16[128,384]{1,0:T(8,128)(2,1)S(1)}, u32[]{:S(2)}, u32[]{:S(2)}) collective-permute-start(bf16[128,384]{1,0:T(8,128)(2,1)} %get-tuple-element.77), channel_id=1, source_target_pairs={{4,0},{5,1},{6,2},{7,3},{12,8},{13,9},{14,10},{15,11},{20,16},{21,... | collective-permute-start | bytes 294920 | tf_op jit(solution)/shard_map/ppermute | solution.py:1021
  93.1 0.6 copy-start.6
  126.5 3.3 %collective-permute-start.1 = (f32[8,640]{1,0:T(8,128)}, f32[8,640]{1,0:T(8,128)S(1)}, u32[]{:S(2)}, u32[]{:S(2)}) collective-permute-start(f32[8,640]{1,0:T(8,128)} %get-tuple-element.84), channel_id=1, source_target_pairs={{4,0},{5,1},{6,2},{7,3},{12,8},{13,9},{14,10},{15,11},{20,16},{21,... | collective-permute-start | bytes 61448 | tf_op jit(solution)/shard_map/ppermute | solution.py:1021
  129.8 0.6 copy-start.8
  149.8 1.7 copy-start.9
  149.8 6.4 %slice-start = ((s8[4718592]{0:T(1024)(128)(4,1)}), s8[524288]{0:T(1024)(128)(4,1)S(1)}, s32[]{:S(2)}) async-start(s8[4718592]{0:T(1024)(128)(4,1)} %bitcast.18), calls=%async_computation.4 | async-start | bytes 1048576
  151.6 4.7 %slice-start.1 = ((s8[4718592]{0:T(1024)(128)(4,1)}), s8[4194304]{0:T(1024)(128)(4,1)S(1)}, s32[]{:S(2)}) async-start(s8[4718592]{0:T(1024)(128)(4,1)} %bitcast.18), calls=%async_computation.5 | async-start | bytes 8388608
  151.6 4.7 %copy-start.5 = (bf16[3072,384]{1,0:T(8,128)(2,1)S(1)}, bf16[3072,384]{1,0:T(8,128)(2,1)}, u32[]{:S(2)}) copy-start(bf16[3072,384]{1,0:T(8,128)(2,1)} %get-tuple-element.71.refs_13_) | copy-start | bytes 7077892
  156.3 2.6 %copy-start.7 = (bf16[16,640]{1,0:T(8,128)(2,1)S(1)}, bf16[16,640]{1,0:T(8,128)(2,1)}, u32[]{:S(2)}) copy-start(bf16[16,640]{1,0:T(8,128)(2,1)} %get-tuple-element.87) | copy-start | bytes 61444
  159.4 7.0 %copy-start = (f32[8,640]{1,0:T(8,128)S(1)}, f32[8,640]{1,0:T(8,128)}, u32[]{:S(2)}) copy-start(f32[8,640]{1,0:T(8,128)} %get-tuple-element.88.m_scan) | copy-start | bytes 61444
  159.4 7.0 %copy-start.1 = (f32[8,640]{1,0:T(8,128)S(1)}, f32[8,640]{1,0:T(8,128)}, u32[]{:S(2)}) copy-start(f32[8,640]{1,0:T(8,128)} %get-tuple-element.89.m_rim) | copy-start | bytes 61444
  159.4 7.0 %copy-start.2 = (f32[16,256]{1,0:T(8,128)S(1)}, f32[16,256]{1,0:T(8,128)}, u32[]{:S(2)}) copy-start(f32[16,256]{1,0:T(8,128)} %get-tuple-element.91.m_dt) | copy-start | bytes 49156
  159.4 7.0 %copy-start.3 = (f32[8,384]{1,0:T(8,128)S(1)}, f32[8,384]{1,0:T(8,128)}, u32[]{:S(2)}) copy-start(f32[8,384]{1,0:T(8,128)} %get-tuple-element.90.m_gate) | copy-start | bytes 36868
  159.5 7.0 %copy-start.4 = (f32[1,768]{1,0:T(1,128)S(1)}, f32[1,768]{1,0:T(1,128)}, u32[]{:S(2)}) copy-start(f32[1,768]{1,0:T(1,128)} %get-tuple-element.92.m_gain) | copy-start | bytes 9220
Sparse Core Ops, SparseCore 0:
  64.9 85.6 reduce-scatter.2
  153.4 87.0 reduce-scatter.4
